TPU v7x, 128 devices: a whole 4x4x4 slice. The times are simulated.
128 devices in a mesh: section: 8 (over y, core), row: 16 (over z, x).
Axes of the slice: x: 4, y: 4, z: 4, core: 2. Of those that a mesh axis runs over, the one named last changes fastest.
Arguments:
- diag_blocks: float32 [8, 2, 16, 256, 256], P('section', None, 'row'), may hold values from -9 to 9, as said below
- coupling_blocks: float32 [8, 2, 16, 256, 256], P('section', None, 'row'), as said below
Outputs:
- reduced_diag: float32 [8, 2, 16, 256, 256], P('section', None, 'row')
- reduced_coupling: float32 [8, 2, 16, 256, 256], P('section', None, 'row')
Inputs may be any that keep to these rules, and one draw needn't show every extreme that they name: `diag_blocks`: every block is symmetric. `coupling_blocks`: every block is three times the identity plus a random part whose entries are at most 5 / sqrt(256) in magnitude and whose spectral norm is at most 2.5, so every block is invertible.
All inputs are finite; a program needn't handle non-finite values.
Results may differ from a plain program's by a relative error of at most 0.0003.
Values sent between devices are 32-bit elements; how exact they have to be, the bound alone decides.
No kernel may reach another device: no remote copies, remote signals or barrier semaphores. Data moves between devices by JAX's collectives and lax.ppermute only.
A program may use at most 64 MiB of HBM per device.

v0:
```python
import functools

import jax
import jax.numpy as jnp
from jax import lax
from jax.experimental import pallas as pl
from jax.experimental.pallas import tpu as pltpu
from jax.sharding import PartitionSpec as P

D = 256
B = 16
HALF = 128
F32 = jnp.float32
BF16 = jnp.bfloat16
KAPPA2 = 3.0e7


def dg(a, b, ca, cb):
    return lax.dot_general(a, b, (((ca,), (cb,)), ((), ())), preferred_element_type=F32)


def split2(x):
    h = x.astype(BF16)
    return h, (x - h.astype(F32)).astype(BF16)


def split3(x):
    h = x.astype(BF16)
    r = x - h.astype(F32)
    m = r.astype(BF16)
    return h, m, (r - m.astype(F32)).astype(BF16)


def mm(a, b, ca=1, cb=0, passes=6):
    if passes == 3:
        ah, al = split2(a)
        bh, bl = split2(b)
        return dg(al, bh, ca, cb) + dg(ah, bl, ca, cb) + dg(ah, bh, ca, cb)
    ah, am, al = split3(a)
    bh, bm, bl = split3(b)
    small = dg(al, bh, ca, cb) + dg(ah, bl, ca, cb) + dg(am, bm, ca, cb)
    return (small + (dg(am, bh, ca, cb) + dg(ah, bm, ca, cb))) + dg(ah, bh, ca, cb)


def square_iota():
    return (
        lax.broadcasted_iota(jnp.int32, (D, D), 0),
        lax.broadcasted_iota(jnp.int32, (D, D), 1),
    )


def chol_inv(a_ref, nb):
    row = lax.broadcasted_iota(jnp.int32, (B, HALF), 0)
    lane2 = lax.broadcasted_iota(jnp.int32, (B, D), 1)
    row2 = lax.broadcasted_iota(jnp.int32, (B, D), 0)
    for p in range(D // B):
        k = p * B
        for m in range(nb):
            s = a_ref[m, k : k + B, :]
            cols = [jnp.broadcast_to(s[:, k + c : k + c + 1], (B, HALF)) for c in range(B)]
            own = (lane2 >= k) & (lane2 < k + B)
            s = jnp.where(own, jnp.where(lane2 - k == row2, 1.0, 0.0), s)
            sa, sb = s[:, :HALF], s[:, HALF:]
            pivots = jnp.ones((B, HALF), F32)
            for r in range(B):
                piv = jnp.broadcast_to(cols[r][r : r + 1, :], (B, HALF))
                l = jnp.where(row > r, cols[r] * (1.0 / piv), 0.0)
                pivots = jnp.where(row == r, piv, pivots)
                for c in range(r + 1, B):
                    cols[c] = cols[c] - l * jnp.broadcast_to(cols[c][r : r + 1, :], (B, HALF))
                sa = sa - l * jnp.broadcast_to(sa[r : r + 1, :], (B, HALF))
                sb = sb - l * jnp.broadcast_to(sb[r : r + 1, :], (B, HALF))
            rs = lax.rsqrt(pivots)
            s = jnp.concatenate([sa * rs, sb * rs], 1)
            a_ref[m, k : k + B, :] = s
            if k + B < D:
                n0 = HALF if k + B >= HALF else 0
                h, md, lo = split3(s)
                left = jnp.concatenate([lo, h, md, md, h, h], 0)
                right = jnp.concatenate([h, lo, md, h, md, h], 0)
                u = dg(left[:, n0:], right, 0, 0)
                tail = a_ref[m, k + B :, :]
                lt = lax.broadcasted_iota(jnp.int32, (D - k - B, D), 1)
                kept = jnp.where((lt >= k) & (lt < k + B), 0.0, tail)
                a_ref[m, k + B :, :] = kept - u[k + B - n0 :, :]


TABLE = (
    (6, 1, 3, 8, 0, 0, 2, 7, 7, 9),
    (5, 4, 0, 0, 0, 0, 1, 2, 6, 8),
    (4, 5, 3, 6, 0, 0, 2, 5, 9, 8),
    (6, 3, 1, 8, 2, 5, 3, 10, 8, 9),
)


def eye_value():
    r, c = square_iota()
    return jnp.where(r == c, 1.0, 0.0)


def pair_kernel(pos_ref, c_ref, r0, r1, w_ref, v_ref, buf):
    x = pos_ref[1]
    odd = lax.rem(x, 2)
    high = x // 2
    buf[odd] = c_ref[0]
    buf[1 - odd] = r0[...]
    buf[2 + high] = c_ref[1]
    buf[3 - high] = r1[...]
    w_ref[...] = mm(buf[1], buf[0])
    outer = (x == 0) | (x == 3)

    @pl.when(outer)
    def _():
        v_ref[...] = buf[2]

    @pl.when(jnp.logical_not(outer))
    def _():
        v_ref[...] = mm(buf[3], buf[2])


def window_kernel(tab_ref, c_ref, r0, r1, w, q0, q1, prev_ref, t_ref, buf):
    buf[0] = c_ref[0]
    buf[1] = c_ref[1]
    for k, ref in enumerate((r0, r1, w, q0, q1)):
        buf[2 + k] = ref[...]
    buf[7] = eye_value()

    def step(i, _):
        buf[8 + i] = mm(buf[tab_ref[2 * i]], buf[tab_ref[2 * i + 1]])
        return 0

    lax.fori_loop(0, tab_ref[6], step, 0)
    prev_ref[0] = buf[tab_ref[7]]
    prev_ref[1] = buf[tab_ref[8]]
    t_ref[...] = buf[tab_ref[9]]


def entry_kernel(pos_ref, t1, t2, t3, e_ref, buf):
    z = pos_ref[0]
    buf[0] = eye_value()
    for k, ref in enumerate((t1, t2, t3)):
        buf[1 + k] = ref[...]
    e_ref[...] = buf[z]

    def step(i, _):
        e_ref[...] = mm(buf[z - 1 - i], e_ref[...])
        return 0

    lax.fori_loop(0, z - 1, step, 0)


def factor_kernel(pos_ref, prev_ref, own, other, c_ref, m_ref, x_ref, stat_ref, e_all):
    mine = pos_ref[2]
    e_all[mine] = own[...]
    e_all[1 - mine] = other[...]
    for m in range(2):
        before = mm(prev_ref[m], e_all[m])
        m_ref[m] = before
        m_ref[2 + m] = mm(c_ref[m], before)
    for m in range(4):
        full = m_ref[m]
        x_ref[m] = mm(full, full, 0, 0)
    chol_inv(x_ref, 4)
    r, c = square_iota()
    worst = jnp.zeros((8, HALF), F32)
    for m in range(4):
        inv = jnp.where(c <= r, x_ref[m], 0.0)
        full = m_ref[m]
        x_ref[m] = inv
        size = jnp.sum(jnp.sum(inv * inv, axis=0, keepdims=True), axis=1, keepdims=True)
        size = size * jnp.sum(jnp.sum(full * full, axis=0, keepdims=True), axis=1, keepdims=True)
        worst = jnp.maximum(worst, jnp.broadcast_to(jnp.where(size < KAPPA2, 0.0, 1.0), (8, HALF)))
    stat_ref[...] = worst


def refined(y):
    r, c = square_iota()
    err = mm(y, y, 0, 0, passes=3) - eye_value()
    upper = jnp.where(c > r, err, jnp.where(c == r, 0.5 * err, 0.0))
    return y - mm(y, upper, passes=3)


def finish_kernel(m_ref, x_ref, c_ref, d_ref, n_ref, r_ref, y_ref):
    r, c = square_iota()
    for m in range(4):
        y_ref[m] = refined(mm(m_ref[m], x_ref[m], 1, 1))
    for m in range(2):
        before = y_ref[m]
        q = y_ref[2 + m]
        r_ref[m] = jnp.where(c >= r, mm(q, mm(c_ref[m], before), 0, 0), 0.0)
        n_ref[m] = mm(mm(q, d_ref[m], 0, 0), q)


def chain_kernel(before_ref, c_ref, d_ref, n_ref, r_ref, q_ref, a_ref):
    r, c = square_iota()
    lane = lax.broadcasted_iota(jnp.int32, (1, D), 1)

    def one(m, _):
        n_ref[m] = mm(c_ref[m], before_ref[m])
        a_ref[...] = mm(n_ref[m], n_ref[m], 0, 0)

        def column(k, _):
            a = a_ref[...]
            row = a_ref[pl.ds(k, 1), :]
            pivot = jnp.sum(jnp.where(lane == k, row, 0.0), axis=1, keepdims=True)
            rs = lax.rsqrt(pivot)
            row = jnp.where(lane == k, 1.0, row) * rs
            factor_col = jnp.sum(jnp.where(c == k, a, 0.0), axis=1, keepdims=True) * rs
            below = jnp.where(c == k, 0.0, a) - factor_col * row
            a_ref[...] = jnp.where(r > k, below, jnp.where(r == k, row, a))
            return 0

        lax.fori_loop(0, D, column, 0)
        q_ref[m] = mm(n_ref[m], jnp.where(c <= r, a_ref[...], 0.0), 1, 1)

        def again(_, carry):
            q_ref[m] = refined(q_ref[m])
            return carry

        lax.fori_loop(0, 2, again, 0)
        q = q_ref[m]
        r_ref[m] = jnp.where(c >= r, mm(q, n_ref[m], 0, 0), 0.0)
        n_ref[m] = mm(mm(q, d_ref[m], 0, 0), q)
        return 0

    lax.fori_loop(0, 2, one, 0)


def struct(*shape):
    return jax.ShapeDtypeStruct(shape, F32)


VMEM = pl.BlockSpec(memory_space=pltpu.VMEM)
SMEM = pl.BlockSpec(memory_space=pltpu.SMEM)


def call(kernel, outs, scratch, name, table=True):
    def run(*args):
        specs = [VMEM] * len(args)
        if table:
            specs[0] = SMEM
        return pl.pallas_call(
            kernel,
            out_shape=outs,
            in_specs=specs,
            out_specs=jax.tree.map(lambda _: VMEM, outs),
            scratch_shapes=[pltpu.VMEM(shape, F32) for shape in scratch],
            compiler_params=pltpu.CompilerParams(vmem_limit_bytes=48 * 2**20),
            name=name,
        )(*args)

    return run


SQUARE = struct(D, D)
TWO = struct(2, D, D)
FOUR = struct(4, D, D)
pair = call(pair_kernel, (SQUARE, SQUARE), [(4, D, D)], "pair")
window = call(window_kernel, (TWO, SQUARE), [(11, D, D)], "window")
entry = call(entry_kernel, SQUARE, [(4, D, D)], "entry")
factor = call(factor_kernel, (FOUR, FOUR, struct(8, HALF)), [(2, D, D)], "factor")
finish = call(finish_kernel, (TWO, TWO), [(4, D, D)], "finish", table=False)
chain = call(chain_kernel, (TWO, TWO, TWO), [(D, D)], "chain", table=False)


def x_move(value, to):
    return lax.ppermute(value, "row", [(i, (i // 4) * 4 + to(i % 4)) for i in range(16)])


def z_move(value, s):
    return lax.ppermute(value, "row", [(i, i + 4 * s) for i in range(16 - 4 * s)])


def z_ring(value, s):
    return lax.ppermute(value, "row", [(i, (i + 4 * s) % 16) for i in range(16)])


def x_pairs(value):
    return x_move(value, lambda x: x ^ 1)


def x_mirror(value):
    return x_move(value, lambda x: 3 - x)


def any_in_row(flag):
    moved = [x_move(flag, lambda x, s=s: (x + s) % 4) for s in (1, 2, 3)]
    flag = functools.reduce(jnp.maximum, moved, flag)
    return functools.reduce(jnp.maximum, [z_ring(flag, s) for s in (1, 2, 3)], flag)


def shards(diag_blocks, coupling_blocks):
    diagonal = diag_blocks.reshape(2, D, D)
    coupling = coupling_blocks.reshape(2, D, D)
    position = lax.axis_index("row")
    z, x = position // 4, position % 4
    mine = jnp.where((x == 0) | (x == 3), 1, 0)
    pos = jnp.stack([z, x, mine]).astype(jnp.int32)
    table = jnp.asarray(TABLE, jnp.int32)[x]

    r0, r1 = x_pairs(coupling[0]), x_mirror(coupling[1])
    w, v = pair(pos, coupling, r0, r1)
    q0, q1 = x_mirror(w), x_pairs(v)
    prev, total = window(table, coupling, r0, r1, w, q0, q1)
    below = [z_move(total, s) for s in (1, 2, 3)]
    own = entry(pos, *below)
    full, inv, stat = factor(pos, prev, own, x_pairs(own), coupling)
    bad = any_in_row(stat)
    new, tri = finish(full, inv, coupling, diagonal)

    def step(i, carried):
        before, new, tri = carried
        new_now, tri_now, q = chain(before, coupling, diagonal)
        keep = i == position
        new = jnp.where(keep, new_now, new)
        tri = jnp.where(keep, tri_now, tri)
        return lax.ppermute(q, "row", [(j, j + 1) for j in range(15)]), new, tri

    rounds = jnp.where(bad[0, 0] > 0.0, 16, 0)
    eyes = jnp.broadcast_to(jnp.eye(D, dtype=F32), (2, D, D))
    _, new, tri = lax.fori_loop(0, rounds, step, (eyes, new, tri))
    shape = diag_blocks.shape
    return new.reshape(shape), tri.reshape(shape)


def solution(mesh):
    placed = P("section", None, "row", None, None)
    return jax.shard_map(
        shards,
        mesh=mesh,
        in_specs=(placed, placed),
        out_specs=(placed, placed),
        check_vma=False,
    )
```

profile of v0, /device:TPU:48, one launch (start us, length us, event | category | flops | bytes accessed | tf_op | source)
XLA Modules:
  0.0 86.6 jit_solution(7033441042520391914)
XLA Ops:
  0.6 1.1 %slice_bitcast_fusion = (f32[256,256]{1,0:T(8,128)S(1)}, f32[256,256]{1,0:T(8,128)S(1)}) fusion(f32[1,2,1,256,256]{4,3,2,1,0:T(8,128)} %param.6), kind=kLoop, calls=%fused_computation.2 | loop fusion | bytes 1048576 | tf_op jit(solution)/shard_map/squeeze | solution.py:301
  1.8 1.6 %collective-permute-start.1 = (f32[256,256]{1,0:T(8,128)S(1)}, f32[256,256]{1,0:T(8,128)S(1)}, u32[]{:S(2)}, u32[]{:S(2)}) collective-permute-start(f32[256,256]{1,0:T(8,128)S(1)} %get-tuple-element.88), channel_id=1, source_target_pairs={{0,1},{1,0},{2,3},{3,2},{4,5},{5,4},{6,7},{7,6},{8,9},{9,8},{10,11... | collective-permute-start | bytes 786440 | tf_op jit(solution)/shard_map/ppermute | solution.py:267
  3.3 2.1 %collective-permute-start.2 = (f32[256,256]{1,0:T(8,128)S(1)}, f32[256,256]{1,0:T(8,128)S(1)}, u32[]{:S(2)}, u32[]{:S(2)}) collective-permute-start(f32[256,256]{1,0:T(8,128)S(1)} %get-tuple-element.87), channel_id=1, source_target_pairs={{0,3},{1,2},{2,1},{3,0},{4,7},{5,6},{6,5},{7,4},{8,11},{9,10},{10,... | collective-permute-start | bytes 786440 | tf_op jit(solution)/shard_map/ppermute | solution.py:267
  5.4 0.1 pad_add_fusion.pos_ref
  5.5 4.4 %collective-permute-done.1.r0 = f32[256,256]{1,0:T(8,128)S(1)} collective-permute-done((f32[256,256]{1,0:T(8,128)S(1)}, f32[256,256]{1,0:T(8,128)S(1)}, u32[]{:S(2)}, u32[]{:S(2)}) %collective-permute-start.1) | collective-permute-done | bytes 262176 | tf_op jit(solution)/shard_map/ppermute | solution.py:267
  9.9 2.4 %collective-permute-done.2.r1 = f32[256,256]{1,0:T(8,128)S(1)} collective-permute-done((f32[256,256]{1,0:T(8,128)S(1)}, f32[256,256]{1,0:T(8,128)S(1)}, u32[]{:S(2)}, u32[]{:S(2)}) %collective-permute-start.2) | collective-permute-done | bytes 262176 | tf_op jit(solution)/shard_map/ppermute | solution.py:267
  12.3 1.0 %pair.1 = (f32[256,256]{1,0:T(8,128)S(1)}, f32[256,256]{1,0:T(8,128)S(1)}) custom-call(s32[3]{0:T(128)S(1)} %pad_add_fusion.pos_ref, f32[2,256,256]{2,1,0:T(8,128)S(1)} %bitcast.14, f32[256,256]{1,0:T(8,128)S(1)} %collective-permute-done.1.r0, f32[256,256]{1,0:T(8,128)S(1)} %collective-permute-done.2.r1), custom_call_target="tpu_custom_call" | custom-call | tf_op jit(solution)/shard_map/pair/pallas_call | solution.py:242
  13.3 2.2 %collective-permute-start.3 = (f32[256,256]{1,0:T(8,128)S(1)}, f32[256,256]{1,0:T(8,128)S(1)}, u32[]{:S(2)}, u32[]{:S(2)}) collective-permute-start(f32[256,256]{1,0:T(8,128)S(1)} %get-tuple-element.58.w), channel_id=1, source_target_pairs={{0,3},{1,2},{2,1},{3,0},{4,7},{5,6},{6,5},{7,4},{8,11},{9,10},{10,... | collective-permute-start | bytes 786440 | tf_op jit(solution)/shard_map/ppermute | solution.py:267
  15.5 0.0 collective-permute-start.4
  15.5 0.7 dynamic-slice_bitcast_fusion.tab_ref
  16.2 5.3 %collective-permute-done.3.q0 = f32[256,256]{1,0:T(8,128)S(1)} collective-permute-done((f32[256,256]{1,0:T(8,128)S(1)}, f32[256,256]{1,0:T(8,128)S(1)}, u32[]{:S(2)}, u32[]{:S(2)}) %collective-permute-start.3) | collective-permute-done | bytes 262176 | tf_op jit(solution)/shard_map/ppermute | solution.py:267
  21.5 0.6 collective-permute-done.4.q1
  22.1 1.5 %window.1 = (f32[2,256,256]{2,1,0:T(8,128)S(1)}, f32[256,256]{1,0:T(8,128)S(1)}) custom-call(s32[10]{0:T(128)S(1)} %dynamic-slice_bitcast_fusion.tab_ref, f32[2,256,256]{2,1,0:T(8,128)S(1)} %bitcast.15, f32[256,256]{1,0:T(8,128)S(1)} %collective-permute-done.1.r0, f32[256,256]{1,0:T(8,128)S(1)} %collective-permute-done.2.r1, ...), custom_call_target="tpu_custom_call" | custom-call | tf_op jit(solution)/shard_map/window/pallas_call | solution.py:242
  23.7 3.8 %collective-permute-start.5 = (f32[256,256]{1,0:T(8,128)S(1)}, f32[256,256]{1,0:T(8,128)S(1)}, u32[]{:S(2)}, u32[]{:S(2)}) collective-permute-start(f32[256,256]{1,0:T(8,128)S(1)} %get-tuple-element.61), channel_id=1, source_target_pairs={{0,4},{1,5},{2,6},{3,7},{4,8},{5,9},{6,10},{7,11},{8,12},{9,13},{1... | collective-permute-start | bytes 786440 | tf_op jit(solution)/shard_map/ppermute | solution.py:271
  27.5 2.4 %collective-permute-start.6 = (f32[256,256]{1,0:T(8,128)S(1)}, f32[256,256]{1,0:T(8,128)S(1)}, u32[]{:S(2)}, u32[]{:S(2)}) collective-permute-start(f32[256,256]{1,0:T(8,128)S(1)} %get-tuple-element.61), channel_id=1, source_target_pairs={{0,8},{1,9},{2,10},{3,11},{4,12},{5,13},{6,14},{7,15},{16,24},{17,... | collective-permute-start | bytes 786440 | tf_op jit(solution)/shard_map/ppermute | solution.py:271
  29.9 0.7 collective-permute-start.7
  30.6 6.5 %collective-permute-done.5.t1 = f32[256,256]{1,0:T(8,128)S(1)} collective-permute-done((f32[256,256]{1,0:T(8,128)S(1)}, f32[256,256]{1,0:T(8,128)S(1)}, u32[]{:S(2)}, u32[]{:S(2)}) %collective-permute-start.5) | collective-permute-done | bytes 262176 | tf_op jit(solution)/shard_map/ppermute | solution.py:271
  37.0 0.6 entry.1.own
  37.7 0.3 collective-permute-start.8
  37.9 6.4 %collective-permute-done.8.other = f32[256,256]{1,0:T(8,128)S(1)} collective-permute-done((f32[256,256]{1,0:T(8,128)S(1)}, f32[256,256]{1,0:T(8,128)S(1)}, u32[]{:S(2)}, u32[]{:S(2)}) %collective-permute-start.8) | collective-permute-done | bytes 262176 | tf_op jit(solution)/shard_map/ppermute | solution.py:267
  44.3 16.7 %factor.1 = (f32[4,256,256]{2,1,0:T(8,128)S(1)}, f32[4,256,256]{2,1,0:T(8,128)S(1)}, f32[8,128]{1,0:T(8,128)S(1)}) custom-call(s32[3]{0:T(128)S(1)} %pad_add_fusion.pos_ref, f32[2,256,256]{2,1,0:T(8,128)S(1)} %get-tuple-element.60.prev_ref, f32[256,256]{1,0:T(8,128)S(1)} %entry.1.own, f32[256,256]{1,0:T(8,128)S(1)} %collective-permute-done.8.other, ...), custom_call_target="tpu_custom_call" | custom-call | tf_op jit(solution)/shard_map/factor/pallas_call | solution.py:242
  61.0 1.4 %collective-permute-start.10 = (f32[8,128]{1,0:T(8,128)S(1)}, f32[8,128]{1,0:T(8,128)S(1)}, u32[]{:S(2)}, u32[]{:S(2)}) collective-permute-start(f32[8,128]{1,0:T(8,128)S(1)} %get-tuple-element.66), channel_id=1, source_target_pairs={{0,2},{1,3},{2,0},{3,1},{4,6},{5,7},{6,4},{7,5},{8,10},{9,11},{10,... | collective-permute-start | bytes 12296 | tf_op jit(solution)/shard_map/ppermute | solution.py:267
  62.4 1.4 %collective-permute-start.11 = (f32[8,128]{1,0:T(8,128)S(1)}, f32[8,128]{1,0:T(8,128)S(1)}, u32[]{:S(2)}, u32[]{:S(2)}) collective-permute-start(f32[8,128]{1,0:T(8,128)S(1)} %get-tuple-element.66), channel_id=1, source_target_pairs={{0,3},{1,0},{2,1},{3,2},{4,7},{5,4},{6,5},{7,6},{8,11},{9,8},{10,9... | collective-permute-start | bytes 12296 | tf_op jit(solution)/shard_map/ppermute | solution.py:267
  63.7 0.7 collective-permute-start.9
  64.4 1.8 %collective-permute-done.10 = f32[8,128]{1,0:T(8,128)S(1)} collective-permute-done((f32[8,128]{1,0:T(8,128)S(1)}, f32[8,128]{1,0:T(8,128)S(1)}, u32[]{:S(2)}, u32[]{:S(2)}) %collective-permute-start.10) | collective-permute-done | bytes 4128 | tf_op jit(solution)/shard_map/ppermute | solution.py:267
  66.2 2.4 %collective-permute-done.9 = f32[8,128]{1,0:T(8,128)S(1)} collective-permute-done((f32[8,128]{1,0:T(8,128)S(1)}, f32[8,128]{1,0:T(8,128)S(1)}, u32[]{:S(2)}, u32[]{:S(2)}) %collective-permute-start.9) | collective-permute-done | bytes 4128 | tf_op jit(solution)/shard_map/ppermute | solution.py:267
  68.5 2.8 %collective-permute-start.12 = (f32[8,128]{1,0:T(8,128)S(1)}, f32[8,128]{1,0:T(8,128)S(1)}, u32[]{:S(2)}, u32[]{:S(2)}) collective-permute-start(f32[8,128]{1,0:T(8,128)S(1)} %maximum_maximum_fusion.1), channel_id=1, source_target_pairs={{0,4},{1,5},{2,6},{3,7},{4,8},{5,9},{6,10},{7,11},{8,12},{9,13},{1... | collective-permute-start | bytes 12296 | tf_op jit(solution)/shard_map/ppermute | solution.py:275
  71.4 5.3 %collective-permute-start.13 = (f32[8,128]{1,0:T(8,128)S(1)}, f32[8,128]{1,0:T(8,128)S(1)}, u32[]{:S(2)}, u32[]{:S(2)}) collective-permute-start(f32[8,128]{1,0:T(8,128)S(1)} %maximum_maximum_fusion.1), channel_id=1, source_target_pairs={{0,8},{1,9},{2,10},{3,11},{4,12},{5,13},{6,14},{7,15},{8,0},{9,1},... | collective-permute-start | bytes 12296 | tf_op jit(solution)/shard_map/ppermute | solution.py:275
  76.6 2.5 %collective-permute-start.14 = (f32[8,128]{1,0:T(8,128)S(1)}, f32[8,128]{1,0:T(8,128)S(1)}, u32[]{:S(2)}, u32[]{:S(2)}) collective-permute-start(f32[8,128]{1,0:T(8,128)S(1)} %maximum_maximum_fusion.1), channel_id=1, source_target_pairs={{0,12},{1,13},{2,14},{3,15},{4,0},{5,1},{6,2},{7,3},{8,4},{9,5},{1... | collective-permute-start | bytes 12296 | tf_op jit(solution)/shard_map/ppermute | solution.py:275
  79.2 5.9 %finish.1 = (f32[2,256,256]{2,1,0:T(8,128)}, f32[2,256,256]{2,1,0:T(8,128)}) custom-call(f32[4,256,256]{2,1,0:T(8,128)S(1)} %get-tuple-element.62.m_ref, f32[4,256,256]{2,1,0:T(8,128)S(1)} %get-tuple-element.63.x_ref, f32[2,256,256]{2,1,0:T(8,128)S(1)} %bitcast.17, f32[2,256,256]{2,1,0:T(8,128)S(1)} %bitcast.19), custom_call_target="tpu_custom_call" | custom-call | tf_op jit(solution)/shard_map/finish/pallas_call | solution.py:242
  85.1 0.0 collective-permute-done.14
  85.1 0.6 slice.13
  (14 shorter events, 0.1 us)
Async XLA Ops:
  0.6 11.7 %copy-start = (f32[1,2,1,256,256]{4,3,2,1,0:T(8,128)S(1)}, f32[1,2,1,256,256]{4,3,2,1,0:T(8,128)}, u32[]{:S(2)}) copy-start(f32[1,2,1,256,256]{4,3,2,1,0:T(8,128)} %param.6) | copy-start | bytes 1572868
  1.8 8.1 %collective-permute-start.1 = (f32[256,256]{1,0:T(8,128)S(1)}, f32[256,256]{1,0:T(8,128)S(1)}, u32[]{:S(2)}, u32[]{:S(2)}) collective-permute-start(f32[256,256]{1,0:T(8,128)S(1)} %get-tuple-element.88), channel_id=1, source_target_pairs={{0,1},{1,0},{2,3},{3,2},{4,5},{5,4},{6,7},{7,6},{8,9},{9,8},{10,11... | collective-permute-start | bytes 786440 | tf_op jit(solution)/shard_map/ppermute | solution.py:267
  3.3 9.0 %collective-permute-start.2 = (f32[256,256]{1,0:T(8,128)S(1)}, f32[256,256]{1,0:T(8,128)S(1)}, u32[]{:S(2)}, u32[]{:S(2)}) collective-permute-start(f32[256,256]{1,0:T(8,128)S(1)} %get-tuple-element.87), channel_id=1, source_target_pairs={{0,3},{1,2},{2,1},{3,0},{4,7},{5,6},{6,5},{7,4},{8,11},{9,10},{10,... | collective-permute-start | bytes 786440 | tf_op jit(solution)/shard_map/ppermute | solution.py:267
  13.3 8.2 %collective-permute-start.3 = (f32[256,256]{1,0:T(8,128)S(1)}, f32[256,256]{1,0:T(8,128)S(1)}, u32[]{:S(2)}, u32[]{:S(2)}) collective-permute-start(f32[256,256]{1,0:T(8,128)S(1)} %get-tuple-element.58.w), channel_id=1, source_target_pairs={{0,3},{1,2},{2,1},{3,0},{4,7},{5,6},{6,5},{7,4},{8,11},{9,10},{10,... | collective-permute-start | bytes 786440 | tf_op jit(solution)/shard_map/ppermute | solution.py:267
  15.5 6.6 %collective-permute-start.4 = (f32[256,256]{1,0:T(8,128)S(1)}, f32[256,256]{1,0:T(8,128)S(1)}, u32[]{:S(2)}, u32[]{:S(2)}) collective-permute-start(f32[256,256]{1,0:T(8,128)S(1)} %get-tuple-element.59), channel_id=1, source_target_pairs={{0,1},{1,0},{2,3},{3,2},{4,5},{5,4},{6,7},{7,6},{8,9},{9,8},{10,11... | collective-permute-start | bytes 786440 | tf_op jit(solution)/shard_map/ppermute | solution.py:267
  23.7 13.4 %collective-permute-start.5 = (f32[256,256]{1,0:T(8,128)S(1)}, f32[256,256]{1,0:T(8,128)S(1)}, u32[]{:S(2)}, u32[]{:S(2)}) collective-permute-start(f32[256,256]{1,0:T(8,128)S(1)} %get-tuple-element.61), channel_id=1, source_target_pairs={{0,4},{1,5},{2,6},{3,7},{4,8},{5,9},{6,10},{7,11},{8,12},{9,13},{1... | collective-permute-start | bytes 786440 | tf_op jit(solution)/shard_map/ppermute | solution.py:271
  27.5 9.5 %collective-permute-start.6 = (f32[256,256]{1,0:T(8,128)S(1)}, f32[256,256]{1,0:T(8,128)S(1)}, u32[]{:S(2)}, u32[]{:S(2)}) collective-permute-start(f32[256,256]{1,0:T(8,128)S(1)} %get-tuple-element.61), channel_id=1, source_target_pairs={{0,8},{1,9},{2,10},{3,11},{4,12},{5,13},{6,14},{7,15},{16,24},{17,... | collective-permute-start | bytes 786440 | tf_op jit(solution)/shard_map/ppermute | solution.py:271
  29.9 7.2 %collective-permute-start.7 = (f32[256,256]{1,0:T(8,128)S(1)}, f32[256,256]{1,0:T(8,128)S(1)}, u32[]{:S(2)}, u32[]{:S(2)}) collective-permute-start(f32[256,256]{1,0:T(8,128)S(1)} %get-tuple-element.61), channel_id=1, source_target_pairs={{0,12},{1,13},{2,14},{3,15},{16,28},{17,29},{18,30},{19,31},{32,44... | collective-permute-start | bytes 786440 | tf_op jit(solution)/shard_map/ppermute | solution.py:271
  37.7 6.6 %collective-permute-start.8 = (f32[256,256]{1,0:T(8,128)S(1)}, f32[256,256]{1,0:T(8,128)S(1)}, u32[]{:S(2)}, u32[]{:S(2)}) collective-permute-start(f32[256,256]{1,0:T(8,128)S(1)} %entry.1.own), channel_id=1, source_target_pairs={{0,1},{1,0},{2,3},{3,2},{4,5},{5,4},{6,7},{7,6},{8,9},{9,8},{10,11... | collective-permute-start | bytes 786440 | tf_op jit(solution)/shard_map/ppermute | solution.py:267
  44.3 34.9 %copy-start.1 = (f32[1,2,1,256,256]{4,3,2,1,0:T(8,128)S(1)}, f32[1,2,1,256,256]{4,3,2,1,0:T(8,128)}, u32[]{:S(2)}) copy-start(f32[1,2,1,256,256]{4,3,2,1,0:T(8,128)} %param.5) | copy-start | bytes 1572868
  61.0 5.2 %collective-permute-start.10 = (f32[8,128]{1,0:T(8,128)S(1)}, f32[8,128]{1,0:T(8,128)S(1)}, u32[]{:S(2)}, u32[]{:S(2)}) collective-permute-start(f32[8,128]{1,0:T(8,128)S(1)} %get-tuple-element.66), channel_id=1, source_target_pairs={{0,2},{1,3},{2,0},{3,1},{4,6},{5,7},{6,4},{7,5},{8,10},{9,11},{10,... | collective-permute-start | bytes 12296 | tf_op jit(solution)/shard_map/ppermute | solution.py:267
  62.4 3.8 %collective-permute-start.11 = (f32[8,128]{1,0:T(8,128)S(1)}, f32[8,128]{1,0:T(8,128)S(1)}, u32[]{:S(2)}, u32[]{:S(2)}) collective-permute-start(f32[8,128]{1,0:T(8,128)S(1)} %get-tuple-element.66), channel_id=1, source_target_pairs={{0,3},{1,0},{2,1},{3,2},{4,7},{5,4},{6,5},{7,6},{8,11},{9,8},{10,9... | collective-permute-start | bytes 12296 | tf_op jit(solution)/shard_map/ppermute | solution.py:267
  63.7 4.8 %collective-permute-start.9 = (f32[8,128]{1,0:T(8,128)S(1)}, f32[8,128]{1,0:T(8,128)S(1)}, u32[]{:S(2)}, u32[]{:S(2)}) collective-permute-start(f32[8,128]{1,0:T(8,128)S(1)} %get-tuple-element.66), channel_id=1, source_target_pairs={{0,1},{1,2},{2,3},{3,0},{4,5},{5,6},{6,7},{7,4},{8,9},{9,10},{10,1... | collective-permute-start | bytes 12296 | tf_op jit(solution)/shard_map/ppermute | solution.py:267
  68.5 16.6 %collective-permute-start.12 = (f32[8,128]{1,0:T(8,128)S(1)}, f32[8,128]{1,0:T(8,128)S(1)}, u32[]{:S(2)}, u32[]{:S(2)}) collective-permute-start(f32[8,128]{1,0:T(8,128)S(1)} %maximum_maximum_fusion.1), channel_id=1, source_target_pairs={{0,4},{1,5},{2,6},{3,7},{4,8},{5,9},{6,10},{7,11},{8,12},{9,13},{1... | collective-permute-start | bytes 12296 | tf_op jit(solution)/shard_map/ppermute | solution.py:275
  71.4 13.7 %collective-permute-start.13 = (f32[8,128]{1,0:T(8,128)S(1)}, f32[8,128]{1,0:T(8,128)S(1)}, u32[]{:S(2)}, u32[]{:S(2)}) collective-permute-start(f32[8,128]{1,0:T(8,128)S(1)} %maximum_maximum_fusion.1), channel_id=1, source_target_pairs={{0,8},{1,9},{2,10},{3,11},{4,12},{5,13},{6,14},{7,15},{8,0},{9,1},... | collective-permute-start | bytes 12296 | tf_op jit(solution)/shard_map/ppermute | solution.py:275
  76.6 8.5 %collective-permute-start.14 = (f32[8,128]{1,0:T(8,128)S(1)}, f32[8,128]{1,0:T(8,128)S(1)}, u32[]{:S(2)}, u32[]{:S(2)}) collective-permute-start(f32[8,128]{1,0:T(8,128)S(1)} %maximum_maximum_fusion.1), channel_id=1, source_target_pairs={{0,12},{1,13},{2,14},{3,15},{4,0},{5,1},{6,2},{7,3},{8,4},{9,5},{1... | collective-permute-start | bytes 12296 | tf_op jit(solution)/shard_map/ppermute | solution.py:275
where the time goes:
time: 86.9 us; the launch traced here: 86.6 us
  waiting for transfers between devices  29.7 us (34%)
  starting transfers between devices  27 us (31%)
  Pallas kernels  25.7 us (30%)
  local copies, waits for them, and re-layouts  2.45 us (3%)
  between operations  1.62 us (2%)
    pallas_call x5, Pallas kernels, run(): pl.pallas_call(kernel, out_shape=outs, in_specs=specs, out_specs=jax.tree...  25.7 us
    ppermute x8, waiting for transfers between devices, x_move(): lax.ppermute(value, 'row', [(i, i // 4 * 4 + to(i % 4)) for i in range(16)])  23.2 us
    ppermute x3, starting transfers between devices, z_ring(): lax.ppermute(value, 'row', [(i, (i + 4 * s) % 16) for i in range(16)])  10.6 us
    ppermute x8, starting transfers between devices, x_move(): lax.ppermute(value, 'row', [(i, i // 4 * 4 + to(i % 4)) for i in range(16)])  9.52 us
    ppermute x3, starting transfers between devices, z_move(): lax.ppermute(value, 'row', [(i, i + 4 * s) for i in range(16 - 4 * s)])  6.87 us
    ppermute x3, waiting for transfers between devices, z_move(): lax.ppermute(value, 'row', [(i, i + 4 * s) for i in range(16 - 4 * s)])  6.47 us
  transfers between devices with their start and end apart: 14, of which 8 were waited for; matrix products, arithmetic and copies ran while one was open for 1% of the time, Pallas kernels for 7%

commit v1 on v0

v1 whole, which is shorter than its diff:
```python
import functools

import jax
import jax.numpy as jnp
from jax import lax
from jax.experimental import pallas as pl
from jax.experimental.pallas import tpu as pltpu
from jax.sharding import PartitionSpec as P

D = 256
B = 16
HALF = 128
SOLVE = 3
GRAM = 6
F32 = jnp.float32
BF16 = jnp.bfloat16
LIMIT = 17.97
ORTHO2 = 4.0e-4


def dg(a, b, ca, cb):
    return lax.dot_general(a, b, (((ca,), (cb,)), ((), ())), preferred_element_type=F32)


def split2(x):
    h = x.astype(BF16)
    return h, (x - h.astype(F32)).astype(BF16)


def split3(x):
    h = x.astype(BF16)
    r = x - h.astype(F32)
    m = r.astype(BF16)
    return h, m, (r - m.astype(F32)).astype(BF16)


def mm(a, b, ca=1, cb=0, passes=6):
    if passes == 1:
        return dg(a.astype(BF16), b.astype(BF16), ca, cb)
    if passes == 3:
        ah, al = split2(a)
        bh, bl = split2(b)
        return dg(al, bh, ca, cb) + dg(ah, bl, ca, cb) + dg(ah, bh, ca, cb)
    ah, am, al = split3(a)
    bh, bm, bl = split3(b)
    small = dg(al, bh, ca, cb) + dg(ah, bl, ca, cb) + dg(am, bm, ca, cb)
    return (small + (dg(am, bh, ca, cb) + dg(ah, bm, ca, cb))) + dg(ah, bh, ca, cb)


def square_iota():
    return (
        lax.broadcasted_iota(jnp.int32, (D, D), 0),
        lax.broadcasted_iota(jnp.int32, (D, D), 1),
    )


def pick(value, lanes):
    return jnp.take_along_axis(value, lanes, axis=1)


def row_of(value, r):
    return jnp.broadcast_to(value[r : r + 1, :], (8, HALF))


def chol_inv(refs):
    nb = len(refs)
    row = lax.broadcasted_iota(jnp.int32, (8, HALF), 0)
    lane = lax.broadcasted_iota(jnp.int32, (8, HALF), 1)
    for h in range(2):
        n0 = h * HALF
        rows = lax.broadcasted_iota(jnp.int32, (D - n0, HALF), 0) + n0
        lanes = lax.broadcasted_iota(jnp.int32, (D - n0, HALF), 1) + n0

        def panel(p, carry, h=h, n0=n0, rows=rows, lanes=lanes):
            j = pl.multiple_of(p * B, B)
            k = pl.multiple_of(n0 + p * B, B)
            first = (lane >= j) & (lane < j + 8)
            second = (lane >= j + 8) & (lane < j + B)
            unit = jnp.where(lane - j == row, 1.0, 0.0)
            unit2 = jnp.where(lane - j - 8 == row, 1.0, 0.0)
            at = [jnp.full((8, HALF), j + c, jnp.int32) for c in range(B)]
            below = rows >= k + B
            own = (lanes >= k) & (lanes < k + B)
            tops = [[a[pl.ds(k, 8), i * HALF : (i + 1) * HALF] for i in range(2)] for a in refs]
            bots = [[a[pl.ds(k + 8, 8), i * HALF : (i + 1) * HALF] for i in range(2)] for a in refs]
            ats = [pick(t[h], at[c]) for c in range(8) for t in tops]
            cts = [ats[n::nb] for n in range(nb)]
            ats = [pick(t[h], at[c]) for c in range(8) for t in bots]
            cbs = [ats[n::nb] for n in range(nb)]
            pts = [jnp.ones((8, HALF), F32) for _ in range(nb)]
            pbs = [jnp.ones((8, HALF), F32) for _ in range(nb)]
            for n in range(nb):
                tops[n][h] = jnp.where(first, unit, tops[n][h])
                bots[n][h] = jnp.where(first, 0.0, bots[n][h])
            for r in range(8):
                for n in range(nb):
                    top, bot, ct, cb = tops[n], bots[n], cts[n], cbs[n]
                    piv = row_of(ct[r], r)
                    inv = 1.0 / piv
                    pts[n] = jnp.where(row == r, piv, pts[n])
                    lt = jnp.where(row > r, ct[r] * inv, 0.0)
                    lb = cb[r] * inv
                    for c in range(r + 1, 8):
                        u = row_of(ct[c], r)
                        ct[c] = ct[c] - lt * u
                        cb[c] = cb[c] - lb * u
                    for i in range(2):
                        u = row_of(top[i], r)
                        if r < 7:
                            top[i] = top[i] - lt * u
                        bot[i] = bot[i] - lb * u
            ats = [pick(t[h], at[8 + c]) for c in range(8) for t in bots]
            cts = [ats[n::nb] for n in range(nb)]
            for n in range(nb):
                tops[n][h] = jnp.where(second, 0.0, tops[n][h])
                bots[n][h] = jnp.where(second, unit2, bots[n][h])
            for r in range(8):
                for n in range(nb):
                    bot, ct = bots[n], cts[n]
                    piv = row_of(ct[r], r)
                    pbs[n] = jnp.where(row == r, piv, pbs[n])
                    if r == 7:
                        continue
                    lb = jnp.where(row > r, ct[r] * (1.0 / piv), 0.0)
                    for c in range(r + 1, 8):
                        ct[c] = ct[c] - lb * row_of(ct[c], r)
                    for i in range(2):
                        bot[i] = bot[i] - lb * row_of(bot[i], r)
            scaled = []
            for n in range(nb):
                rt = lax.rsqrt(pts[n])
                rb = lax.rsqrt(pbs[n])
                scaled.append(
                    jnp.concatenate(
                        [
                            jnp.concatenate([tops[n][0] * rt, tops[n][1] * rt], 1),
                            jnp.concatenate([bots[n][0] * rb, bots[n][1] * rb], 1),
                        ],
                        0,
                    )
                )
            updates = []
            for n in range(nb):
                hi, md, lo = split3(scaled[n])
                left = jnp.concatenate([lo, hi, md, md, hi, hi], 0)
                right = jnp.concatenate([hi, lo, md, hi, md, hi], 0)
                updates.append(dg(left[:, n0:], right, 0, 0))
            for n in range(nb):
                for i in range(2):
                    old = refs[n][n0:, i * HALF : (i + 1) * HALF]
                    kept = jnp.where(own, 0.0, old) if i == h else old
                    now = kept - updates[n][:, i * HALF : (i + 1) * HALF]
                    refs[n][n0:, i * HALF : (i + 1) * HALF] = jnp.where(below, now, old)
                refs[n][pl.ds(k, B), :] = scaled[n]
            return carry

        lax.fori_loop(0, HALF // B, panel, 0)


TABLE = (
    (6, 1, 3, 8, 0, 0, 2, 7, 7, 9),
    (5, 4, 0, 0, 0, 0, 1, 2, 6, 8),
    (4, 5, 3, 6, 0, 0, 2, 5, 9, 8),
    (6, 3, 1, 8, 2, 5, 3, 10, 8, 9),
)


def eye_value():
    r, c = square_iota()
    return jnp.where(r == c, 1.0, 0.0)


def pair_kernel(pos_ref, c_ref, r0, r1, w_ref, v_ref, buf):
    x = pos_ref[1]
    odd = lax.rem(x, 2)
    high = x // 2
    buf[odd] = c_ref[0]
    buf[1 - odd] = r0[...]
    buf[2 + high] = c_ref[1]
    buf[3 - high] = r1[...]
    w_ref[...] = mm(buf[1], buf[0])
    outer = (x == 0) | (x == 3)

    @pl.when(outer)
    def _():
        v_ref[...] = buf[2]

    @pl.when(jnp.logical_not(outer))
    def _():
        v_ref[...] = mm(buf[3], buf[2])


def window_kernel(tab_ref, c_ref, r0, r1, w, q0, q1, prev_ref, t_ref, buf):
    buf[0] = c_ref[0]
    buf[1] = c_ref[1]
    for k, ref in enumerate((r0, r1, w, q0, q1)):
        buf[2 + k] = ref[...]
    buf[7] = eye_value()

    def step(i, _):
        buf[8 + i] = mm(buf[tab_ref[2 * i]], buf[tab_ref[2 * i + 1]])
        return 0

    lax.fori_loop(0, tab_ref[6], step, 0)
    prev_ref[0] = buf[tab_ref[7]]
    prev_ref[1] = buf[tab_ref[8]]
    t_ref[...] = buf[tab_ref[9]]


def entry_kernel(pos_ref, t1, t2, t3, e_ref, buf):
    z = pos_ref[0]
    buf[0] = eye_value()
    for k, ref in enumerate((t1, t2, t3)):
        buf[1 + k] = ref[...]
    e_ref[...] = buf[z]

    def step(i, _):
        e_ref[...] = mm(buf[z - 1 - i], e_ref[...])
        return 0

    lax.fori_loop(0, z - 1, step, 0)


def refinement(y, passes):
    r, c = square_iota()
    err = mm(y, y, 0, 0, passes=3) - jnp.where(r == c, 1.0, 0.0)
    upper = jnp.where(c > r, err, jnp.where(c == r, 0.5 * err, 0.0))
    return mm(y, upper, passes=passes), err


def total_of(value):
    return jnp.sum(jnp.sum(value, axis=0, keepdims=True), axis=1, keepdims=True)


def solve_kernel(
    pos_ref, prev_ref, own, other, c_ref, d_ref, n_ref, r_ref, before_ref, stat_ref, *scratch
):
    refs, m_ref, now = scratch[:4], scratch[4], scratch[5]
    mine = pos_ref[2]
    now[mine] = own[...]
    now[1 - mine] = other[...]

    def products(t, carry):
        left = [jnp.where(t == 0, prev_ref[m], c_ref[m]) for m in range(2)]
        out = [mm(left[m], now[m], passes=SOLVE) for m in range(2)]
        for m in range(2):
            now[m] = out[m]
            m_ref[t, m] = out[m]
        return carry

    lax.fori_loop(0, 2, products, 0)
    for m in range(2):
        before_ref[m] = m_ref[0, m]

    def grams(t, carry):
        out = [mm(m_ref[t, m], m_ref[t, m], 0, 0, passes=GRAM) for m in range(2)]
        for m in range(2):
            now[m] = out[m]

        @pl.when(t == 0)
        def _():
            for m in range(2):
                refs[m][...] = now[m]

        @pl.when(t == 1)
        def _():
            for m in range(2):
                refs[2 + m][...] = now[m]

        return carry

    lax.fori_loop(0, 2, grams, 0)
    chol_inv(refs)
    r, c = square_iota()

    def factors(t, worst):
        inv = [
            jnp.where(c <= r, jnp.where(t == 0, refs[m][...], refs[2 + m][...]), 0.0)
            for m in range(2)
        ]
        ys = [mm(m_ref[t, m], inv[m], 1, 1, passes=SOLVE) for m in range(2)]
        for m in range(2):
            change, err = refinement(ys[m], 1)
            m_ref[t, m] = ys[m] - change
            worst = jnp.maximum(worst, jnp.where(total_of(err * err) < ORTHO2, 0.0, 1.0))
        return worst

    worst = lax.fori_loop(0, 2, factors, jnp.zeros((1, 1), F32))
    stat_ref[...] = jnp.broadcast_to(worst, (8, HALF))

    def results(t, carry):
        left = [jnp.where(t == 0, c_ref[m], d_ref[m]) for m in range(2)]
        part = [mm(left[m], m_ref[t, m], passes=SOLVE) for m in range(2)]
        out = [mm(m_ref[1, m], part[m], 0, 0, passes=SOLVE) for m in range(2)]
        for m in range(2):
            now[m] = out[m]

        @pl.when(t == 0)
        def _():
            for m in range(2):
                r_ref[m] = jnp.where(c >= r, now[m], 0.0)

        @pl.when(t == 1)
        def _():
            for m in range(2):
                n_ref[m] = now[m]

        return carry

    lax.fori_loop(0, 2, results, 0)


def gauge_kernel(pos_ref, prev_ref, c_ref, out_ref, g_ref, b_ref):
    eye = eye_value()
    row = lax.broadcasted_iota(jnp.int32, (8, HALF), 0)
    lane = lax.broadcasted_iota(jnp.int32, (8, HALF), 1)
    norms = []
    for m in range(2):
        full = mm(c_ref[m], prev_ref[m], passes=3)
        gram = mm(full, full, 0, 0, passes=3)
        norm = jnp.sqrt(total_of(gram * gram))
        g_ref[m] = gram / norm
    for m in range(2):
        b_ref[m] = mm(g_ref[m], g_ref[m], passes=3)
    for _ in range(3):
        for m in range(2):
            b_ref[m] = mm(b_ref[m], b_ref[m], passes=3)
    for m in range(2):
        top = jnp.exp(0.0625 * 0.5 * jnp.log(total_of(b_ref[m] * b_ref[m]))) * 1.02
        b_ref[m] = eye - g_ref[m] / top
    for t in range(10):
        for m in range(2):
            b_ref[m] = mm(b_ref[m], b_ref[m], passes=3 if t < 5 else 1)
    out = jnp.zeros((8, HALF), F32)
    for m in range(2):
        norm = jnp.maximum(total_of(b_ref[m] * b_ref[m]), 1.0e-30)
        low = jnp.maximum(1.0 - jnp.exp(jnp.log(norm) / 2048.0), 1.0e-9)
        value = jnp.broadcast_to(-jnp.log(low), (8, HALF))
        out = jnp.where((row == m) & (lane == pos_ref[3]), value, out)
    out_ref[...] = out


def decide_kernel(bound_ref, stat_ref, out_ref):
    v = bound_ref[...]
    lane = lax.broadcasted_iota(jnp.int32, (8, HALF), 1)
    bound = v
    for z in range(3):
        whole = jnp.sum(jnp.where(lane == 4 * z + 3, v, 0.0), axis=1, keepdims=True)
        bound = bound + jnp.where(lane >= 4 * z + 4, whole, 0.0)
    bound = jnp.where(lane < 16, bound, 0.0)
    worst = jnp.max(jnp.max(bound, axis=0, keepdims=True), axis=1, keepdims=True)[0, 0]
    failed = jnp.max(jnp.max(stat_ref[...], axis=0, keepdims=True), axis=1, keepdims=True)[0, 0]
    fine = worst < LIMIT
    out_ref[0] = jnp.where(fine, 0, 16)
    out_ref[1] = jnp.where(fine & (failed > 0.0), 1, 0)


def chain_kernel(before_ref, c_ref, d_ref, n_ref, r_ref, q_ref, a_ref):
    r, c = square_iota()
    lane = lax.broadcasted_iota(jnp.int32, (1, D), 1)

    def orthonormal(m):
        q_ref[m] = n_ref[m]

        def column(k, _):
            a = a_ref[...]
            row = a_ref[pl.ds(k, 1), :]
            pivot = jnp.sum(jnp.where(lane == k, row, 0.0), axis=1, keepdims=True)
            rs = lax.rsqrt(pivot)
            row = jnp.where(lane == k, 1.0, row) * rs
            factor_col = jnp.sum(jnp.where(c == k, a, 0.0), axis=1, keepdims=True) * rs
            below = jnp.where(c == k, 0.0, a) - factor_col * row
            a_ref[...] = jnp.where(r > k, below, jnp.where(r == k, row, a))
            return 0

        def turn(t, carry):
            gram = mm(q_ref[m], q_ref[m], 0, 0)
            mean = total_of(jnp.where(r == c, gram, 0.0)) / D
            shift = jnp.where(t == 0, 1.0e-5, 0.0) * mean
            a_ref[...] = gram + jnp.where(r == c, shift, 0.0)
            lax.fori_loop(0, D, column, 0)
            q_ref[m] = mm(q_ref[m], jnp.where(c <= r, a_ref[...], 0.0), 1, 1)
            return carry

        def again(_, carry):
            q_ref[m] = q_ref[m] - refinement(q_ref[m], 3)[0]
            return carry

        lax.fori_loop(0, 3, turn, 0)
        lax.fori_loop(0, 2, again, 0)

    def one(m, carry):
        def half(t, carry):
            n_ref[m] = jnp.where(t == 0, before_ref[m], mm(c_ref[m], q_ref[m]))
            orthonormal(m)
            return carry

        q_ref[m] = before_ref[m]
        lax.fori_loop(0, 2, half, 0)
        q = q_ref[m]
        r_ref[m] = jnp.where(c >= r, mm(q, n_ref[m], 0, 0), 0.0)
        n_ref[m] = mm(mm(q, d_ref[m], 0, 0), q)
        return carry

    lax.fori_loop(0, 2, one, 0)


def struct(*shape):
    return jax.ShapeDtypeStruct(shape, F32)


VMEM = pl.BlockSpec(memory_space=pltpu.VMEM)
SMEM = pl.BlockSpec(memory_space=pltpu.SMEM)


def call(kernel, outs, scratch, name, table=True):
    def run(*args):
        specs = [VMEM] * len(args)
        if table:
            specs[0] = SMEM
        return pl.pallas_call(
            kernel,
            out_shape=outs,
            in_specs=specs,
            out_specs=jax.tree.map(lambda _: VMEM, outs),
            scratch_shapes=[pltpu.VMEM(shape, F32) for shape in scratch],
            compiler_params=pltpu.CompilerParams(vmem_limit_bytes=48 * 2**20),
            name=name,
        )(*args)

    return run


SQUARE = struct(D, D)
TWO = struct(2, D, D)
TILE = struct(8, HALF)
pair = call(pair_kernel, (SQUARE, SQUARE), [(4, D, D)], "pair")
window = call(window_kernel, (TWO, SQUARE), [(11, D, D)], "window")
entry = call(entry_kernel, SQUARE, [(4, D, D)], "entry")
solve = call(
    solve_kernel,
    (TWO, TWO, TWO, TILE),
    [(D, D)] * 4 + [(2, 2, D, D), (2, D, D)],
    "solve",
)
gauge = call(gauge_kernel, TILE, [(2, D, D), (2, D, D)], "gauge")
chain = call(chain_kernel, (TWO, TWO, TWO), [(D, D)], "chain", table=False)


def decide(bound, stat):
    return pl.pallas_call(
        decide_kernel,
        out_shape=jax.ShapeDtypeStruct((2,), jnp.int32),
        in_specs=[VMEM, VMEM],
        out_specs=SMEM,
        name="decide",
    )(bound, stat)


def x_move(value, to):
    return lax.ppermute(value, "row", [(i, (i // 4) * 4 + to(i % 4)) for i in range(16)])


def z_move(value, s):
    return lax.ppermute(value, "row", [(i, i + 4 * s) for i in range(16 - 4 * s)])


def z_ring(value, s):
    return lax.ppermute(value, "row", [(i, (i + 4 * s) % 16) for i in range(16)])


def x_pairs(value):
    return x_move(value, lambda x: x ^ 1)


def x_mirror(value):
    return x_move(value, lambda x: 3 - x)


def largest_in_row(value):
    moved = [x_move(value, lambda x, s=s: (x + s) % 4) for s in (1, 2, 3)]
    value = functools.reduce(jnp.maximum, moved, value)
    return functools.reduce(jnp.maximum, [z_ring(value, s) for s in (1, 2, 3)], value)


def shards(diag_blocks, coupling_blocks):
    diagonal = diag_blocks.reshape(2, D, D)
    coupling = coupling_blocks.reshape(2, D, D)
    position = lax.axis_index("row")
    z, x = position // 4, position % 4
    mine = jnp.where((x == 0) | (x == 3), 1, 0)
    pos = jnp.stack([z, x, mine, position]).astype(jnp.int32)
    table = jnp.asarray(TABLE, jnp.int32)[x]

    r0, r1 = x_pairs(coupling[0]), x_mirror(coupling[1])
    w, v = pair(pos, coupling, r0, r1)
    q0, q1 = x_mirror(w), x_pairs(v)
    prev, total = window(table, coupling, r0, r1, w, q0, q1)
    below = [z_move(total, s) for s in (1, 2, 3)]
    bound = largest_in_row(gauge(pos, prev, coupling))
    own = entry(pos, *below)
    new, tri, before, stat = solve(pos, prev, own, x_pairs(own), coupling, diagonal)
    rounds = decide(bound, stat)

    def local(_, carried):
        new, tri, q = chain(carried[0], coupling, diagonal)
        return q, new, tri

    _, new, tri = lax.fori_loop(0, rounds[1], local, (before, new, tri))

    def step(i, carried):
        q, new, tri = carried
        new_now, tri_now, q = chain(q, coupling, diagonal)
        keep = i == position
        new = jnp.where(keep, new_now, new)
        tri = jnp.where(keep, tri_now, tri)
        return lax.ppermute(q, "row", [(j, j + 1) for j in range(15)]), new, tri

    eyes = jnp.broadcast_to(jnp.eye(D, dtype=F32), (2, D, D))
    _, new, tri = lax.fori_loop(0, rounds[0], step, (eyes, new, tri))
    shape = diag_blocks.shape
    return new.reshape(shape), tri.reshape(shape)


def solution(mesh):
    placed = P("section", None, "row", None, None)
    return jax.shard_map(
        shards,
        mesh=mesh,
        in_specs=(placed, placed),
        out_specs=(placed, placed),
        check_vma=False,
    )
```

time: 86.9 us -> 8380 us (96.43)
  Pallas kernels: 25.7 us -> 8100 us
  waiting for transfers between devices: 29.7 us -> 170 us
    pallas_call x5 -> x21, Pallas kernels: 25.7 us -> 8100 us  [run(): pl.pallas_call(kernel, out_shape=outs, in_specs=specs, out_specs=jax.tree...]
    ppermute x0 -> x16, waiting for transfers between devices: none -> 144 us  [step(): return (lax.ppermute(q, 'row', [(j, j + 1) for j in range(15)]), new, tri)]
  transfers between devices with their start and end apart: 14 -> 30, of which waited for: 8 -> 25; matrix products, arithmetic and copies ran while one was open for 1% -> 0% of each run, Pallas kernels for 7% -> 0%
where the time goes in v1:
time: 8380 us
  Pallas kernels  8100 us (97%)
  waiting for transfers between devices  170 us (2%)
    pallas_call x21, Pallas kernels, run(): pl.pallas_call(kernel, out_shape=outs, in_specs=specs, out_specs=jax.tree...  8100 us
  transfers between devices with their start and end apart: 30, of which 25 were waited for; matrix products, arithmetic and copies ran while one was open for 0% of the time, Pallas kernels for 0%

profile of v1, /device:TPU:48, one launch (start us, length us, event | category | flops | bytes accessed | tf_op | source)
XLA Modules:
  0.0 8379.2 jit_solution(11428926764097933439)
XLA Ops:
  59.5 19.2 solve.1
  82.9 8296.1 %while.29 = (s32[]{:T(128)}, f32[2,256,256]{2,1,0:T(8,128)S(1)}, f32[2,256,256]{2,1,0:T(8,128)}, f32[2,256,256]{2,1,0:T(8,128)}, s32[]{:T(128)}, /*index=5*/f32[...) while((s32[]{:T(128)}, f32[2,256,256]{2,1,0:T(8,128)S(1)}, ...), condition=%wide.region_3.4_spmd, body=%wide.region_2.3_spmd.sunk | while | flops 262147 | bytes 5243023 | solution.py:520
  83.5 504.6 %chain.3 = (f32[2,256,256]{2,1,0:T(8,128)S(1)}, f32[2,256,256]{2,1,0:T(8,128)S(1)}, f32[2,256,256]{2,1,0:T(8,128)S(1)}) custom-call(f32[2,256,256]{2,1,0:T(8,128)S(1)} %get-tuple-element.285.before_ref, f32[2,256,256]{2,1,0:T(8,128)S(1)} %get-tuple-element.298.c_ref, f32[2,256,256]{2,1,0:T(8,128)S(1)} %get-tuple-element.299.d_ref), custom_call_target="tpu_custom_call" | custom-call | tf_op jit(solution)/shard_map/while/body/chain/pallas_call | solution.py:421
  602.0 504.6 %chain.3 = (f32[2,256,256]{2,1,0:T(8,128)S(1)}, f32[2,256,256]{2,1,0:T(8,128)S(1)}, f32[2,256,256]{2,1,0:T(8,128)S(1)}) custom-call(f32[2,256,256]{2,1,0:T(8,128)S(1)} %get-tuple-element.285.before_ref, f32[2,256,256]{2,1,0:T(8,128)S(1)} %get-tuple-element.298.c_ref, f32[2,256,256]{2,1,0:T(8,128)S(1)} %get-tuple-element.299.d_ref), custom_call_target="tpu_custom_call" | custom-call | tf_op jit(solution)/shard_map/while/body/chain/pallas_call | solution.py:421
  1110.8 8.9 collective-permute-done
  1120.5 504.6 %chain.3 = (f32[2,256,256]{2,1,0:T(8,128)S(1)}, f32[2,256,256]{2,1,0:T(8,128)S(1)}, f32[2,256,256]{2,1,0:T(8,128)S(1)}) custom-call(f32[2,256,256]{2,1,0:T(8,128)S(1)} %get-tuple-element.285.before_ref, f32[2,256,256]{2,1,0:T(8,128)S(1)} %get-tuple-element.298.c_ref, f32[2,256,256]{2,1,0:T(8,128)S(1)} %get-tuple-element.299.d_ref), custom_call_target="tpu_custom_call" | custom-call | tf_op jit(solution)/shard_map/while/body/chain/pallas_call | solution.py:421
  1629.3 8.9 collective-permute-done
  1638.9 504.6 %chain.3 = (f32[2,256,256]{2,1,0:T(8,128)S(1)}, f32[2,256,256]{2,1,0:T(8,128)S(1)}, f32[2,256,256]{2,1,0:T(8,128)S(1)}) custom-call(f32[2,256,256]{2,1,0:T(8,128)S(1)} %get-tuple-element.285.before_ref, f32[2,256,256]{2,1,0:T(8,128)S(1)} %get-tuple-element.298.c_ref, f32[2,256,256]{2,1,0:T(8,128)S(1)} %get-tuple-element.299.d_ref), custom_call_target="tpu_custom_call" | custom-call | tf_op jit(solution)/shard_map/while/body/chain/pallas_call | solution.py:421
  2147.8 8.9 collective-permute-done
  2157.4 504.6 %chain.3 = (f32[2,256,256]{2,1,0:T(8,128)S(1)}, f32[2,256,256]{2,1,0:T(8,128)S(1)}, f32[2,256,256]{2,1,0:T(8,128)S(1)}) custom-call(f32[2,256,256]{2,1,0:T(8,128)S(1)} %get-tuple-element.285.before_ref, f32[2,256,256]{2,1,0:T(8,128)S(1)} %get-tuple-element.298.c_ref, f32[2,256,256]{2,1,0:T(8,128)S(1)} %get-tuple-element.299.d_ref), custom_call_target="tpu_custom_call" | custom-call | tf_op jit(solution)/shard_map/while/body/chain/pallas_call | solution.py:421
  2665.0 10.1 collective-permute-done
  2675.9 504.6 %chain.3 = (f32[2,256,256]{2,1,0:T(8,128)S(1)}, f32[2,256,256]{2,1,0:T(8,128)S(1)}, f32[2,256,256]{2,1,0:T(8,128)S(1)}) custom-call(f32[2,256,256]{2,1,0:T(8,128)S(1)} %get-tuple-element.285.before_ref, f32[2,256,256]{2,1,0:T(8,128)S(1)} %get-tuple-element.298.c_ref, f32[2,256,256]{2,1,0:T(8,128)S(1)} %get-tuple-element.299.d_ref), custom_call_target="tpu_custom_call" | custom-call | tf_op jit(solution)/shard_map/while/body/chain/pallas_call | solution.py:421
  3184.7 8.9 collective-permute-done
  3194.3 504.6 %chain.3 = (f32[2,256,256]{2,1,0:T(8,128)S(1)}, f32[2,256,256]{2,1,0:T(8,128)S(1)}, f32[2,256,256]{2,1,0:T(8,128)S(1)}) custom-call(f32[2,256,256]{2,1,0:T(8,128)S(1)} %get-tuple-element.285.before_ref, f32[2,256,256]{2,1,0:T(8,128)S(1)} %get-tuple-element.298.c_ref, f32[2,256,256]{2,1,0:T(8,128)S(1)} %get-tuple-element.299.d_ref), custom_call_target="tpu_custom_call" | custom-call | tf_op jit(solution)/shard_map/while/body/chain/pallas_call | solution.py:421
  3703.2 8.9 collective-permute-done
  3712.8 504.6 %chain.3 = (f32[2,256,256]{2,1,0:T(8,128)S(1)}, f32[2,256,256]{2,1,0:T(8,128)S(1)}, f32[2,256,256]{2,1,0:T(8,128)S(1)}) custom-call(f32[2,256,256]{2,1,0:T(8,128)S(1)} %get-tuple-element.285.before_ref, f32[2,256,256]{2,1,0:T(8,128)S(1)} %get-tuple-element.298.c_ref, f32[2,256,256]{2,1,0:T(8,128)S(1)} %get-tuple-element.299.d_ref), custom_call_target="tpu_custom_call" | custom-call | tf_op jit(solution)/shard_map/while/body/chain/pallas_call | solution.py:421
  4221.6 8.9 collective-permute-done
  4231.3 504.6 %chain.3 = (f32[2,256,256]{2,1,0:T(8,128)S(1)}, f32[2,256,256]{2,1,0:T(8,128)S(1)}, f32[2,256,256]{2,1,0:T(8,128)S(1)}) custom-call(f32[2,256,256]{2,1,0:T(8,128)S(1)} %get-tuple-element.285.before_ref, f32[2,256,256]{2,1,0:T(8,128)S(1)} %get-tuple-element.298.c_ref, f32[2,256,256]{2,1,0:T(8,128)S(1)} %get-tuple-element.299.d_ref), custom_call_target="tpu_custom_call" | custom-call | tf_op jit(solution)/shard_map/while/body/chain/pallas_call | solution.py:421
  4740.1 8.9 collective-permute-done
  4749.7 504.6 %chain.3 = (f32[2,256,256]{2,1,0:T(8,128)S(1)}, f32[2,256,256]{2,1,0:T(8,128)S(1)}, f32[2,256,256]{2,1,0:T(8,128)S(1)}) custom-call(f32[2,256,256]{2,1,0:T(8,128)S(1)} %get-tuple-element.285.before_ref, f32[2,256,256]{2,1,0:T(8,128)S(1)} %get-tuple-element.298.c_ref, f32[2,256,256]{2,1,0:T(8,128)S(1)} %get-tuple-element.299.d_ref), custom_call_target="tpu_custom_call" | custom-call | tf_op jit(solution)/shard_map/while/body/chain/pallas_call | solution.py:421
  5258.6 8.9 collective-permute-done
  5268.2 504.6 %chain.3 = (f32[2,256,256]{2,1,0:T(8,128)S(1)}, f32[2,256,256]{2,1,0:T(8,128)S(1)}, f32[2,256,256]{2,1,0:T(8,128)S(1)}) custom-call(f32[2,256,256]{2,1,0:T(8,128)S(1)} %get-tuple-element.285.before_ref, f32[2,256,256]{2,1,0:T(8,128)S(1)} %get-tuple-element.298.c_ref, f32[2,256,256]{2,1,0:T(8,128)S(1)} %get-tuple-element.299.d_ref), custom_call_target="tpu_custom_call" | custom-call | tf_op jit(solution)/shard_map/while/body/chain/pallas_call | solution.py:421
  5777.0 8.9 collective-permute-done
  5786.7 504.6 %chain.3 = (f32[2,256,256]{2,1,0:T(8,128)S(1)}, f32[2,256,256]{2,1,0:T(8,128)S(1)}, f32[2,256,256]{2,1,0:T(8,128)S(1)}) custom-call(f32[2,256,256]{2,1,0:T(8,128)S(1)} %get-tuple-element.285.before_ref, f32[2,256,256]{2,1,0:T(8,128)S(1)} %get-tuple-element.298.c_ref, f32[2,256,256]{2,1,0:T(8,128)S(1)} %get-tuple-element.299.d_ref), custom_call_target="tpu_custom_call" | custom-call | tf_op jit(solution)/shard_map/while/body/chain/pallas_call | solution.py:421
  6295.5 8.9 collective-permute-done
  6305.1 504.6 %chain.3 = (f32[2,256,256]{2,1,0:T(8,128)S(1)}, f32[2,256,256]{2,1,0:T(8,128)S(1)}, f32[2,256,256]{2,1,0:T(8,128)S(1)}) custom-call(f32[2,256,256]{2,1,0:T(8,128)S(1)} %get-tuple-element.285.before_ref, f32[2,256,256]{2,1,0:T(8,128)S(1)} %get-tuple-element.298.c_ref, f32[2,256,256]{2,1,0:T(8,128)S(1)} %get-tuple-element.299.d_ref), custom_call_target="tpu_custom_call" | custom-call | tf_op jit(solution)/shard_map/while/body/chain/pallas_call | solution.py:421
  6814.0 8.9 collective-permute-done
  6823.6 504.6 %chain.3 = (f32[2,256,256]{2,1,0:T(8,128)S(1)}, f32[2,256,256]{2,1,0:T(8,128)S(1)}, f32[2,256,256]{2,1,0:T(8,128)S(1)}) custom-call(f32[2,256,256]{2,1,0:T(8,128)S(1)} %get-tuple-element.285.before_ref, f32[2,256,256]{2,1,0:T(8,128)S(1)} %get-tuple-element.298.c_ref, f32[2,256,256]{2,1,0:T(8,128)S(1)} %get-tuple-element.299.d_ref), custom_call_target="tpu_custom_call" | custom-call | tf_op jit(solution)/shard_map/while/body/chain/pallas_call | solution.py:421
  7332.4 8.9 collective-permute-done
  7342.1 504.6 %chain.3 = (f32[2,256,256]{2,1,0:T(8,128)S(1)}, f32[2,256,256]{2,1,0:T(8,128)S(1)}, f32[2,256,256]{2,1,0:T(8,128)S(1)}) custom-call(f32[2,256,256]{2,1,0:T(8,128)S(1)} %get-tuple-element.285.before_ref, f32[2,256,256]{2,1,0:T(8,128)S(1)} %get-tuple-element.298.c_ref, f32[2,256,256]{2,1,0:T(8,128)S(1)} %get-tuple-element.299.d_ref), custom_call_target="tpu_custom_call" | custom-call | tf_op jit(solution)/shard_map/while/body/chain/pallas_call | solution.py:421
  7850.9 8.9 collective-permute-done
  7860.5 504.6 %chain.3 = (f32[2,256,256]{2,1,0:T(8,128)S(1)}, f32[2,256,256]{2,1,0:T(8,128)S(1)}, f32[2,256,256]{2,1,0:T(8,128)S(1)}) custom-call(f32[2,256,256]{2,1,0:T(8,128)S(1)} %get-tuple-element.285.before_ref, f32[2,256,256]{2,1,0:T(8,128)S(1)} %get-tuple-element.298.c_ref, f32[2,256,256]{2,1,0:T(8,128)S(1)} %get-tuple-element.299.d_ref), custom_call_target="tpu_custom_call" | custom-call | tf_op jit(solution)/shard_map/while/body/chain/pallas_call | solution.py:421
  (82 shorter events, 147.2 us)
Async XLA Ops:
  0.6 11.7 copy-start.1
  1.8 8.1 collective-permute-start.1
  3.3 9.0 collective-permute-start.2
  13.3 8.2 collective-permute-start.3
  15.5 6.6 collective-permute-start.4
  23.7 28.6 collective-permute-start.5
  27.5 24.7 collective-permute-start.6
  29.9 22.4 collective-permute-start.7
  36.3 5.2 collective-permute-start.10
  37.2 4.3 collective-permute-start.11
  41.5 4.8 collective-permute-start.9
  46.3 13.2 copy-start.2
  46.3 6.9 collective-permute-start.12
  46.9 7.0 collective-permute-start.13
  52.2 3.6 collective-permute-start.14
  52.9 6.6 collective-permute-start.8
  588.1 13.2 collective-permute-start
  1106.6 13.2 collective-permute-start
  1625.1 13.2 collective-permute-start
  2143.5 13.2 collective-permute-start
  2662.0 13.2 collective-permute-start
  3180.5 13.2 collective-permute-start
  3698.9 13.2 collective-permute-start
  4217.4 13.2 collective-permute-start
  4735.9 13.2 collective-permute-start
  5254.3 13.2 collective-permute-start
  5772.8 13.2 collective-permute-start
  6291.3 13.2 collective-permute-start
  6809.7 13.2 collective-permute-start
  7328.2 13.2 collective-permute-start
  7846.7 13.2 collective-permute-start
  8365.1 13.2 collective-permute-start
  (1 other events, 0.6 us)

commit v2 on v1

--- a/solution.py
+++ b/solution.py
@@ -233,7 +233,19 @@
 
 
 def solve_kernel(
-    pos_ref, prev_ref, own, other, c_ref, d_ref, n_ref, r_ref, before_ref, stat_ref, *scratch
+    pos_ref,
+    prev_ref,
+    own,
+    other,
+    c_ref,
+    d_ref,
+    bound_ref,
+    n_ref,
+    r_ref,
+    before_ref,
+    trips_ref,
+    whole_ref,
+    *scratch,
 ):
     refs, m_ref, now = scratch[:4], scratch[4], scratch[5]
     mine = pos_ref[2]
@@ -286,7 +298,9 @@
         return worst
 
     worst = lax.fori_loop(0, 2, factors, jnp.zeros((1, 1), F32))
-    stat_ref[...] = jnp.broadcast_to(worst, (8, HALF))
+    fine = bound_of(bound_ref[...]) < LIMIT
+    trips_ref[0] = jnp.where(fine, jnp.where(worst[0, 0] > 0.0, 1, 0), 16)
+    whole_ref[0] = jnp.where(fine, 0, 1)
 
     def results(t, carry):
         left = [jnp.where(t == 0, c_ref[m], d_ref[m]) for m in range(2)]
@@ -340,69 +354,14 @@
     out_ref[...] = out
 
 
-def decide_kernel(bound_ref, stat_ref, out_ref):
-    v = bound_ref[...]
+def bound_of(v):
     lane = lax.broadcasted_iota(jnp.int32, (8, HALF), 1)
     bound = v
     for z in range(3):
         whole = jnp.sum(jnp.where(lane == 4 * z + 3, v, 0.0), axis=1, keepdims=True)
         bound = bound + jnp.where(lane >= 4 * z + 4, whole, 0.0)
     bound = jnp.where(lane < 16, bound, 0.0)
-    worst = jnp.max(jnp.max(bound, axis=0, keepdims=True), axis=1, keepdims=True)[0, 0]
-    failed = jnp.max(jnp.max(stat_ref[...], axis=0, keepdims=True), axis=1, keepdims=True)[0, 0]
-    fine = worst < LIMIT
-    out_ref[0] = jnp.where(fine, 0, 16)
-    out_ref[1] = jnp.where(fine & (failed > 0.0), 1, 0)
-
-
-def chain_kernel(before_ref, c_ref, d_ref, n_ref, r_ref, q_ref, a_ref):
-    r, c = square_iota()
-    lane = lax.broadcasted_iota(jnp.int32, (1, D), 1)
-
-    def orthonormal(m):
-        q_ref[m] = n_ref[m]
-
-        def column(k, _):
-            a = a_ref[...]
-            row = a_ref[pl.ds(k, 1), :]
-            pivot = jnp.sum(jnp.where(lane == k, row, 0.0), axis=1, keepdims=True)
-            rs = lax.rsqrt(pivot)
-            row = jnp.where(lane == k, 1.0, row) * rs
-            factor_col = jnp.sum(jnp.where(c == k, a, 0.0), axis=1, keepdims=True) * rs
-            below = jnp.where(c == k, 0.0, a) - factor_col * row
-            a_ref[...] = jnp.where(r > k, below, jnp.where(r == k, row, a))
-            return 0
-
-        def turn(t, carry):
-            gram = mm(q_ref[m], q_ref[m], 0, 0)
-            mean = total_of(jnp.where(r == c, gram, 0.0)) / D
-            shift = jnp.where(t == 0, 1.0e-5, 0.0) * mean
-            a_ref[...] = gram + jnp.where(r == c, shift, 0.0)
-            lax.fori_loop(0, D, column, 0)
-            q_ref[m] = mm(q_ref[m], jnp.where(c <= r, a_ref[...], 0.0), 1, 1)
-            return carry
-
-        def again(_, carry):
-            q_ref[m] = q_ref[m] - refinement(q_ref[m], 3)[0]
-            return carry
-
-        lax.fori_loop(0, 3, turn, 0)
-        lax.fori_loop(0, 2, again, 0)
-
-    def one(m, carry):
-        def half(t, carry):
-            n_ref[m] = jnp.where(t == 0, before_ref[m], mm(c_ref[m], q_ref[m]))
-            orthonormal(m)
-            return carry
-
-        q_ref[m] = before_ref[m]
-        lax.fori_loop(0, 2, half, 0)
-        q = q_ref[m]
-        r_ref[m] = jnp.where(c >= r, mm(q, n_ref[m], 0, 0), 0.0)
-        n_ref[m] = mm(mm(q, d_ref[m], 0, 0), q)
-        return carry
-
-    lax.fori_loop(0, 2, one, 0)
+    return jnp.max(jnp.max(bound, axis=0, keepdims=True), axis=1, keepdims=True)[0, 0]
 
 
 def struct(*shape):
@@ -422,7 +381,7 @@
             kernel,
             out_shape=outs,
             in_specs=specs,
-            out_specs=jax.tree.map(lambda _: VMEM, outs),
+            out_specs=jax.tree.map(lambda o: SMEM if o.dtype == jnp.int32 else VMEM, outs),
             scratch_shapes=[pltpu.VMEM(shape, F32) for shape in scratch],
             compiler_params=pltpu.CompilerParams(vmem_limit_bytes=48 * 2**20),
             name=name,
@@ -434,27 +393,50 @@
 SQUARE = struct(D, D)
 TWO = struct(2, D, D)
 TILE = struct(8, HALF)
+COUNT = jax.ShapeDtypeStruct((1,), jnp.int32)
 pair = call(pair_kernel, (SQUARE, SQUARE), [(4, D, D)], "pair")
 window = call(window_kernel, (TWO, SQUARE), [(11, D, D)], "window")
 entry = call(entry_kernel, SQUARE, [(4, D, D)], "entry")
 solve = call(
     solve_kernel,
-    (TWO, TWO, TWO, TILE),
+    (TWO, TWO, TWO, COUNT, COUNT),
     [(D, D)] * 4 + [(2, 2, D, D), (2, D, D)],
     "solve",
 )
 gauge = call(gauge_kernel, TILE, [(2, D, D), (2, D, D)], "gauge")
-chain = call(chain_kernel, (TWO, TWO, TWO), [(D, D)], "chain", table=False)
-
-
-def decide(bound, stat):
-    return pl.pallas_call(
-        decide_kernel,
-        out_shape=jax.ShapeDtypeStruct((2,), jnp.int32),
-        in_specs=[VMEM, VMEM],
-        out_specs=SMEM,
-        name="decide",
-    )(bound, stat)
+
+
+highest = lax.Precision.HIGHEST
+
+
+def product(left, right):
+    return jnp.matmul(left, right, precision=highest, preferred_element_type=F32)
+
+
+def flip(value):
+    return jnp.swapaxes(value, -1, -2)
+
+
+def orthonormal(panel):
+    def turn(t, y):
+        gram = product(flip(y), y)
+        mean = jnp.trace(gram, axis1=-2, axis2=-1)[:, None, None] / D
+        gram = gram + jnp.where(t == 0, 1.0e-5, 0.0) * mean * jnp.eye(D, dtype=F32)
+        lower = jnp.linalg.cholesky(gram)
+        return flip(lax.linalg.triangular_solve(lower, flip(y), left_side=True, lower=True))
+
+    return lax.fori_loop(0, 3, turn, panel)
+
+
+def one_block(before, coupling, diagonal):
+    def half(t, carried):
+        panel, q = carried
+        panel = jnp.where(t == 0, panel, product(coupling, q))
+        return panel, orthonormal(panel)
+
+    panel, q = lax.fori_loop(0, 2, half, (before, before))
+    new = product(product(flip(q), diagonal), q)
+    return new, jnp.triu(product(flip(q), panel)), q
 
 
 def x_move(value, to):
@@ -497,27 +479,32 @@
     q0, q1 = x_mirror(w), x_pairs(v)
     prev, total = window(table, coupling, r0, r1, w, q0, q1)
     below = [z_move(total, s) for s in (1, 2, 3)]
-    bound = largest_in_row(gauge(pos, prev, coupling))
+    gauged = gauge(pos, prev, coupling)
     own = entry(pos, *below)
-    new, tri, before, stat = solve(pos, prev, own, x_pairs(own), coupling, diagonal)
-    rounds = decide(bound, stat)
-
-    def local(_, carried):
-        new, tri, q = chain(carried[0], coupling, diagonal)
-        return q, new, tri
-
-    _, new, tri = lax.fori_loop(0, rounds[1], local, (before, new, tri))
+    gauged, own = lax.optimization_barrier((gauged, own))
+    other = x_pairs(own)
+    bound = largest_in_row(gauged)
+    new, tri, before, trips, whole = solve(
+        pos, prev, own, other, coupling, diagonal, bound
+    )
+    whole = whole.reshape(()) > 0
 
     def step(i, carried):
         q, new, tri = carried
-        new_now, tri_now, q = chain(q, coupling, diagonal)
-        keep = i == position
+        q = jnp.where(whole & (i == 0), jnp.eye(D, dtype=F32), q)
+        new_now, tri_now, q = one_block(q, coupling, diagonal)
+        keep = (i == position) | jnp.logical_not(whole)
         new = jnp.where(keep, new_now, new)
         tri = jnp.where(keep, tri_now, tri)
-        return lax.ppermute(q, "row", [(j, j + 1) for j in range(15)]), new, tri
-
-    eyes = jnp.broadcast_to(jnp.eye(D, dtype=F32), (2, D, D))
-    _, new, tri = lax.fori_loop(0, rounds[0], step, (eyes, new, tri))
+        q = lax.cond(
+            whole,
+            lambda q: lax.ppermute(q, "row", [(j, j + 1) for j in range(15)]),
+            lambda q: q,
+            q,
+        )
+        return q, new, tri
+
+    _, new, tri = lax.fori_loop(0, trips.reshape(()), step, (before, new, tri))
     shape = diag_blocks.shape
     return new.reshape(shape), tri.reshape(shape)
 

time: 8380 us -> 11400 us (1.36)
  other arithmetic: 36.5 us -> 10300 us
  Pallas kernels: 8100 us -> 28.6 us
  local copies, waits for them, and re-layouts: 3.77 us -> 450 us
  matrix products: 0 us -> 331 us
    another operation x0 -> x1344, other arithmetic: none -> 10200 us  [the longest x960 6420 us: turn(): lower = jnp.linalg.cholesky(gram)]
    pallas_call x21 -> x5, Pallas kernels: 8100 us -> 28.6 us  [run(): pl.pallas_call(kernel, out_shape=outs, in_specs=specs, out_specs=jax.tree...]
    another operation x0 -> x864, local copies, waits for them, and re-layouts: none -> 388 us
    another operation x0 -> x480, matrix products: none -> 179 us  [the longest x288 117 us: turn(): lax.linalg.triangular_solve(lower, flip(y), left_side=True, lower=True)]
    dot_general x0 -> x176, matrix products: none -> 152 us  [product(): jnp.matmul(left, right, precision=highest, preferred_element_type=F32)]
where the time goes in v2:
time: 11400 us
  other arithmetic  10300 us (90%)
  local copies, waits for them, and re-layouts  450 us (4%)
  matrix products  331 us (3%)
  waiting for transfers between devices  202 us (2%)
    another operation x960, other arithmetic, turn(): lower = jnp.linalg.cholesky(gram)  6420 us
    another operation x384, other arithmetic, turn(): lax.linalg.triangular_solve(lower, flip(y), left_side=True, lower=True)  3790 us
    another operation x576, local copies, waits for them, and re-layouts  377 us

profile of v2, /device:TPU:48, one launch (start us, length us, event | category | flops | bytes accessed | tf_op | source)
XLA Modules:
  0.0 11372.1 jit_solution(15216831058508502515)
XLA Ops:
  76.3 11295.6 %while.68 = (s32[]{:T(128)}, f32[2,256,256]{2,1,0:T(8,128)}, f32[2,256,256]{2,1,0:T(8,128)}, f32[2,256,256]{2,1,0:T(8,128)}, s32[]{:T(128)}, /*index=5*/pred[]{:...) while((s32[]{:T(128)}, f32[2,256,256]{2,1,0:T(8,128)}, ...), condition=%wide.region_12.13_spmd, body=%wide.region_0.12_spmd.sunk | while | flops 2419032832 | bytes 38607924 | solution.py:507
  77.3 684.9 %while.69 = (s32[]{:T(128)}, f32[2,256,256]{2,1,0:T(8,128)S(1)}, f32[2,256,256]{1,2,0:T(8,128)S(1)}, f32[2,256,256]{2,1,0:T(8,128)S(1)}, s32[]{:T(128)}, /*index...) while((s32[]{:T(128)}, f32[2,256,256]{2,1,0:T(8,128)S(1)}, ...), condition=%wide.region_9.9_spmd, body=%wide.region_1.8_spmd.sunk | while | flops 1210352128 | bytes 15405615 | solution.py:437
  420.7 341.4 %while.70 = (s32[]{:T(128)}, f32[2,256,256]{1,2,0:T(8,128)S(1)}, s32[]{:T(128)}, s32[]{:T(128)}, f32[]{:T(128)}, /*index=5*/f32[]{:T(128)}, f32[]{:T(128)}, s32[]{:T(128)}) while((s32[]{:T(128)}, f32[2,256,256]{1,2,0:T(8,128)S(1)}, s32[]{:T(128)}, s32[]{:T(128)}, f32[]{:T(128)}, /*index=5*/f32[]{:T(128)}, f32[]{:T(128)}, s32[]{:T(128)}) %tuple.130), condition=%wide.region_8.7_spmd, body=%wide.region_2.6_spmd.sunk | while | flops 807567872 | bytes 12259688 | solution.py:428
  784.3 684.9 %while.69 = (s32[]{:T(128)}, f32[2,256,256]{2,1,0:T(8,128)S(1)}, f32[2,256,256]{1,2,0:T(8,128)S(1)}, f32[2,256,256]{2,1,0:T(8,128)S(1)}, s32[]{:T(128)}, /*index...) while((s32[]{:T(128)}, f32[2,256,256]{2,1,0:T(8,128)S(1)}, ...), condition=%wide.region_9.9_spmd, body=%wide.region_1.8_spmd.sunk | while | flops 1210352128 | bytes 15405615 | solution.py:437
  1127.7 341.4 %while.70 = (s32[]{:T(128)}, f32[2,256,256]{1,2,0:T(8,128)S(1)}, s32[]{:T(128)}, s32[]{:T(128)}, f32[]{:T(128)}, /*index=5*/f32[]{:T(128)}, f32[]{:T(128)}, s32[]{:T(128)}) while((s32[]{:T(128)}, f32[2,256,256]{1,2,0:T(8,128)S(1)}, s32[]{:T(128)}, s32[]{:T(128)}, f32[]{:T(128)}, /*index=5*/f32[]{:T(128)}, f32[]{:T(128)}, s32[]{:T(128)}) %tuple.130), condition=%wide.region_8.7_spmd, body=%wide.region_2.6_spmd.sunk | while | flops 807567872 | bytes 12259688 | solution.py:428
  1490.4 684.9 %while.69 = (s32[]{:T(128)}, f32[2,256,256]{2,1,0:T(8,128)S(1)}, f32[2,256,256]{1,2,0:T(8,128)S(1)}, f32[2,256,256]{2,1,0:T(8,128)S(1)}, s32[]{:T(128)}, /*index...) while((s32[]{:T(128)}, f32[2,256,256]{2,1,0:T(8,128)S(1)}, ...), condition=%wide.region_9.9_spmd, body=%wide.region_1.8_spmd.sunk | while | flops 1210352128 | bytes 15405615 | solution.py:437
  1491.4 341.4 %while.70 = (s32[]{:T(128)}, f32[2,256,256]{1,2,0:T(8,128)S(1)}, s32[]{:T(128)}, s32[]{:T(128)}, f32[]{:T(128)}, /*index=5*/f32[]{:T(128)}, f32[]{:T(128)}, s32[]{:T(128)}) while((s32[]{:T(128)}, f32[2,256,256]{1,2,0:T(8,128)S(1)}, s32[]{:T(128)}, s32[]{:T(128)}, f32[]{:T(128)}, /*index=5*/f32[]{:T(128)}, f32[]{:T(128)}, s32[]{:T(128)}) %tuple.130), condition=%wide.region_8.7_spmd, body=%wide.region_2.6_spmd.sunk | while | flops 807567872 | bytes 12259688 | solution.py:428
  2196.3 684.9 %while.69 = (s32[]{:T(128)}, f32[2,256,256]{2,1,0:T(8,128)S(1)}, f32[2,256,256]{1,2,0:T(8,128)S(1)}, f32[2,256,256]{2,1,0:T(8,128)S(1)}, s32[]{:T(128)}, /*index...) while((s32[]{:T(128)}, f32[2,256,256]{2,1,0:T(8,128)S(1)}, ...), condition=%wide.region_9.9_spmd, body=%wide.region_1.8_spmd.sunk | while | flops 1210352128 | bytes 15405615 | solution.py:437
  2197.3 341.4 %while.70 = (s32[]{:T(128)}, f32[2,256,256]{1,2,0:T(8,128)S(1)}, s32[]{:T(128)}, s32[]{:T(128)}, f32[]{:T(128)}, /*index=5*/f32[]{:T(128)}, f32[]{:T(128)}, s32[]{:T(128)}) while((s32[]{:T(128)}, f32[2,256,256]{1,2,0:T(8,128)S(1)}, s32[]{:T(128)}, s32[]{:T(128)}, f32[]{:T(128)}, /*index=5*/f32[]{:T(128)}, f32[]{:T(128)}, s32[]{:T(128)}) %tuple.130), condition=%wide.region_8.7_spmd, body=%wide.region_2.6_spmd.sunk | while | flops 807567872 | bytes 12259688 | solution.py:428
  2539.7 341.4 %while.70 = (s32[]{:T(128)}, f32[2,256,256]{1,2,0:T(8,128)S(1)}, s32[]{:T(128)}, s32[]{:T(128)}, f32[]{:T(128)}, /*index=5*/f32[]{:T(128)}, f32[]{:T(128)}, s32[]{:T(128)}) while((s32[]{:T(128)}, f32[2,256,256]{1,2,0:T(8,128)S(1)}, s32[]{:T(128)}, s32[]{:T(128)}, f32[]{:T(128)}, /*index=5*/f32[]{:T(128)}, f32[]{:T(128)}, s32[]{:T(128)}) %tuple.130), condition=%wide.region_8.7_spmd, body=%wide.region_2.6_spmd.sunk | while | flops 807567872 | bytes 12259688 | solution.py:428
  2902.2 684.9 %while.69 = (s32[]{:T(128)}, f32[2,256,256]{2,1,0:T(8,128)S(1)}, f32[2,256,256]{1,2,0:T(8,128)S(1)}, f32[2,256,256]{2,1,0:T(8,128)S(1)}, s32[]{:T(128)}, /*index...) while((s32[]{:T(128)}, f32[2,256,256]{2,1,0:T(8,128)S(1)}, ...), condition=%wide.region_9.9_spmd, body=%wide.region_1.8_spmd.sunk | while | flops 1210352128 | bytes 15405615 | solution.py:437
  3245.6 341.4 %while.70 = (s32[]{:T(128)}, f32[2,256,256]{1,2,0:T(8,128)S(1)}, s32[]{:T(128)}, s32[]{:T(128)}, f32[]{:T(128)}, /*index=5*/f32[]{:T(128)}, f32[]{:T(128)}, s32[]{:T(128)}) while((s32[]{:T(128)}, f32[2,256,256]{1,2,0:T(8,128)S(1)}, s32[]{:T(128)}, s32[]{:T(128)}, f32[]{:T(128)}, /*index=5*/f32[]{:T(128)}, f32[]{:T(128)}, s32[]{:T(128)}) %tuple.130), condition=%wide.region_8.7_spmd, body=%wide.region_2.6_spmd.sunk | while | flops 807567872 | bytes 12259688 | solution.py:428
  3608.1 684.9 %while.69 = (s32[]{:T(128)}, f32[2,256,256]{2,1,0:T(8,128)S(1)}, f32[2,256,256]{1,2,0:T(8,128)S(1)}, f32[2,256,256]{2,1,0:T(8,128)S(1)}, s32[]{:T(128)}, /*index...) while((s32[]{:T(128)}, f32[2,256,256]{2,1,0:T(8,128)S(1)}, ...), condition=%wide.region_9.9_spmd, body=%wide.region_1.8_spmd.sunk | while | flops 1210352128 | bytes 15405615 | solution.py:437
  4314.0 684.9 %while.69 = (s32[]{:T(128)}, f32[2,256,256]{2,1,0:T(8,128)S(1)}, f32[2,256,256]{1,2,0:T(8,128)S(1)}, f32[2,256,256]{2,1,0:T(8,128)S(1)}, s32[]{:T(128)}, /*index...) while((s32[]{:T(128)}, f32[2,256,256]{2,1,0:T(8,128)S(1)}, ...), condition=%wide.region_9.9_spmd, body=%wide.region_1.8_spmd.sunk | while | flops 1210352128 | bytes 15405615 | solution.py:437
  4315.1 341.4 %while.70 = (s32[]{:T(128)}, f32[2,256,256]{1,2,0:T(8,128)S(1)}, s32[]{:T(128)}, s32[]{:T(128)}, f32[]{:T(128)}, /*index=5*/f32[]{:T(128)}, f32[]{:T(128)}, s32[]{:T(128)}) while((s32[]{:T(128)}, f32[2,256,256]{1,2,0:T(8,128)S(1)}, s32[]{:T(128)}, s32[]{:T(128)}, f32[]{:T(128)}, /*index=5*/f32[]{:T(128)}, f32[]{:T(128)}, s32[]{:T(128)}) %tuple.130), condition=%wide.region_8.7_spmd, body=%wide.region_2.6_spmd.sunk | while | flops 807567872 | bytes 12259688 | solution.py:428
  4657.5 341.4 %while.70 = (s32[]{:T(128)}, f32[2,256,256]{1,2,0:T(8,128)S(1)}, s32[]{:T(128)}, s32[]{:T(128)}, f32[]{:T(128)}, /*index=5*/f32[]{:T(128)}, f32[]{:T(128)}, s32[]{:T(128)}) while((s32[]{:T(128)}, f32[2,256,256]{1,2,0:T(8,128)S(1)}, s32[]{:T(128)}, s32[]{:T(128)}, f32[]{:T(128)}, /*index=5*/f32[]{:T(128)}, f32[]{:T(128)}, s32[]{:T(128)}) %tuple.130), condition=%wide.region_8.7_spmd, body=%wide.region_2.6_spmd.sunk | while | flops 807567872 | bytes 12259688 | solution.py:428
  5020.0 684.9 %while.69 = (s32[]{:T(128)}, f32[2,256,256]{2,1,0:T(8,128)S(1)}, f32[2,256,256]{1,2,0:T(8,128)S(1)}, f32[2,256,256]{2,1,0:T(8,128)S(1)}, s32[]{:T(128)}, /*index...) while((s32[]{:T(128)}, f32[2,256,256]{2,1,0:T(8,128)S(1)}, ...), condition=%wide.region_9.9_spmd, body=%wide.region_1.8_spmd.sunk | while | flops 1210352128 | bytes 15405615 | solution.py:437
  5363.4 341.4 %while.70 = (s32[]{:T(128)}, f32[2,256,256]{1,2,0:T(8,128)S(1)}, s32[]{:T(128)}, s32[]{:T(128)}, f32[]{:T(128)}, /*index=5*/f32[]{:T(128)}, f32[]{:T(128)}, s32[]{:T(128)}) while((s32[]{:T(128)}, f32[2,256,256]{1,2,0:T(8,128)S(1)}, s32[]{:T(128)}, s32[]{:T(128)}, f32[]{:T(128)}, /*index=5*/f32[]{:T(128)}, f32[]{:T(128)}, s32[]{:T(128)}) %tuple.130), condition=%wide.region_8.7_spmd, body=%wide.region_2.6_spmd.sunk | while | flops 807567872 | bytes 12259688 | solution.py:428
  5725.9 684.9 %while.69 = (s32[]{:T(128)}, f32[2,256,256]{2,1,0:T(8,128)S(1)}, f32[2,256,256]{1,2,0:T(8,128)S(1)}, f32[2,256,256]{2,1,0:T(8,128)S(1)}, s32[]{:T(128)}, /*index...) while((s32[]{:T(128)}, f32[2,256,256]{2,1,0:T(8,128)S(1)}, ...), condition=%wide.region_9.9_spmd, body=%wide.region_1.8_spmd.sunk | while | flops 1210352128 | bytes 15405615 | solution.py:437
  6431.8 684.9 %while.69 = (s32[]{:T(128)}, f32[2,256,256]{2,1,0:T(8,128)S(1)}, f32[2,256,256]{1,2,0:T(8,128)S(1)}, f32[2,256,256]{2,1,0:T(8,128)S(1)}, s32[]{:T(128)}, /*index...) while((s32[]{:T(128)}, f32[2,256,256]{2,1,0:T(8,128)S(1)}, ...), condition=%wide.region_9.9_spmd, body=%wide.region_1.8_spmd.sunk | while | flops 1210352128 | bytes 15405615 | solution.py:437
  6432.8 341.4 %while.70 = (s32[]{:T(128)}, f32[2,256,256]{1,2,0:T(8,128)S(1)}, s32[]{:T(128)}, s32[]{:T(128)}, f32[]{:T(128)}, /*index=5*/f32[]{:T(128)}, f32[]{:T(128)}, s32[]{:T(128)}) while((s32[]{:T(128)}, f32[2,256,256]{1,2,0:T(8,128)S(1)}, s32[]{:T(128)}, s32[]{:T(128)}, f32[]{:T(128)}, /*index=5*/f32[]{:T(128)}, f32[]{:T(128)}, s32[]{:T(128)}) %tuple.130), condition=%wide.region_8.7_spmd, body=%wide.region_2.6_spmd.sunk | while | flops 807567872 | bytes 12259688 | solution.py:428
  6775.3 341.4 %while.70 = (s32[]{:T(128)}, f32[2,256,256]{1,2,0:T(8,128)S(1)}, s32[]{:T(128)}, s32[]{:T(128)}, f32[]{:T(128)}, /*index=5*/f32[]{:T(128)}, f32[]{:T(128)}, s32[]{:T(128)}) while((s32[]{:T(128)}, f32[2,256,256]{1,2,0:T(8,128)S(1)}, s32[]{:T(128)}, s32[]{:T(128)}, f32[]{:T(128)}, /*index=5*/f32[]{:T(128)}, f32[]{:T(128)}, s32[]{:T(128)}) %tuple.130), condition=%wide.region_8.7_spmd, body=%wide.region_2.6_spmd.sunk | while | flops 807567872 | bytes 12259688 | solution.py:428
  7137.7 684.9 %while.69 = (s32[]{:T(128)}, f32[2,256,256]{2,1,0:T(8,128)S(1)}, f32[2,256,256]{1,2,0:T(8,128)S(1)}, f32[2,256,256]{2,1,0:T(8,128)S(1)}, s32[]{:T(128)}, /*index...) while((s32[]{:T(128)}, f32[2,256,256]{2,1,0:T(8,128)S(1)}, ...), condition=%wide.region_9.9_spmd, body=%wide.region_1.8_spmd.sunk | while | flops 1210352128 | bytes 15405615 | solution.py:437
  7481.2 341.4 %while.70 = (s32[]{:T(128)}, f32[2,256,256]{1,2,0:T(8,128)S(1)}, s32[]{:T(128)}, s32[]{:T(128)}, f32[]{:T(128)}, /*index=5*/f32[]{:T(128)}, f32[]{:T(128)}, s32[]{:T(128)}) while((s32[]{:T(128)}, f32[2,256,256]{1,2,0:T(8,128)S(1)}, s32[]{:T(128)}, s32[]{:T(128)}, f32[]{:T(128)}, /*index=5*/f32[]{:T(128)}, f32[]{:T(128)}, s32[]{:T(128)}) %tuple.130), condition=%wide.region_8.7_spmd, body=%wide.region_2.6_spmd.sunk | while | flops 807567872 | bytes 12259688 | solution.py:428
  7843.7 684.9 %while.69 = (s32[]{:T(128)}, f32[2,256,256]{2,1,0:T(8,128)S(1)}, f32[2,256,256]{1,2,0:T(8,128)S(1)}, f32[2,256,256]{2,1,0:T(8,128)S(1)}, s32[]{:T(128)}, /*index...) while((s32[]{:T(128)}, f32[2,256,256]{2,1,0:T(8,128)S(1)}, ...), condition=%wide.region_9.9_spmd, body=%wide.region_1.8_spmd.sunk | while | flops 1210352128 | bytes 15405615 | solution.py:437
  8549.6 684.9 %while.69 = (s32[]{:T(128)}, f32[2,256,256]{2,1,0:T(8,128)S(1)}, f32[2,256,256]{1,2,0:T(8,128)S(1)}, f32[2,256,256]{2,1,0:T(8,128)S(1)}, s32[]{:T(128)}, /*index...) while((s32[]{:T(128)}, f32[2,256,256]{2,1,0:T(8,128)S(1)}, ...), condition=%wide.region_9.9_spmd, body=%wide.region_1.8_spmd.sunk | while | flops 1210352128 | bytes 15405615 | solution.py:437
  8893.0 341.4 %while.70 = (s32[]{:T(128)}, f32[2,256,256]{1,2,0:T(8,128)S(1)}, s32[]{:T(128)}, s32[]{:T(128)}, f32[]{:T(128)}, /*index=5*/f32[]{:T(128)}, f32[]{:T(128)}, s32[]{:T(128)}) while((s32[]{:T(128)}, f32[2,256,256]{1,2,0:T(8,128)S(1)}, s32[]{:T(128)}, s32[]{:T(128)}, f32[]{:T(128)}, /*index=5*/f32[]{:T(128)}, f32[]{:T(128)}, s32[]{:T(128)}) %tuple.130), condition=%wide.region_8.7_spmd, body=%wide.region_2.6_spmd.sunk | while | flops 807567872 | bytes 12259688 | solution.py:428
  9255.5 684.9 %while.69 = (s32[]{:T(128)}, f32[2,256,256]{2,1,0:T(8,128)S(1)}, f32[2,256,256]{1,2,0:T(8,128)S(1)}, f32[2,256,256]{2,1,0:T(8,128)S(1)}, s32[]{:T(128)}, /*index...) while((s32[]{:T(128)}, f32[2,256,256]{2,1,0:T(8,128)S(1)}, ...), condition=%wide.region_9.9_spmd, body=%wide.region_1.8_spmd.sunk | while | flops 1210352128 | bytes 15405615 | solution.py:437
  9598.9 341.4 %while.70 = (s32[]{:T(128)}, f32[2,256,256]{1,2,0:T(8,128)S(1)}, s32[]{:T(128)}, s32[]{:T(128)}, f32[]{:T(128)}, /*index=5*/f32[]{:T(128)}, f32[]{:T(128)}, s32[]{:T(128)}) while((s32[]{:T(128)}, f32[2,256,256]{1,2,0:T(8,128)S(1)}, s32[]{:T(128)}, s32[]{:T(128)}, f32[]{:T(128)}, /*index=5*/f32[]{:T(128)}, f32[]{:T(128)}, s32[]{:T(128)}) %tuple.130), condition=%wide.region_8.7_spmd, body=%wide.region_2.6_spmd.sunk | while | flops 807567872 | bytes 12259688 | solution.py:428
  9961.4 684.9 %while.69 = (s32[]{:T(128)}, f32[2,256,256]{2,1,0:T(8,128)S(1)}, f32[2,256,256]{1,2,0:T(8,128)S(1)}, f32[2,256,256]{2,1,0:T(8,128)S(1)}, s32[]{:T(128)}, /*index...) while((s32[]{:T(128)}, f32[2,256,256]{2,1,0:T(8,128)S(1)}, ...), condition=%wide.region_9.9_spmd, body=%wide.region_1.8_spmd.sunk | while | flops 1210352128 | bytes 15405615 | solution.py:437
  10667.4 684.9 %while.69 = (s32[]{:T(128)}, f32[2,256,256]{2,1,0:T(8,128)S(1)}, f32[2,256,256]{1,2,0:T(8,128)S(1)}, f32[2,256,256]{2,1,0:T(8,128)S(1)}, s32[]{:T(128)}, /*index...) while((s32[]{:T(128)}, f32[2,256,256]{2,1,0:T(8,128)S(1)}, ...), condition=%wide.region_9.9_spmd, body=%wide.region_1.8_spmd.sunk | while | flops 1210352128 | bytes 15405615 | solution.py:437
  11010.8 341.4 %while.70 = (s32[]{:T(128)}, f32[2,256,256]{1,2,0:T(8,128)S(1)}, s32[]{:T(128)}, s32[]{:T(128)}, f32[]{:T(128)}, /*index=5*/f32[]{:T(128)}, f32[]{:T(128)}, s32[]{:T(128)}) while((s32[]{:T(128)}, f32[2,256,256]{1,2,0:T(8,128)S(1)}, s32[]{:T(128)}, s32[]{:T(128)}, f32[]{:T(128)}, /*index=5*/f32[]{:T(128)}, f32[]{:T(128)}, s32[]{:T(128)}) %tuple.130), condition=%wide.region_8.7_spmd, body=%wide.region_2.6_spmd.sunk | while | flops 807567872 | bytes 12259688 | solution.py:428
  (4043 shorter events, 17749.3 us)
Async XLA Ops:
  1.8 8.1 collective-permute-start.1
  3.3 9.0 collective-permute-start.2
  13.3 8.2 collective-permute-start.3
  15.5 6.6 collective-permute-start.4
  23.7 13.4 collective-permute-start.5
  27.5 9.5 collective-permute-start.6
  29.9 7.2 collective-permute-start.7
  36.3 19.6 copy-start.1
  37.7 5.2 collective-permute-start.10
  38.6 4.3 collective-permute-start.11
  40.3 4.8 collective-permute-start.9
  40.6 15.2 collective-permute-start.8
  45.1 9.4 collective-permute-start.12
  48.0 6.6 collective-permute-start.13
  52.0 3.9 collective-permute-start.14
  766.9 15.4 copy-start.2
  766.9 14.5 collective-permute-start
  1473.8 13.7 collective-permute-start
  2179.9 13.5 collective-permute-start
  2885.8 13.5 collective-permute-start
  3591.8 13.5 collective-permute-start
  4297.7 13.5 collective-permute-start
  5003.6 13.5 collective-permute-start
  5709.5 13.5 collective-permute-start
  6415.5 13.5 collective-permute-start
  7121.4 13.5 collective-permute-start
  7827.3 13.5 collective-permute-start
  8533.2 13.5 collective-permute-start
  9239.1 13.5 collective-permute-start
  9945.1 13.5 collective-permute-start
  10651.0 13.5 collective-permute-start
  11356.9 13.5 collective-permute-start
  (80 other events, 305.3 us)

commit v3 on v2

--- a/solution.py
+++ b/solution.py
@@ -459,10 +459,8 @@
     return x_move(value, lambda x: 3 - x)
 
 
-def largest_in_row(value):
-    moved = [x_move(value, lambda x, s=s: (x + s) % 4) for s in (1, 2, 3)]
-    value = functools.reduce(jnp.maximum, moved, value)
-    return functools.reduce(jnp.maximum, [z_ring(value, s) for s in (1, 2, 3)], value)
+def largest(value, moves):
+    return functools.reduce(jnp.maximum, moves, value)
 
 
 def shards(diag_blocks, coupling_blocks):
@@ -480,10 +478,12 @@
     prev, total = window(table, coupling, r0, r1, w, q0, q1)
     below = [z_move(total, s) for s in (1, 2, 3)]
     gauged = gauge(pos, prev, coupling)
+    gauged = largest(gauged, [x_move(gauged, lambda x, s=s: (x + s) % 4) for s in (1, 2, 3)])
+    gauged, *below = lax.optimization_barrier((gauged, *below))
     own = entry(pos, *below)
     gauged, own = lax.optimization_barrier((gauged, own))
     other = x_pairs(own)
-    bound = largest_in_row(gauged)
+    bound = largest(gauged, [z_ring(gauged, s) for s in (1, 2, 3)])
     new, tri, before, trips, whole = solve(
         pos, prev, own, other, coupling, diagonal, bound
     )

time: 11400 us -> 11400 us (level)
  no operation moved by 1% of the time
where the time goes in v3:
time: 11400 us
  other arithmetic  10300 us (90%)
  local copies, waits for them, and re-layouts  450 us (4%)
  matrix products  331 us (3%)
  waiting for transfers between devices  202 us (2%)
    another operation x960, other arithmetic, turn(): lower = jnp.linalg.cholesky(gram)  6420 us
    another operation x384, other arithmetic, turn(): lax.linalg.triangular_solve(lower, flip(y), left_side=True, lower=True)  3790 us
    another operation x576, local copies, waits for them, and re-layouts  377 us

profile of v3, /device:TPU:48, one launch (start us, length us, event | category | flops | bytes accessed | tf_op | source)
XLA Modules:
  0.0 11370.2 jit_solution(3587264082568002514)
XLA Ops:
  75.6 11294.4 %while.68 = (s32[]{:T(128)}, f32[2,256,256]{2,1,0:T(8,128)}, f32[2,256,256]{2,1,0:T(8,128)}, f32[2,256,256]{2,1,0:T(8,128)}, s32[]{:T(128)}, /*index=5*/pred[]{:...) while((s32[]{:T(128)}, f32[2,256,256]{2,1,0:T(8,128)}, ...), condition=%wide.region_12.13_spmd, body=%wide.region_0.12_spmd.sunk | while | flops 2419032832 | bytes 38607924 | solution.py:507
  76.6 684.9 %while.69 = (s32[]{:T(128)}, f32[2,256,256]{2,1,0:T(8,128)S(1)}, f32[2,256,256]{1,2,0:T(8,128)S(1)}, f32[2,256,256]{2,1,0:T(8,128)S(1)}, s32[]{:T(128)}, /*index...) while((s32[]{:T(128)}, f32[2,256,256]{2,1,0:T(8,128)S(1)}, ...), condition=%wide.region_9.9_spmd, body=%wide.region_1.8_spmd.sunk | while | flops 1210352128 | bytes 15405615 | solution.py:437
  420.1 341.4 %while.70 = (s32[]{:T(128)}, f32[2,256,256]{1,2,0:T(8,128)S(1)}, s32[]{:T(128)}, s32[]{:T(128)}, f32[]{:T(128)}, /*index=5*/f32[]{:T(128)}, f32[]{:T(128)}, s32[]{:T(128)}) while((s32[]{:T(128)}, f32[2,256,256]{1,2,0:T(8,128)S(1)}, s32[]{:T(128)}, s32[]{:T(128)}, f32[]{:T(128)}, /*index=5*/f32[]{:T(128)}, f32[]{:T(128)}, s32[]{:T(128)}) %tuple.132), condition=%wide.region_8.7_spmd, body=%wide.region_2.6_spmd.sunk | while | flops 807567872 | bytes 12259688 | solution.py:428
  782.5 684.9 %while.69 = (s32[]{:T(128)}, f32[2,256,256]{2,1,0:T(8,128)S(1)}, f32[2,256,256]{1,2,0:T(8,128)S(1)}, f32[2,256,256]{2,1,0:T(8,128)S(1)}, s32[]{:T(128)}, /*index...) while((s32[]{:T(128)}, f32[2,256,256]{2,1,0:T(8,128)S(1)}, ...), condition=%wide.region_9.9_spmd, body=%wide.region_1.8_spmd.sunk | while | flops 1210352128 | bytes 15405615 | solution.py:437
  1488.5 684.9 %while.69 = (s32[]{:T(128)}, f32[2,256,256]{2,1,0:T(8,128)S(1)}, f32[2,256,256]{1,2,0:T(8,128)S(1)}, f32[2,256,256]{2,1,0:T(8,128)S(1)}, s32[]{:T(128)}, /*index...) while((s32[]{:T(128)}, f32[2,256,256]{2,1,0:T(8,128)S(1)}, ...), condition=%wide.region_9.9_spmd, body=%wide.region_1.8_spmd.sunk | while | flops 1210352128 | bytes 15405615 | solution.py:437
  1489.5 341.4 %while.70 = (s32[]{:T(128)}, f32[2,256,256]{1,2,0:T(8,128)S(1)}, s32[]{:T(128)}, s32[]{:T(128)}, f32[]{:T(128)}, /*index=5*/f32[]{:T(128)}, f32[]{:T(128)}, s32[]{:T(128)}) while((s32[]{:T(128)}, f32[2,256,256]{1,2,0:T(8,128)S(1)}, s32[]{:T(128)}, s32[]{:T(128)}, f32[]{:T(128)}, /*index=5*/f32[]{:T(128)}, f32[]{:T(128)}, s32[]{:T(128)}) %tuple.132), condition=%wide.region_8.7_spmd, body=%wide.region_2.6_spmd.sunk | while | flops 807567872 | bytes 12259688 | solution.py:428
  1831.9 341.4 %while.70 = (s32[]{:T(128)}, f32[2,256,256]{1,2,0:T(8,128)S(1)}, s32[]{:T(128)}, s32[]{:T(128)}, f32[]{:T(128)}, /*index=5*/f32[]{:T(128)}, f32[]{:T(128)}, s32[]{:T(128)}) while((s32[]{:T(128)}, f32[2,256,256]{1,2,0:T(8,128)S(1)}, s32[]{:T(128)}, s32[]{:T(128)}, f32[]{:T(128)}, /*index=5*/f32[]{:T(128)}, f32[]{:T(128)}, s32[]{:T(128)}) %tuple.132), condition=%wide.region_8.7_spmd, body=%wide.region_2.6_spmd.sunk | while | flops 807567872 | bytes 12259688 | solution.py:428
  2194.4 684.9 %while.69 = (s32[]{:T(128)}, f32[2,256,256]{2,1,0:T(8,128)S(1)}, f32[2,256,256]{1,2,0:T(8,128)S(1)}, f32[2,256,256]{2,1,0:T(8,128)S(1)}, s32[]{:T(128)}, /*index...) while((s32[]{:T(128)}, f32[2,256,256]{2,1,0:T(8,128)S(1)}, ...), condition=%wide.region_9.9_spmd, body=%wide.region_1.8_spmd.sunk | while | flops 1210352128 | bytes 15405615 | solution.py:437
  2537.8 341.4 %while.70 = (s32[]{:T(128)}, f32[2,256,256]{1,2,0:T(8,128)S(1)}, s32[]{:T(128)}, s32[]{:T(128)}, f32[]{:T(128)}, /*index=5*/f32[]{:T(128)}, f32[]{:T(128)}, s32[]{:T(128)}) while((s32[]{:T(128)}, f32[2,256,256]{1,2,0:T(8,128)S(1)}, s32[]{:T(128)}, s32[]{:T(128)}, f32[]{:T(128)}, /*index=5*/f32[]{:T(128)}, f32[]{:T(128)}, s32[]{:T(128)}) %tuple.132), condition=%wide.region_8.7_spmd, body=%wide.region_2.6_spmd.sunk | while | flops 807567872 | bytes 12259688 | solution.py:428
  2900.3 684.9 %while.69 = (s32[]{:T(128)}, f32[2,256,256]{2,1,0:T(8,128)S(1)}, f32[2,256,256]{1,2,0:T(8,128)S(1)}, f32[2,256,256]{2,1,0:T(8,128)S(1)}, s32[]{:T(128)}, /*index...) while((s32[]{:T(128)}, f32[2,256,256]{2,1,0:T(8,128)S(1)}, ...), condition=%wide.region_9.9_spmd, body=%wide.region_1.8_spmd.sunk | while | flops 1210352128 | bytes 15405615 | solution.py:437
  3606.2 684.9 %while.69 = (s32[]{:T(128)}, f32[2,256,256]{2,1,0:T(8,128)S(1)}, f32[2,256,256]{1,2,0:T(8,128)S(1)}, f32[2,256,256]{2,1,0:T(8,128)S(1)}, s32[]{:T(128)}, /*index...) while((s32[]{:T(128)}, f32[2,256,256]{2,1,0:T(8,128)S(1)}, ...), condition=%wide.region_9.9_spmd, body=%wide.region_1.8_spmd.sunk | while | flops 1210352128 | bytes 15405615 | solution.py:437
  3607.2 341.4 %while.70 = (s32[]{:T(128)}, f32[2,256,256]{1,2,0:T(8,128)S(1)}, s32[]{:T(128)}, s32[]{:T(128)}, f32[]{:T(128)}, /*index=5*/f32[]{:T(128)}, f32[]{:T(128)}, s32[]{:T(128)}) while((s32[]{:T(128)}, f32[2,256,256]{1,2,0:T(8,128)S(1)}, s32[]{:T(128)}, s32[]{:T(128)}, f32[]{:T(128)}, /*index=5*/f32[]{:T(128)}, f32[]{:T(128)}, s32[]{:T(128)}) %tuple.132), condition=%wide.region_8.7_spmd, body=%wide.region_2.6_spmd.sunk | while | flops 807567872 | bytes 12259688 | solution.py:428
  3949.7 341.4 %while.70 = (s32[]{:T(128)}, f32[2,256,256]{1,2,0:T(8,128)S(1)}, s32[]{:T(128)}, s32[]{:T(128)}, f32[]{:T(128)}, /*index=5*/f32[]{:T(128)}, f32[]{:T(128)}, s32[]{:T(128)}) while((s32[]{:T(128)}, f32[2,256,256]{1,2,0:T(8,128)S(1)}, s32[]{:T(128)}, s32[]{:T(128)}, f32[]{:T(128)}, /*index=5*/f32[]{:T(128)}, f32[]{:T(128)}, s32[]{:T(128)}) %tuple.132), condition=%wide.region_8.7_spmd, body=%wide.region_2.6_spmd.sunk | while | flops 807567872 | bytes 12259688 | solution.py:428
  4312.2 684.9 %while.69 = (s32[]{:T(128)}, f32[2,256,256]{2,1,0:T(8,128)S(1)}, f32[2,256,256]{1,2,0:T(8,128)S(1)}, f32[2,256,256]{2,1,0:T(8,128)S(1)}, s32[]{:T(128)}, /*index...) while((s32[]{:T(128)}, f32[2,256,256]{2,1,0:T(8,128)S(1)}, ...), condition=%wide.region_9.9_spmd, body=%wide.region_1.8_spmd.sunk | while | flops 1210352128 | bytes 15405615 | solution.py:437
  4655.6 341.4 %while.70 = (s32[]{:T(128)}, f32[2,256,256]{1,2,0:T(8,128)S(1)}, s32[]{:T(128)}, s32[]{:T(128)}, f32[]{:T(128)}, /*index=5*/f32[]{:T(128)}, f32[]{:T(128)}, s32[]{:T(128)}) while((s32[]{:T(128)}, f32[2,256,256]{1,2,0:T(8,128)S(1)}, s32[]{:T(128)}, s32[]{:T(128)}, f32[]{:T(128)}, /*index=5*/f32[]{:T(128)}, f32[]{:T(128)}, s32[]{:T(128)}) %tuple.132), condition=%wide.region_8.7_spmd, body=%wide.region_2.6_spmd.sunk | while | flops 807567872 | bytes 12259688 | solution.py:428
  5018.1 684.9 %while.69 = (s32[]{:T(128)}, f32[2,256,256]{2,1,0:T(8,128)S(1)}, f32[2,256,256]{1,2,0:T(8,128)S(1)}, f32[2,256,256]{2,1,0:T(8,128)S(1)}, s32[]{:T(128)}, /*index...) while((s32[]{:T(128)}, f32[2,256,256]{2,1,0:T(8,128)S(1)}, ...), condition=%wide.region_9.9_spmd, body=%wide.region_1.8_spmd.sunk | while | flops 1210352128 | bytes 15405615 | solution.py:437
  5724.0 684.9 %while.69 = (s32[]{:T(128)}, f32[2,256,256]{2,1,0:T(8,128)S(1)}, f32[2,256,256]{1,2,0:T(8,128)S(1)}, f32[2,256,256]{2,1,0:T(8,128)S(1)}, s32[]{:T(128)}, /*index...) while((s32[]{:T(128)}, f32[2,256,256]{2,1,0:T(8,128)S(1)}, ...), condition=%wide.region_9.9_spmd, body=%wide.region_1.8_spmd.sunk | while | flops 1210352128 | bytes 15405615 | solution.py:437
  6067.4 341.4 %while.70 = (s32[]{:T(128)}, f32[2,256,256]{1,2,0:T(8,128)S(1)}, s32[]{:T(128)}, s32[]{:T(128)}, f32[]{:T(128)}, /*index=5*/f32[]{:T(128)}, f32[]{:T(128)}, s32[]{:T(128)}) while((s32[]{:T(128)}, f32[2,256,256]{1,2,0:T(8,128)S(1)}, s32[]{:T(128)}, s32[]{:T(128)}, f32[]{:T(128)}, /*index=5*/f32[]{:T(128)}, f32[]{:T(128)}, s32[]{:T(128)}) %tuple.132), condition=%wide.region_8.7_spmd, body=%wide.region_2.6_spmd.sunk | while | flops 807567872 | bytes 12259688 | solution.py:428
  6429.9 684.9 %while.69 = (s32[]{:T(128)}, f32[2,256,256]{2,1,0:T(8,128)S(1)}, f32[2,256,256]{1,2,0:T(8,128)S(1)}, f32[2,256,256]{2,1,0:T(8,128)S(1)}, s32[]{:T(128)}, /*index...) while((s32[]{:T(128)}, f32[2,256,256]{2,1,0:T(8,128)S(1)}, ...), condition=%wide.region_9.9_spmd, body=%wide.region_1.8_spmd.sunk | while | flops 1210352128 | bytes 15405615 | solution.py:437
  6773.4 341.4 %while.70 = (s32[]{:T(128)}, f32[2,256,256]{1,2,0:T(8,128)S(1)}, s32[]{:T(128)}, s32[]{:T(128)}, f32[]{:T(128)}, /*index=5*/f32[]{:T(128)}, f32[]{:T(128)}, s32[]{:T(128)}) while((s32[]{:T(128)}, f32[2,256,256]{1,2,0:T(8,128)S(1)}, s32[]{:T(128)}, s32[]{:T(128)}, f32[]{:T(128)}, /*index=5*/f32[]{:T(128)}, f32[]{:T(128)}, s32[]{:T(128)}) %tuple.132), condition=%wide.region_8.7_spmd, body=%wide.region_2.6_spmd.sunk | while | flops 807567872 | bytes 12259688 | solution.py:428
  7135.8 684.9 %while.69 = (s32[]{:T(128)}, f32[2,256,256]{2,1,0:T(8,128)S(1)}, f32[2,256,256]{1,2,0:T(8,128)S(1)}, f32[2,256,256]{2,1,0:T(8,128)S(1)}, s32[]{:T(128)}, /*index...) while((s32[]{:T(128)}, f32[2,256,256]{2,1,0:T(8,128)S(1)}, ...), condition=%wide.region_9.9_spmd, body=%wide.region_1.8_spmd.sunk | while | flops 1210352128 | bytes 15405615 | solution.py:437
  7841.8 684.9 %while.69 = (s32[]{:T(128)}, f32[2,256,256]{2,1,0:T(8,128)S(1)}, f32[2,256,256]{1,2,0:T(8,128)S(1)}, f32[2,256,256]{2,1,0:T(8,128)S(1)}, s32[]{:T(128)}, /*index...) while((s32[]{:T(128)}, f32[2,256,256]{2,1,0:T(8,128)S(1)}, ...), condition=%wide.region_9.9_spmd, body=%wide.region_1.8_spmd.sunk | while | flops 1210352128 | bytes 15405615 | solution.py:437
  7842.8 341.4 %while.70 = (s32[]{:T(128)}, f32[2,256,256]{1,2,0:T(8,128)S(1)}, s32[]{:T(128)}, s32[]{:T(128)}, f32[]{:T(128)}, /*index=5*/f32[]{:T(128)}, f32[]{:T(128)}, s32[]{:T(128)}) while((s32[]{:T(128)}, f32[2,256,256]{1,2,0:T(8,128)S(1)}, s32[]{:T(128)}, s32[]{:T(128)}, f32[]{:T(128)}, /*index=5*/f32[]{:T(128)}, f32[]{:T(128)}, s32[]{:T(128)}) %tuple.132), condition=%wide.region_8.7_spmd, body=%wide.region_2.6_spmd.sunk | while | flops 807567872 | bytes 12259688 | solution.py:428
  8185.2 341.4 %while.70 = (s32[]{:T(128)}, f32[2,256,256]{1,2,0:T(8,128)S(1)}, s32[]{:T(128)}, s32[]{:T(128)}, f32[]{:T(128)}, /*index=5*/f32[]{:T(128)}, f32[]{:T(128)}, s32[]{:T(128)}) while((s32[]{:T(128)}, f32[2,256,256]{1,2,0:T(8,128)S(1)}, s32[]{:T(128)}, s32[]{:T(128)}, f32[]{:T(128)}, /*index=5*/f32[]{:T(128)}, f32[]{:T(128)}, s32[]{:T(128)}) %tuple.132), condition=%wide.region_8.7_spmd, body=%wide.region_2.6_spmd.sunk | while | flops 807567872 | bytes 12259688 | solution.py:428
  8547.7 684.9 %while.69 = (s32[]{:T(128)}, f32[2,256,256]{2,1,0:T(8,128)S(1)}, f32[2,256,256]{1,2,0:T(8,128)S(1)}, f32[2,256,256]{2,1,0:T(8,128)S(1)}, s32[]{:T(128)}, /*index...) while((s32[]{:T(128)}, f32[2,256,256]{2,1,0:T(8,128)S(1)}, ...), condition=%wide.region_9.9_spmd, body=%wide.region_1.8_spmd.sunk | while | flops 1210352128 | bytes 15405615 | solution.py:437
  8891.1 341.4 %while.70 = (s32[]{:T(128)}, f32[2,256,256]{1,2,0:T(8,128)S(1)}, s32[]{:T(128)}, s32[]{:T(128)}, f32[]{:T(128)}, /*index=5*/f32[]{:T(128)}, f32[]{:T(128)}, s32[]{:T(128)}) while((s32[]{:T(128)}, f32[2,256,256]{1,2,0:T(8,128)S(1)}, s32[]{:T(128)}, s32[]{:T(128)}, f32[]{:T(128)}, /*index=5*/f32[]{:T(128)}, f32[]{:T(128)}, s32[]{:T(128)}) %tuple.132), condition=%wide.region_8.7_spmd, body=%wide.region_2.6_spmd.sunk | while | flops 807567872 | bytes 12259688 | solution.py:428
  9253.6 684.9 %while.69 = (s32[]{:T(128)}, f32[2,256,256]{2,1,0:T(8,128)S(1)}, f32[2,256,256]{1,2,0:T(8,128)S(1)}, f32[2,256,256]{2,1,0:T(8,128)S(1)}, s32[]{:T(128)}, /*index...) while((s32[]{:T(128)}, f32[2,256,256]{2,1,0:T(8,128)S(1)}, ...), condition=%wide.region_9.9_spmd, body=%wide.region_1.8_spmd.sunk | while | flops 1210352128 | bytes 15405615 | solution.py:437
  9959.5 684.9 %while.69 = (s32[]{:T(128)}, f32[2,256,256]{2,1,0:T(8,128)S(1)}, f32[2,256,256]{1,2,0:T(8,128)S(1)}, f32[2,256,256]{2,1,0:T(8,128)S(1)}, s32[]{:T(128)}, /*index...) while((s32[]{:T(128)}, f32[2,256,256]{2,1,0:T(8,128)S(1)}, ...), condition=%wide.region_9.9_spmd, body=%wide.region_1.8_spmd.sunk | while | flops 1210352128 | bytes 15405615 | solution.py:437
  9960.5 341.4 %while.70 = (s32[]{:T(128)}, f32[2,256,256]{1,2,0:T(8,128)S(1)}, s32[]{:T(128)}, s32[]{:T(128)}, f32[]{:T(128)}, /*index=5*/f32[]{:T(128)}, f32[]{:T(128)}, s32[]{:T(128)}) while((s32[]{:T(128)}, f32[2,256,256]{1,2,0:T(8,128)S(1)}, s32[]{:T(128)}, s32[]{:T(128)}, f32[]{:T(128)}, /*index=5*/f32[]{:T(128)}, f32[]{:T(128)}, s32[]{:T(128)}) %tuple.132), condition=%wide.region_8.7_spmd, body=%wide.region_2.6_spmd.sunk | while | flops 807567872 | bytes 12259688 | solution.py:428
  10303.0 341.4 %while.70 = (s32[]{:T(128)}, f32[2,256,256]{1,2,0:T(8,128)S(1)}, s32[]{:T(128)}, s32[]{:T(128)}, f32[]{:T(128)}, /*index=5*/f32[]{:T(128)}, f32[]{:T(128)}, s32[]{:T(128)}) while((s32[]{:T(128)}, f32[2,256,256]{1,2,0:T(8,128)S(1)}, s32[]{:T(128)}, s32[]{:T(128)}, f32[]{:T(128)}, /*index=5*/f32[]{:T(128)}, f32[]{:T(128)}, s32[]{:T(128)}) %tuple.132), condition=%wide.region_8.7_spmd, body=%wide.region_2.6_spmd.sunk | while | flops 807567872 | bytes 12259688 | solution.py:428
  10665.5 684.9 %while.69 = (s32[]{:T(128)}, f32[2,256,256]{2,1,0:T(8,128)S(1)}, f32[2,256,256]{1,2,0:T(8,128)S(1)}, f32[2,256,256]{2,1,0:T(8,128)S(1)}, s32[]{:T(128)}, /*index...) while((s32[]{:T(128)}, f32[2,256,256]{2,1,0:T(8,128)S(1)}, ...), condition=%wide.region_9.9_spmd, body=%wide.region_1.8_spmd.sunk | while | flops 1210352128 | bytes 15405615 | solution.py:437
  11008.9 341.4 %while.70 = (s32[]{:T(128)}, f32[2,256,256]{1,2,0:T(8,128)S(1)}, s32[]{:T(128)}, s32[]{:T(128)}, f32[]{:T(128)}, /*index=5*/f32[]{:T(128)}, f32[]{:T(128)}, s32[]{:T(128)}) while((s32[]{:T(128)}, f32[2,256,256]{1,2,0:T(8,128)S(1)}, s32[]{:T(128)}, s32[]{:T(128)}, f32[]{:T(128)}, /*index=5*/f32[]{:T(128)}, f32[]{:T(128)}, s32[]{:T(128)}) %tuple.132), condition=%wide.region_8.7_spmd, body=%wide.region_2.6_spmd.sunk | while | flops 807567872 | bytes 12259688 | solution.py:428
  (4043 shorter events, 17746.2 us)
Async XLA Ops:
  1.8 8.1 collective-permute-start.1
  3.3 9.0 collective-permute-start.2
  13.3 8.2 collective-permute-start.3
  15.5 6.6 collective-permute-start.4
  23.7 21.8 collective-permute-start.10
  24.3 21.1 collective-permute-start.8
  28.2 17.3 collective-permute-start.9
  36.9 4.9 collective-permute-start.5
  37.0 5.5 collective-permute-start.6
  41.8 3.6 collective-permute-start.7
  46.1 9.1 collective-permute-start.11
  46.2 5.4 collective-permute-start.12
  47.2 6.0 collective-permute-start.13
  51.6 3.6 collective-permute-start.14
  766.2 13.5 collective-permute-start
  1472.1 14.3 copy-start.2
  1472.1 13.5 collective-permute-start
  2178.0 13.5 collective-permute-start
  2884.0 13.5 collective-permute-start
  3589.9 14.3 copy-start.2
  3589.9 13.5 collective-permute-start
  4295.8 13.5 collective-permute-start
  5001.7 13.5 collective-permute-start
  5707.6 13.5 collective-permute-start
  6413.6 13.5 collective-permute-start
  7119.5 13.5 collective-permute-start
  7825.4 13.5 collective-permute-start
  8531.3 13.5 collective-permute-start
  9237.3 13.5 collective-permute-start
  9943.2 13.5 collective-permute-start
  10649.1 13.5 collective-permute-start
  11355.0 13.5 collective-permute-start
  (80 other events, 300.6 us)

commit v4 on v3

--- a/solution.py
+++ b/solution.py
@@ -14,7 +14,7 @@
 GRAM = 6
 F32 = jnp.float32
 BF16 = jnp.bfloat16
-LIMIT = 17.97
+LIMIT = 16.59
 ORTHO2 = 4.0e-4
 
 
@@ -79,8 +79,8 @@
             unit = jnp.where(lane - j == row, 1.0, 0.0)
             unit2 = jnp.where(lane - j - 8 == row, 1.0, 0.0)
             at = [jnp.full((8, HALF), j + c, jnp.int32) for c in range(B)]
-            below = rows >= k + B
-            own = (lanes >= k) & (lanes < k + B)
+            own = (rows >= k + B) & (lanes >= k) & (lanes < k + B)
+            later = lax.broadcasted_iota(jnp.int32, (B, D - n0), 1) >= j + B
             tops = [[a[pl.ds(k, 8), i * HALF : (i + 1) * HALF] for i in range(2)] for a in refs]
             bots = [[a[pl.ds(k + 8, 8), i * HALF : (i + 1) * HALF] for i in range(2)] for a in refs]
             ats = [pick(t[h], at[c]) for c in range(8) for t in tops]
@@ -142,15 +142,17 @@
             updates = []
             for n in range(nb):
                 hi, md, lo = split3(scaled[n])
+                right = jnp.concatenate([hi, lo, md, hi, md, hi], 0)
+                hi, md, lo = split3(jnp.where(later, scaled[n][:, n0:], 0.0))
                 left = jnp.concatenate([lo, hi, md, md, hi, hi], 0)
-                right = jnp.concatenate([hi, lo, md, hi, md, hi], 0)
-                updates.append(dg(left[:, n0:], right, 0, 0))
+                updates.append(dg(left, right, 0, 0))
             for n in range(nb):
                 for i in range(2):
                     old = refs[n][n0:, i * HALF : (i + 1) * HALF]
                     kept = jnp.where(own, 0.0, old) if i == h else old
-                    now = kept - updates[n][:, i * HALF : (i + 1) * HALF]
-                    refs[n][n0:, i * HALF : (i + 1) * HALF] = jnp.where(below, now, old)
+                    refs[n][n0:, i * HALF : (i + 1) * HALF] = (
+                        kept - updates[n][:, i * HALF : (i + 1) * HALF]
+                    )
                 refs[n][pl.ds(k, B), :] = scaled[n]
             return carry
 
@@ -254,7 +256,7 @@
 
     def products(t, carry):
         left = [jnp.where(t == 0, prev_ref[m], c_ref[m]) for m in range(2)]
-        out = [mm(left[m], now[m], passes=SOLVE) for m in range(2)]
+        out = [mm(left[m], now[m]) for m in range(2)]
         for m in range(2):
             now[m] = out[m]
             m_ref[t, m] = out[m]
@@ -290,7 +292,7 @@
             jnp.where(c <= r, jnp.where(t == 0, refs[m][...], refs[2 + m][...]), 0.0)
             for m in range(2)
         ]
-        ys = [mm(m_ref[t, m], inv[m], 1, 1, passes=SOLVE) for m in range(2)]
+        ys = [mm(m_ref[t, m], inv[m], 1, 1) for m in range(2)]
         for m in range(2):
             change, err = refinement(ys[m], 1)
             m_ref[t, m] = ys[m] - change

time: 11400 us -> 11400 us (level)
  no operation moved by 1% of the time
where the time goes in v4:
time: 11400 us
  other arithmetic  10300 us (90%)
  local copies, waits for them, and re-layouts  450 us (4%)
  matrix products  331 us (3%)
  waiting for transfers between devices  202 us (2%)
    another operation x960, other arithmetic, turn(): lower = jnp.linalg.cholesky(gram)  6420 us
    another operation x384, other arithmetic, turn(): lax.linalg.triangular_solve(lower, flip(y), left_side=True, lower=True)  3790 us
    another operation x576, local copies, waits for them, and re-layouts  377 us

profile of v4, /device:TPU:48, one launch (start us, length us, event | category | flops | bytes accessed | tf_op | source)
XLA Modules:
  0.0 11371.0 jit_solution(17048617780709806247)
XLA Ops:
  76.4 11294.4 %while.68 = (s32[]{:T(128)}, f32[2,256,256]{2,1,0:T(8,128)}, f32[2,256,256]{2,1,0:T(8,128)}, f32[2,256,256]{2,1,0:T(8,128)}, s32[]{:T(128)}, /*index=5*/pred[]{:...) while((s32[]{:T(128)}, f32[2,256,256]{2,1,0:T(8,128)}, ...), condition=%wide.region_12.13_spmd, body=%wide.region_0.12_spmd.sunk | while | flops 2419032832 | bytes 38607924 | solution.py:509
  77.4 684.9 %while.69 = (s32[]{:T(128)}, f32[2,256,256]{2,1,0:T(8,128)S(1)}, f32[2,256,256]{1,2,0:T(8,128)S(1)}, f32[2,256,256]{2,1,0:T(8,128)S(1)}, s32[]{:T(128)}, /*index...) while((s32[]{:T(128)}, f32[2,256,256]{2,1,0:T(8,128)S(1)}, ...), condition=%wide.region_9.9_spmd, body=%wide.region_1.8_spmd.sunk | while | flops 1210352128 | bytes 15405615 | solution.py:439
  420.9 341.4 %while.70 = (s32[]{:T(128)}, f32[2,256,256]{1,2,0:T(8,128)S(1)}, s32[]{:T(128)}, s32[]{:T(128)}, f32[]{:T(128)}, /*index=5*/f32[]{:T(128)}, f32[]{:T(128)}, s32[]{:T(128)}) while((s32[]{:T(128)}, f32[2,256,256]{1,2,0:T(8,128)S(1)}, s32[]{:T(128)}, s32[]{:T(128)}, f32[]{:T(128)}, /*index=5*/f32[]{:T(128)}, f32[]{:T(128)}, s32[]{:T(128)}) %tuple.132), condition=%wide.region_8.7_spmd, body=%wide.region_2.6_spmd.sunk | while | flops 807567872 | bytes 12259688 | solution.py:430
  783.3 684.9 %while.69 = (s32[]{:T(128)}, f32[2,256,256]{2,1,0:T(8,128)S(1)}, f32[2,256,256]{1,2,0:T(8,128)S(1)}, f32[2,256,256]{2,1,0:T(8,128)S(1)}, s32[]{:T(128)}, /*index...) while((s32[]{:T(128)}, f32[2,256,256]{2,1,0:T(8,128)S(1)}, ...), condition=%wide.region_9.9_spmd, body=%wide.region_1.8_spmd.sunk | while | flops 1210352128 | bytes 15405615 | solution.py:439
  1489.3 684.9 %while.69 = (s32[]{:T(128)}, f32[2,256,256]{2,1,0:T(8,128)S(1)}, f32[2,256,256]{1,2,0:T(8,128)S(1)}, f32[2,256,256]{2,1,0:T(8,128)S(1)}, s32[]{:T(128)}, /*index...) while((s32[]{:T(128)}, f32[2,256,256]{2,1,0:T(8,128)S(1)}, ...), condition=%wide.region_9.9_spmd, body=%wide.region_1.8_spmd.sunk | while | flops 1210352128 | bytes 15405615 | solution.py:439
  1490.3 341.4 %while.70 = (s32[]{:T(128)}, f32[2,256,256]{1,2,0:T(8,128)S(1)}, s32[]{:T(128)}, s32[]{:T(128)}, f32[]{:T(128)}, /*index=5*/f32[]{:T(128)}, f32[]{:T(128)}, s32[]{:T(128)}) while((s32[]{:T(128)}, f32[2,256,256]{1,2,0:T(8,128)S(1)}, s32[]{:T(128)}, s32[]{:T(128)}, f32[]{:T(128)}, /*index=5*/f32[]{:T(128)}, f32[]{:T(128)}, s32[]{:T(128)}) %tuple.132), condition=%wide.region_8.7_spmd, body=%wide.region_2.6_spmd.sunk | while | flops 807567872 | bytes 12259688 | solution.py:430
  1832.7 341.4 %while.70 = (s32[]{:T(128)}, f32[2,256,256]{1,2,0:T(8,128)S(1)}, s32[]{:T(128)}, s32[]{:T(128)}, f32[]{:T(128)}, /*index=5*/f32[]{:T(128)}, f32[]{:T(128)}, s32[]{:T(128)}) while((s32[]{:T(128)}, f32[2,256,256]{1,2,0:T(8,128)S(1)}, s32[]{:T(128)}, s32[]{:T(128)}, f32[]{:T(128)}, /*index=5*/f32[]{:T(128)}, f32[]{:T(128)}, s32[]{:T(128)}) %tuple.132), condition=%wide.region_8.7_spmd, body=%wide.region_2.6_spmd.sunk | while | flops 807567872 | bytes 12259688 | solution.py:430
  2195.2 684.9 %while.69 = (s32[]{:T(128)}, f32[2,256,256]{2,1,0:T(8,128)S(1)}, f32[2,256,256]{1,2,0:T(8,128)S(1)}, f32[2,256,256]{2,1,0:T(8,128)S(1)}, s32[]{:T(128)}, /*index...) while((s32[]{:T(128)}, f32[2,256,256]{2,1,0:T(8,128)S(1)}, ...), condition=%wide.region_9.9_spmd, body=%wide.region_1.8_spmd.sunk | while | flops 1210352128 | bytes 15405615 | solution.py:439
  2538.6 341.4 %while.70 = (s32[]{:T(128)}, f32[2,256,256]{1,2,0:T(8,128)S(1)}, s32[]{:T(128)}, s32[]{:T(128)}, f32[]{:T(128)}, /*index=5*/f32[]{:T(128)}, f32[]{:T(128)}, s32[]{:T(128)}) while((s32[]{:T(128)}, f32[2,256,256]{1,2,0:T(8,128)S(1)}, s32[]{:T(128)}, s32[]{:T(128)}, f32[]{:T(128)}, /*index=5*/f32[]{:T(128)}, f32[]{:T(128)}, s32[]{:T(128)}) %tuple.132), condition=%wide.region_8.7_spmd, body=%wide.region_2.6_spmd.sunk | while | flops 807567872 | bytes 12259688 | solution.py:430
  2901.1 684.9 %while.69 = (s32[]{:T(128)}, f32[2,256,256]{2,1,0:T(8,128)S(1)}, f32[2,256,256]{1,2,0:T(8,128)S(1)}, f32[2,256,256]{2,1,0:T(8,128)S(1)}, s32[]{:T(128)}, /*index...) while((s32[]{:T(128)}, f32[2,256,256]{2,1,0:T(8,128)S(1)}, ...), condition=%wide.region_9.9_spmd, body=%wide.region_1.8_spmd.sunk | while | flops 1210352128 | bytes 15405615 | solution.py:439
  3607.0 684.9 %while.69 = (s32[]{:T(128)}, f32[2,256,256]{2,1,0:T(8,128)S(1)}, f32[2,256,256]{1,2,0:T(8,128)S(1)}, f32[2,256,256]{2,1,0:T(8,128)S(1)}, s32[]{:T(128)}, /*index...) while((s32[]{:T(128)}, f32[2,256,256]{2,1,0:T(8,128)S(1)}, ...), condition=%wide.region_9.9_spmd, body=%wide.region_1.8_spmd.sunk | while | flops 1210352128 | bytes 15405615 | solution.py:439
  3608.0 341.4 %while.70 = (s32[]{:T(128)}, f32[2,256,256]{1,2,0:T(8,128)S(1)}, s32[]{:T(128)}, s32[]{:T(128)}, f32[]{:T(128)}, /*index=5*/f32[]{:T(128)}, f32[]{:T(128)}, s32[]{:T(128)}) while((s32[]{:T(128)}, f32[2,256,256]{1,2,0:T(8,128)S(1)}, s32[]{:T(128)}, s32[]{:T(128)}, f32[]{:T(128)}, /*index=5*/f32[]{:T(128)}, f32[]{:T(128)}, s32[]{:T(128)}) %tuple.132), condition=%wide.region_8.7_spmd, body=%wide.region_2.6_spmd.sunk | while | flops 807567872 | bytes 12259688 | solution.py:430
  3950.5 341.4 %while.70 = (s32[]{:T(128)}, f32[2,256,256]{1,2,0:T(8,128)S(1)}, s32[]{:T(128)}, s32[]{:T(128)}, f32[]{:T(128)}, /*index=5*/f32[]{:T(128)}, f32[]{:T(128)}, s32[]{:T(128)}) while((s32[]{:T(128)}, f32[2,256,256]{1,2,0:T(8,128)S(1)}, s32[]{:T(128)}, s32[]{:T(128)}, f32[]{:T(128)}, /*index=5*/f32[]{:T(128)}, f32[]{:T(128)}, s32[]{:T(128)}) %tuple.132), condition=%wide.region_8.7_spmd, body=%wide.region_2.6_spmd.sunk | while | flops 807567872 | bytes 12259688 | solution.py:430
  4313.0 684.9 %while.69 = (s32[]{:T(128)}, f32[2,256,256]{2,1,0:T(8,128)S(1)}, f32[2,256,256]{1,2,0:T(8,128)S(1)}, f32[2,256,256]{2,1,0:T(8,128)S(1)}, s32[]{:T(128)}, /*index...) while((s32[]{:T(128)}, f32[2,256,256]{2,1,0:T(8,128)S(1)}, ...), condition=%wide.region_9.9_spmd, body=%wide.region_1.8_spmd.sunk | while | flops 1210352128 | bytes 15405615 | solution.py:439
  4656.4 341.4 %while.70 = (s32[]{:T(128)}, f32[2,256,256]{1,2,0:T(8,128)S(1)}, s32[]{:T(128)}, s32[]{:T(128)}, f32[]{:T(128)}, /*index=5*/f32[]{:T(128)}, f32[]{:T(128)}, s32[]{:T(128)}) while((s32[]{:T(128)}, f32[2,256,256]{1,2,0:T(8,128)S(1)}, s32[]{:T(128)}, s32[]{:T(128)}, f32[]{:T(128)}, /*index=5*/f32[]{:T(128)}, f32[]{:T(128)}, s32[]{:T(128)}) %tuple.132), condition=%wide.region_8.7_spmd, body=%wide.region_2.6_spmd.sunk | while | flops 807567872 | bytes 12259688 | solution.py:430
  5018.9 684.9 %while.69 = (s32[]{:T(128)}, f32[2,256,256]{2,1,0:T(8,128)S(1)}, f32[2,256,256]{1,2,0:T(8,128)S(1)}, f32[2,256,256]{2,1,0:T(8,128)S(1)}, s32[]{:T(128)}, /*index...) while((s32[]{:T(128)}, f32[2,256,256]{2,1,0:T(8,128)S(1)}, ...), condition=%wide.region_9.9_spmd, body=%wide.region_1.8_spmd.sunk | while | flops 1210352128 | bytes 15405615 | solution.py:439
  5724.8 684.9 %while.69 = (s32[]{:T(128)}, f32[2,256,256]{2,1,0:T(8,128)S(1)}, f32[2,256,256]{1,2,0:T(8,128)S(1)}, f32[2,256,256]{2,1,0:T(8,128)S(1)}, s32[]{:T(128)}, /*index...) while((s32[]{:T(128)}, f32[2,256,256]{2,1,0:T(8,128)S(1)}, ...), condition=%wide.region_9.9_spmd, body=%wide.region_1.8_spmd.sunk | while | flops 1210352128 | bytes 15405615 | solution.py:439
  6068.2 341.4 %while.70 = (s32[]{:T(128)}, f32[2,256,256]{1,2,0:T(8,128)S(1)}, s32[]{:T(128)}, s32[]{:T(128)}, f32[]{:T(128)}, /*index=5*/f32[]{:T(128)}, f32[]{:T(128)}, s32[]{:T(128)}) while((s32[]{:T(128)}, f32[2,256,256]{1,2,0:T(8,128)S(1)}, s32[]{:T(128)}, s32[]{:T(128)}, f32[]{:T(128)}, /*index=5*/f32[]{:T(128)}, f32[]{:T(128)}, s32[]{:T(128)}) %tuple.132), condition=%wide.region_8.7_spmd, body=%wide.region_2.6_spmd.sunk | while | flops 807567872 | bytes 12259688 | solution.py:430
  6430.7 684.9 %while.69 = (s32[]{:T(128)}, f32[2,256,256]{2,1,0:T(8,128)S(1)}, f32[2,256,256]{1,2,0:T(8,128)S(1)}, f32[2,256,256]{2,1,0:T(8,128)S(1)}, s32[]{:T(128)}, /*index...) while((s32[]{:T(128)}, f32[2,256,256]{2,1,0:T(8,128)S(1)}, ...), condition=%wide.region_9.9_spmd, body=%wide.region_1.8_spmd.sunk | while | flops 1210352128 | bytes 15405615 | solution.py:439
  6774.2 341.4 %while.70 = (s32[]{:T(128)}, f32[2,256,256]{1,2,0:T(8,128)S(1)}, s32[]{:T(128)}, s32[]{:T(128)}, f32[]{:T(128)}, /*index=5*/f32[]{:T(128)}, f32[]{:T(128)}, s32[]{:T(128)}) while((s32[]{:T(128)}, f32[2,256,256]{1,2,0:T(8,128)S(1)}, s32[]{:T(128)}, s32[]{:T(128)}, f32[]{:T(128)}, /*index=5*/f32[]{:T(128)}, f32[]{:T(128)}, s32[]{:T(128)}) %tuple.132), condition=%wide.region_8.7_spmd, body=%wide.region_2.6_spmd.sunk | while | flops 807567872 | bytes 12259688 | solution.py:430
  7136.6 684.9 %while.69 = (s32[]{:T(128)}, f32[2,256,256]{2,1,0:T(8,128)S(1)}, f32[2,256,256]{1,2,0:T(8,128)S(1)}, f32[2,256,256]{2,1,0:T(8,128)S(1)}, s32[]{:T(128)}, /*index...) while((s32[]{:T(128)}, f32[2,256,256]{2,1,0:T(8,128)S(1)}, ...), condition=%wide.region_9.9_spmd, body=%wide.region_1.8_spmd.sunk | while | flops 1210352128 | bytes 15405615 | solution.py:439
  7842.6 684.9 %while.69 = (s32[]{:T(128)}, f32[2,256,256]{2,1,0:T(8,128)S(1)}, f32[2,256,256]{1,2,0:T(8,128)S(1)}, f32[2,256,256]{2,1,0:T(8,128)S(1)}, s32[]{:T(128)}, /*index...) while((s32[]{:T(128)}, f32[2,256,256]{2,1,0:T(8,128)S(1)}, ...), condition=%wide.region_9.9_spmd, body=%wide.region_1.8_spmd.sunk | while | flops 1210352128 | bytes 15405615 | solution.py:439
  7843.6 341.4 %while.70 = (s32[]{:T(128)}, f32[2,256,256]{1,2,0:T(8,128)S(1)}, s32[]{:T(128)}, s32[]{:T(128)}, f32[]{:T(128)}, /*index=5*/f32[]{:T(128)}, f32[]{:T(128)}, s32[]{:T(128)}) while((s32[]{:T(128)}, f32[2,256,256]{1,2,0:T(8,128)S(1)}, s32[]{:T(128)}, s32[]{:T(128)}, f32[]{:T(128)}, /*index=5*/f32[]{:T(128)}, f32[]{:T(128)}, s32[]{:T(128)}) %tuple.132), condition=%wide.region_8.7_spmd, body=%wide.region_2.6_spmd.sunk | while | flops 807567872 | bytes 12259688 | solution.py:430
  8186.0 341.4 %while.70 = (s32[]{:T(128)}, f32[2,256,256]{1,2,0:T(8,128)S(1)}, s32[]{:T(128)}, s32[]{:T(128)}, f32[]{:T(128)}, /*index=5*/f32[]{:T(128)}, f32[]{:T(128)}, s32[]{:T(128)}) while((s32[]{:T(128)}, f32[2,256,256]{1,2,0:T(8,128)S(1)}, s32[]{:T(128)}, s32[]{:T(128)}, f32[]{:T(128)}, /*index=5*/f32[]{:T(128)}, f32[]{:T(128)}, s32[]{:T(128)}) %tuple.132), condition=%wide.region_8.7_spmd, body=%wide.region_2.6_spmd.sunk | while | flops 807567872 | bytes 12259688 | solution.py:430
  8548.5 684.9 %while.69 = (s32[]{:T(128)}, f32[2,256,256]{2,1,0:T(8,128)S(1)}, f32[2,256,256]{1,2,0:T(8,128)S(1)}, f32[2,256,256]{2,1,0:T(8,128)S(1)}, s32[]{:T(128)}, /*index...) while((s32[]{:T(128)}, f32[2,256,256]{2,1,0:T(8,128)S(1)}, ...), condition=%wide.region_9.9_spmd, body=%wide.region_1.8_spmd.sunk | while | flops 1210352128 | bytes 15405615 | solution.py:439
  8891.9 341.4 %while.70 = (s32[]{:T(128)}, f32[2,256,256]{1,2,0:T(8,128)S(1)}, s32[]{:T(128)}, s32[]{:T(128)}, f32[]{:T(128)}, /*index=5*/f32[]{:T(128)}, f32[]{:T(128)}, s32[]{:T(128)}) while((s32[]{:T(128)}, f32[2,256,256]{1,2,0:T(8,128)S(1)}, s32[]{:T(128)}, s32[]{:T(128)}, f32[]{:T(128)}, /*index=5*/f32[]{:T(128)}, f32[]{:T(128)}, s32[]{:T(128)}) %tuple.132), condition=%wide.region_8.7_spmd, body=%wide.region_2.6_spmd.sunk | while | flops 807567872 | bytes 12259688 | solution.py:430
  9254.4 684.9 %while.69 = (s32[]{:T(128)}, f32[2,256,256]{2,1,0:T(8,128)S(1)}, f32[2,256,256]{1,2,0:T(8,128)S(1)}, f32[2,256,256]{2,1,0:T(8,128)S(1)}, s32[]{:T(128)}, /*index...) while((s32[]{:T(128)}, f32[2,256,256]{2,1,0:T(8,128)S(1)}, ...), condition=%wide.region_9.9_spmd, body=%wide.region_1.8_spmd.sunk | while | flops 1210352128 | bytes 15405615 | solution.py:439
  9960.3 684.9 %while.69 = (s32[]{:T(128)}, f32[2,256,256]{2,1,0:T(8,128)S(1)}, f32[2,256,256]{1,2,0:T(8,128)S(1)}, f32[2,256,256]{2,1,0:T(8,128)S(1)}, s32[]{:T(128)}, /*index...) while((s32[]{:T(128)}, f32[2,256,256]{2,1,0:T(8,128)S(1)}, ...), condition=%wide.region_9.9_spmd, body=%wide.region_1.8_spmd.sunk | while | flops 1210352128 | bytes 15405615 | solution.py:439
  9961.3 341.4 %while.70 = (s32[]{:T(128)}, f32[2,256,256]{1,2,0:T(8,128)S(1)}, s32[]{:T(128)}, s32[]{:T(128)}, f32[]{:T(128)}, /*index=5*/f32[]{:T(128)}, f32[]{:T(128)}, s32[]{:T(128)}) while((s32[]{:T(128)}, f32[2,256,256]{1,2,0:T(8,128)S(1)}, s32[]{:T(128)}, s32[]{:T(128)}, f32[]{:T(128)}, /*index=5*/f32[]{:T(128)}, f32[]{:T(128)}, s32[]{:T(128)}) %tuple.132), condition=%wide.region_8.7_spmd, body=%wide.region_2.6_spmd.sunk | while | flops 807567872 | bytes 12259688 | solution.py:430
  10303.8 341.4 %while.70 = (s32[]{:T(128)}, f32[2,256,256]{1,2,0:T(8,128)S(1)}, s32[]{:T(128)}, s32[]{:T(128)}, f32[]{:T(128)}, /*index=5*/f32[]{:T(128)}, f32[]{:T(128)}, s32[]{:T(128)}) while((s32[]{:T(128)}, f32[2,256,256]{1,2,0:T(8,128)S(1)}, s32[]{:T(128)}, s32[]{:T(128)}, f32[]{:T(128)}, /*index=5*/f32[]{:T(128)}, f32[]{:T(128)}, s32[]{:T(128)}) %tuple.132), condition=%wide.region_8.7_spmd, body=%wide.region_2.6_spmd.sunk | while | flops 807567872 | bytes 12259688 | solution.py:430
  10666.3 684.9 %while.69 = (s32[]{:T(128)}, f32[2,256,256]{2,1,0:T(8,128)S(1)}, f32[2,256,256]{1,2,0:T(8,128)S(1)}, f32[2,256,256]{2,1,0:T(8,128)S(1)}, s32[]{:T(128)}, /*index...) while((s32[]{:T(128)}, f32[2,256,256]{2,1,0:T(8,128)S(1)}, ...), condition=%wide.region_9.9_spmd, body=%wide.region_1.8_spmd.sunk | while | flops 1210352128 | bytes 15405615 | solution.py:439
  11009.7 341.4 %while.70 = (s32[]{:T(128)}, f32[2,256,256]{1,2,0:T(8,128)S(1)}, s32[]{:T(128)}, s32[]{:T(128)}, f32[]{:T(128)}, /*index=5*/f32[]{:T(128)}, f32[]{:T(128)}, s32[]{:T(128)}) while((s32[]{:T(128)}, f32[2,256,256]{1,2,0:T(8,128)S(1)}, s32[]{:T(128)}, s32[]{:T(128)}, f32[]{:T(128)}, /*index=5*/f32[]{:T(128)}, f32[]{:T(128)}, s32[]{:T(128)}) %tuple.132), condition=%wide.region_8.7_spmd, body=%wide.region_2.6_spmd.sunk | while | flops 807567872 | bytes 12259688 | solution.py:430
  (4043 shorter events, 17747.0 us)
Async XLA Ops:
  1.8 8.1 collective-permute-start.1
  3.3 9.0 collective-permute-start.2
  13.3 8.2 collective-permute-start.3
  15.5 6.6 collective-permute-start.4
  23.7 21.8 collective-permute-start.10
  24.3 21.1 collective-permute-start.8
  28.2 17.3 collective-permute-start.9
  36.9 4.9 collective-permute-start.5
  37.0 5.5 collective-permute-start.6
  41.8 3.6 collective-permute-start.7
  46.1 9.1 collective-permute-start.11
  46.2 5.4 collective-permute-start.12
  47.2 6.0 collective-permute-start.13
  51.6 3.6 collective-permute-start.14
  767.0 13.5 collective-permute-start
  1472.9 14.3 copy-start.2
  1472.9 13.5 collective-permute-start
  2178.8 13.5 collective-permute-start
  2884.8 13.5 collective-permute-start
  3590.7 14.3 copy-start.2
  3590.7 13.5 collective-permute-start
  4296.6 13.5 collective-permute-start
  5002.5 13.5 collective-permute-start
  5708.4 13.5 collective-permute-start
  6414.4 13.5 collective-permute-start
  7120.3 13.5 collective-permute-start
  7826.2 13.5 collective-permute-start
  8532.1 13.5 collective-permute-start
  9238.1 13.5 collective-permute-start
  9944.0 13.5 collective-permute-start
  10649.9 13.5 collective-permute-start
  11355.8 13.5 collective-permute-start
  (80 other events, 300.6 us)

commit v5 on v4

--- a/solution.py
+++ b/solution.py
@@ -180,16 +180,11 @@
     buf[1 - odd] = r0[...]
     buf[2 + high] = c_ref[1]
     buf[3 - high] = r1[...]
-    w_ref[...] = mm(buf[1], buf[0])
+    w = mm(buf[1], buf[0])
+    v = mm(buf[3], buf[2])
     outer = (x == 0) | (x == 3)
-
-    @pl.when(outer)
-    def _():
-        v_ref[...] = buf[2]
-
-    @pl.when(jnp.logical_not(outer))
-    def _():
-        v_ref[...] = mm(buf[3], buf[2])
+    w_ref[...] = w
+    v_ref[...] = jnp.where(outer, buf[2], v)
 
 
 def window_kernel(tab_ref, c_ref, r0, r1, w, q0, q1, prev_ref, t_ref, buf):
@@ -234,10 +229,21 @@
     return jnp.sum(jnp.sum(value, axis=0, keepdims=True), axis=1, keepdims=True)
 
 
+def head_kernel(pos_ref, prev_ref, own, c_ref, head_ref, gram_ref):
+    mine = pos_ref[2]
+    before = mm(prev_ref[mine], own[...])
+    after = mm(c_ref[mine], before)
+    head_ref[0] = before
+    head_ref[1] = after
+    gram_ref[0] = mm(before, before, 0, 0, passes=GRAM)
+    gram_ref[1] = mm(after, after, 0, 0, passes=GRAM)
+
+
 def solve_kernel(
     pos_ref,
     prev_ref,
-    own,
+    head_ref,
+    gram_ref,
     other,
     c_ref,
     d_ref,
@@ -250,40 +256,20 @@
     *scratch,
 ):
     refs, m_ref, now = scratch[:4], scratch[4], scratch[5]
-    mine = pos_ref[2]
-    now[mine] = own[...]
-    now[1 - mine] = other[...]
-
-    def products(t, carry):
-        left = [jnp.where(t == 0, prev_ref[m], c_ref[m]) for m in range(2)]
-        out = [mm(left[m], now[m]) for m in range(2)]
-        for m in range(2):
-            now[m] = out[m]
-            m_ref[t, m] = out[m]
-        return carry
-
-    lax.fori_loop(0, 2, products, 0)
-    for m in range(2):
-        before_ref[m] = m_ref[0, m]
-
-    def grams(t, carry):
-        out = [mm(m_ref[t, m], m_ref[t, m], 0, 0, passes=GRAM) for m in range(2)]
-        for m in range(2):
-            now[m] = out[m]
-
-        @pl.when(t == 0)
-        def _():
-            for m in range(2):
-                refs[m][...] = now[m]
-
-        @pl.when(t == 1)
-        def _():
-            for m in range(2):
-                refs[2 + m][...] = now[m]
-
-        return carry
-
-    lax.fori_loop(0, 2, grams, 0)
+    slots = (pos_ref[2], 1 - pos_ref[2])
+    rest = slots[1]
+    before = mm(prev_ref[rest], other[...])
+    after = mm(c_ref[rest], before)
+    m_ref[0, 0] = head_ref[0]
+    m_ref[1, 0] = head_ref[1]
+    m_ref[0, 1] = before
+    m_ref[1, 1] = after
+    refs[0][...] = gram_ref[0]
+    refs[2][...] = gram_ref[1]
+    refs[1][...] = mm(before, before, 0, 0, passes=GRAM)
+    refs[3][...] = mm(after, after, 0, 0, passes=GRAM)
+    for n, m in enumerate(slots):
+        before_ref[m] = m_ref[0, n]
     chol_inv(refs)
     r, c = square_iota()
 
@@ -305,7 +291,7 @@
     whole_ref[0] = jnp.where(fine, 0, 1)
 
     def results(t, carry):
-        left = [jnp.where(t == 0, c_ref[m], d_ref[m]) for m in range(2)]
+        left = [jnp.where(t == 0, c_ref[m], d_ref[m]) for m in slots]
         part = [mm(left[m], m_ref[t, m], passes=SOLVE) for m in range(2)]
         out = [mm(m_ref[1, m], part[m], 0, 0, passes=SOLVE) for m in range(2)]
         for m in range(2):
@@ -313,13 +299,13 @@
 
         @pl.when(t == 0)
         def _():
-            for m in range(2):
-                r_ref[m] = jnp.where(c >= r, now[m], 0.0)
+            for n, m in enumerate(slots):
+                r_ref[m] = jnp.where(c >= r, now[n], 0.0)
 
         @pl.when(t == 1)
         def _():
-            for m in range(2):
-                n_ref[m] = now[m]
+            for n, m in enumerate(slots):
+                n_ref[m] = now[n]
 
         return carry
 
@@ -405,6 +391,7 @@
     [(D, D)] * 4 + [(2, 2, D, D), (2, D, D)],
     "solve",
 )
+head = call(head_kernel, (TWO, TWO), [], "head")
 gauge = call(gauge_kernel, TILE, [(2, D, D), (2, D, D)], "gauge")
 
 
@@ -487,7 +474,7 @@
     other = x_pairs(own)
     bound = largest(gauged, [z_ring(gauged, s) for s in (1, 2, 3)])
     new, tri, before, trips, whole = solve(
-        pos, prev, own, other, coupling, diagonal, bound
+        pos, prev, *head(pos, prev, own, coupling), other, coupling, diagonal, bound
     )
     whole = whole.reshape(()) > 0
 

time: 11400 us -> 11400 us (level)
  no operation moved by 1% of the time
where the time goes in v5:
time: 11400 us
  other arithmetic  10300 us (90%)
  local copies, waits for them, and re-layouts  450 us (4%)
  matrix products  331 us (3%)
  waiting for transfers between devices  200 us (2%)
    another operation x960, other arithmetic, turn(): lower = jnp.linalg.cholesky(gram)  6420 us
    another operation x384, other arithmetic, turn(): lax.linalg.triangular_solve(lower, flip(y), left_side=True, lower=True)  3790 us
    another operation x576, local copies, waits for them, and re-layouts  377 us

profile of v5, /device:TPU:48, one launch (start us, length us, event | category | flops | bytes accessed | tf_op | source)
XLA Modules:
  0.0 11368.0 jit_solution(2071430230515885384)
XLA Ops:
  75.6 11292.2 %while.68 = (s32[]{:T(128)}, f32[2,256,256]{2,1,0:T(8,128)}, f32[2,256,256]{2,1,0:T(8,128)}, f32[2,256,256]{2,1,0:T(8,128)}, s32[]{:T(128)}, /*index=5*/pred[]{:...) while((s32[]{:T(128)}, f32[2,256,256]{2,1,0:T(8,128)}, ...), condition=%wide.region_12.13_spmd, body=%wide.region_0.12_spmd.sunk | while | flops 2419032832 | bytes 36510736 | solution.py:496
  76.6 684.9 %while.69 = (s32[]{:T(128)}, f32[2,256,256]{2,1,0:T(8,128)S(1)}, f32[2,256,256]{1,2,0:T(8,128)S(1)}, f32[2,256,256]{2,1,0:T(8,128)S(1)}, s32[]{:T(128)}, /*index...) while((s32[]{:T(128)}, f32[2,256,256]{2,1,0:T(8,128)S(1)}, ...), condition=%wide.region_9.9_spmd, body=%wide.region_1.8_spmd.sunk | while | flops 1210352128 | bytes 15405615 | solution.py:426
  420.1 341.4 %while.70 = (s32[]{:T(128)}, f32[2,256,256]{1,2,0:T(8,128)S(1)}, s32[]{:T(128)}, s32[]{:T(128)}, f32[]{:T(128)}, /*index=5*/f32[]{:T(128)}, f32[]{:T(128)}, s32[]{:T(128)}) while((s32[]{:T(128)}, f32[2,256,256]{1,2,0:T(8,128)S(1)}, s32[]{:T(128)}, s32[]{:T(128)}, f32[]{:T(128)}, /*index=5*/f32[]{:T(128)}, f32[]{:T(128)}, s32[]{:T(128)}) %tuple.132), condition=%wide.region_8.7_spmd, body=%wide.region_2.6_spmd.sunk | while | flops 807567872 | bytes 12259688 | solution.py:417
  782.4 684.9 %while.69 = (s32[]{:T(128)}, f32[2,256,256]{2,1,0:T(8,128)S(1)}, f32[2,256,256]{1,2,0:T(8,128)S(1)}, f32[2,256,256]{2,1,0:T(8,128)S(1)}, s32[]{:T(128)}, /*index...) while((s32[]{:T(128)}, f32[2,256,256]{2,1,0:T(8,128)S(1)}, ...), condition=%wide.region_9.9_spmd, body=%wide.region_1.8_spmd.sunk | while | flops 1210352128 | bytes 15405615 | solution.py:426
  783.4 341.4 %while.70 = (s32[]{:T(128)}, f32[2,256,256]{1,2,0:T(8,128)S(1)}, s32[]{:T(128)}, s32[]{:T(128)}, f32[]{:T(128)}, /*index=5*/f32[]{:T(128)}, f32[]{:T(128)}, s32[]{:T(128)}) while((s32[]{:T(128)}, f32[2,256,256]{1,2,0:T(8,128)S(1)}, s32[]{:T(128)}, s32[]{:T(128)}, f32[]{:T(128)}, /*index=5*/f32[]{:T(128)}, f32[]{:T(128)}, s32[]{:T(128)}) %tuple.132), condition=%wide.region_8.7_spmd, body=%wide.region_2.6_spmd.sunk | while | flops 807567872 | bytes 12259688 | solution.py:417
  1488.2 684.9 %while.69 = (s32[]{:T(128)}, f32[2,256,256]{2,1,0:T(8,128)S(1)}, f32[2,256,256]{1,2,0:T(8,128)S(1)}, f32[2,256,256]{2,1,0:T(8,128)S(1)}, s32[]{:T(128)}, /*index...) while((s32[]{:T(128)}, f32[2,256,256]{2,1,0:T(8,128)S(1)}, ...), condition=%wide.region_9.9_spmd, body=%wide.region_1.8_spmd.sunk | while | flops 1210352128 | bytes 15405615 | solution.py:426
  1489.2 341.4 %while.70 = (s32[]{:T(128)}, f32[2,256,256]{1,2,0:T(8,128)S(1)}, s32[]{:T(128)}, s32[]{:T(128)}, f32[]{:T(128)}, /*index=5*/f32[]{:T(128)}, f32[]{:T(128)}, s32[]{:T(128)}) while((s32[]{:T(128)}, f32[2,256,256]{1,2,0:T(8,128)S(1)}, s32[]{:T(128)}, s32[]{:T(128)}, f32[]{:T(128)}, /*index=5*/f32[]{:T(128)}, f32[]{:T(128)}, s32[]{:T(128)}) %tuple.132), condition=%wide.region_8.7_spmd, body=%wide.region_2.6_spmd.sunk | while | flops 807567872 | bytes 12259688 | solution.py:417
  1831.6 341.4 %while.70 = (s32[]{:T(128)}, f32[2,256,256]{1,2,0:T(8,128)S(1)}, s32[]{:T(128)}, s32[]{:T(128)}, f32[]{:T(128)}, /*index=5*/f32[]{:T(128)}, f32[]{:T(128)}, s32[]{:T(128)}) while((s32[]{:T(128)}, f32[2,256,256]{1,2,0:T(8,128)S(1)}, s32[]{:T(128)}, s32[]{:T(128)}, f32[]{:T(128)}, /*index=5*/f32[]{:T(128)}, f32[]{:T(128)}, s32[]{:T(128)}) %tuple.132), condition=%wide.region_8.7_spmd, body=%wide.region_2.6_spmd.sunk | while | flops 807567872 | bytes 12259688 | solution.py:417
  2194.0 684.9 %while.69 = (s32[]{:T(128)}, f32[2,256,256]{2,1,0:T(8,128)S(1)}, f32[2,256,256]{1,2,0:T(8,128)S(1)}, f32[2,256,256]{2,1,0:T(8,128)S(1)}, s32[]{:T(128)}, /*index...) while((s32[]{:T(128)}, f32[2,256,256]{2,1,0:T(8,128)S(1)}, ...), condition=%wide.region_9.9_spmd, body=%wide.region_1.8_spmd.sunk | while | flops 1210352128 | bytes 15405615 | solution.py:426
  2537.4 341.4 %while.70 = (s32[]{:T(128)}, f32[2,256,256]{1,2,0:T(8,128)S(1)}, s32[]{:T(128)}, s32[]{:T(128)}, f32[]{:T(128)}, /*index=5*/f32[]{:T(128)}, f32[]{:T(128)}, s32[]{:T(128)}) while((s32[]{:T(128)}, f32[2,256,256]{1,2,0:T(8,128)S(1)}, s32[]{:T(128)}, s32[]{:T(128)}, f32[]{:T(128)}, /*index=5*/f32[]{:T(128)}, f32[]{:T(128)}, s32[]{:T(128)}) %tuple.132), condition=%wide.region_8.7_spmd, body=%wide.region_2.6_spmd.sunk | while | flops 807567872 | bytes 12259688 | solution.py:417
  2899.8 684.9 %while.69 = (s32[]{:T(128)}, f32[2,256,256]{2,1,0:T(8,128)S(1)}, f32[2,256,256]{1,2,0:T(8,128)S(1)}, f32[2,256,256]{2,1,0:T(8,128)S(1)}, s32[]{:T(128)}, /*index...) while((s32[]{:T(128)}, f32[2,256,256]{2,1,0:T(8,128)S(1)}, ...), condition=%wide.region_9.9_spmd, body=%wide.region_1.8_spmd.sunk | while | flops 1210352128 | bytes 15405615 | solution.py:426
  3605.5 684.9 %while.69 = (s32[]{:T(128)}, f32[2,256,256]{2,1,0:T(8,128)S(1)}, f32[2,256,256]{1,2,0:T(8,128)S(1)}, f32[2,256,256]{2,1,0:T(8,128)S(1)}, s32[]{:T(128)}, /*index...) while((s32[]{:T(128)}, f32[2,256,256]{2,1,0:T(8,128)S(1)}, ...), condition=%wide.region_9.9_spmd, body=%wide.region_1.8_spmd.sunk | while | flops 1210352128 | bytes 15405615 | solution.py:426
  3949.0 341.4 %while.70 = (s32[]{:T(128)}, f32[2,256,256]{1,2,0:T(8,128)S(1)}, s32[]{:T(128)}, s32[]{:T(128)}, f32[]{:T(128)}, /*index=5*/f32[]{:T(128)}, f32[]{:T(128)}, s32[]{:T(128)}) while((s32[]{:T(128)}, f32[2,256,256]{1,2,0:T(8,128)S(1)}, s32[]{:T(128)}, s32[]{:T(128)}, f32[]{:T(128)}, /*index=5*/f32[]{:T(128)}, f32[]{:T(128)}, s32[]{:T(128)}) %tuple.132), condition=%wide.region_8.7_spmd, body=%wide.region_2.6_spmd.sunk | while | flops 807567872 | bytes 12259688 | solution.py:417
  4311.3 684.9 %while.69 = (s32[]{:T(128)}, f32[2,256,256]{2,1,0:T(8,128)S(1)}, f32[2,256,256]{1,2,0:T(8,128)S(1)}, f32[2,256,256]{2,1,0:T(8,128)S(1)}, s32[]{:T(128)}, /*index...) while((s32[]{:T(128)}, f32[2,256,256]{2,1,0:T(8,128)S(1)}, ...), condition=%wide.region_9.9_spmd, body=%wide.region_1.8_spmd.sunk | while | flops 1210352128 | bytes 15405615 | solution.py:426
  4654.8 341.4 %while.70 = (s32[]{:T(128)}, f32[2,256,256]{1,2,0:T(8,128)S(1)}, s32[]{:T(128)}, s32[]{:T(128)}, f32[]{:T(128)}, /*index=5*/f32[]{:T(128)}, f32[]{:T(128)}, s32[]{:T(128)}) while((s32[]{:T(128)}, f32[2,256,256]{1,2,0:T(8,128)S(1)}, s32[]{:T(128)}, s32[]{:T(128)}, f32[]{:T(128)}, /*index=5*/f32[]{:T(128)}, f32[]{:T(128)}, s32[]{:T(128)}) %tuple.132), condition=%wide.region_8.7_spmd, body=%wide.region_2.6_spmd.sunk | while | flops 807567872 | bytes 12259688 | solution.py:417
  5017.1 684.9 %while.69 = (s32[]{:T(128)}, f32[2,256,256]{2,1,0:T(8,128)S(1)}, f32[2,256,256]{1,2,0:T(8,128)S(1)}, f32[2,256,256]{2,1,0:T(8,128)S(1)}, s32[]{:T(128)}, /*index...) while((s32[]{:T(128)}, f32[2,256,256]{2,1,0:T(8,128)S(1)}, ...), condition=%wide.region_9.9_spmd, body=%wide.region_1.8_spmd.sunk | while | flops 1210352128 | bytes 15405615 | solution.py:426
  5018.1 341.4 %while.70 = (s32[]{:T(128)}, f32[2,256,256]{1,2,0:T(8,128)S(1)}, s32[]{:T(128)}, s32[]{:T(128)}, f32[]{:T(128)}, /*index=5*/f32[]{:T(128)}, f32[]{:T(128)}, s32[]{:T(128)}) while((s32[]{:T(128)}, f32[2,256,256]{1,2,0:T(8,128)S(1)}, s32[]{:T(128)}, s32[]{:T(128)}, f32[]{:T(128)}, /*index=5*/f32[]{:T(128)}, f32[]{:T(128)}, s32[]{:T(128)}) %tuple.132), condition=%wide.region_8.7_spmd, body=%wide.region_2.6_spmd.sunk | while | flops 807567872 | bytes 12259688 | solution.py:417
  5722.9 684.9 %while.69 = (s32[]{:T(128)}, f32[2,256,256]{2,1,0:T(8,128)S(1)}, f32[2,256,256]{1,2,0:T(8,128)S(1)}, f32[2,256,256]{2,1,0:T(8,128)S(1)}, s32[]{:T(128)}, /*index...) while((s32[]{:T(128)}, f32[2,256,256]{2,1,0:T(8,128)S(1)}, ...), condition=%wide.region_9.9_spmd, body=%wide.region_1.8_spmd.sunk | while | flops 1210352128 | bytes 15405615 | solution.py:426
  5723.9 341.4 %while.70 = (s32[]{:T(128)}, f32[2,256,256]{1,2,0:T(8,128)S(1)}, s32[]{:T(128)}, s32[]{:T(128)}, f32[]{:T(128)}, /*index=5*/f32[]{:T(128)}, f32[]{:T(128)}, s32[]{:T(128)}) while((s32[]{:T(128)}, f32[2,256,256]{1,2,0:T(8,128)S(1)}, s32[]{:T(128)}, s32[]{:T(128)}, f32[]{:T(128)}, /*index=5*/f32[]{:T(128)}, f32[]{:T(128)}, s32[]{:T(128)}) %tuple.132), condition=%wide.region_8.7_spmd, body=%wide.region_2.6_spmd.sunk | while | flops 807567872 | bytes 12259688 | solution.py:417
  6428.7 684.9 %while.69 = (s32[]{:T(128)}, f32[2,256,256]{2,1,0:T(8,128)S(1)}, f32[2,256,256]{1,2,0:T(8,128)S(1)}, f32[2,256,256]{2,1,0:T(8,128)S(1)}, s32[]{:T(128)}, /*index...) while((s32[]{:T(128)}, f32[2,256,256]{2,1,0:T(8,128)S(1)}, ...), condition=%wide.region_9.9_spmd, body=%wide.region_1.8_spmd.sunk | while | flops 1210352128 | bytes 15405615 | solution.py:426
  6772.1 341.4 %while.70 = (s32[]{:T(128)}, f32[2,256,256]{1,2,0:T(8,128)S(1)}, s32[]{:T(128)}, s32[]{:T(128)}, f32[]{:T(128)}, /*index=5*/f32[]{:T(128)}, f32[]{:T(128)}, s32[]{:T(128)}) while((s32[]{:T(128)}, f32[2,256,256]{1,2,0:T(8,128)S(1)}, s32[]{:T(128)}, s32[]{:T(128)}, f32[]{:T(128)}, /*index=5*/f32[]{:T(128)}, f32[]{:T(128)}, s32[]{:T(128)}) %tuple.132), condition=%wide.region_8.7_spmd, body=%wide.region_2.6_spmd.sunk | while | flops 807567872 | bytes 12259688 | solution.py:417
  7134.5 684.9 %while.69 = (s32[]{:T(128)}, f32[2,256,256]{2,1,0:T(8,128)S(1)}, f32[2,256,256]{1,2,0:T(8,128)S(1)}, f32[2,256,256]{2,1,0:T(8,128)S(1)}, s32[]{:T(128)}, /*index...) while((s32[]{:T(128)}, f32[2,256,256]{2,1,0:T(8,128)S(1)}, ...), condition=%wide.region_9.9_spmd, body=%wide.region_1.8_spmd.sunk | while | flops 1210352128 | bytes 15405615 | solution.py:426
  7840.3 684.9 %while.69 = (s32[]{:T(128)}, f32[2,256,256]{2,1,0:T(8,128)S(1)}, f32[2,256,256]{1,2,0:T(8,128)S(1)}, f32[2,256,256]{2,1,0:T(8,128)S(1)}, s32[]{:T(128)}, /*index...) while((s32[]{:T(128)}, f32[2,256,256]{2,1,0:T(8,128)S(1)}, ...), condition=%wide.region_9.9_spmd, body=%wide.region_1.8_spmd.sunk | while | flops 1210352128 | bytes 15405615 | solution.py:426
  8183.7 341.4 %while.70 = (s32[]{:T(128)}, f32[2,256,256]{1,2,0:T(8,128)S(1)}, s32[]{:T(128)}, s32[]{:T(128)}, f32[]{:T(128)}, /*index=5*/f32[]{:T(128)}, f32[]{:T(128)}, s32[]{:T(128)}) while((s32[]{:T(128)}, f32[2,256,256]{1,2,0:T(8,128)S(1)}, s32[]{:T(128)}, s32[]{:T(128)}, f32[]{:T(128)}, /*index=5*/f32[]{:T(128)}, f32[]{:T(128)}, s32[]{:T(128)}) %tuple.132), condition=%wide.region_8.7_spmd, body=%wide.region_2.6_spmd.sunk | while | flops 807567872 | bytes 12259688 | solution.py:417
  8546.1 684.9 %while.69 = (s32[]{:T(128)}, f32[2,256,256]{2,1,0:T(8,128)S(1)}, f32[2,256,256]{1,2,0:T(8,128)S(1)}, f32[2,256,256]{2,1,0:T(8,128)S(1)}, s32[]{:T(128)}, /*index...) while((s32[]{:T(128)}, f32[2,256,256]{2,1,0:T(8,128)S(1)}, ...), condition=%wide.region_9.9_spmd, body=%wide.region_1.8_spmd.sunk | while | flops 1210352128 | bytes 15405615 | solution.py:426
  8889.5 341.4 %while.70 = (s32[]{:T(128)}, f32[2,256,256]{1,2,0:T(8,128)S(1)}, s32[]{:T(128)}, s32[]{:T(128)}, f32[]{:T(128)}, /*index=5*/f32[]{:T(128)}, f32[]{:T(128)}, s32[]{:T(128)}) while((s32[]{:T(128)}, f32[2,256,256]{1,2,0:T(8,128)S(1)}, s32[]{:T(128)}, s32[]{:T(128)}, f32[]{:T(128)}, /*index=5*/f32[]{:T(128)}, f32[]{:T(128)}, s32[]{:T(128)}) %tuple.132), condition=%wide.region_8.7_spmd, body=%wide.region_2.6_spmd.sunk | while | flops 807567872 | bytes 12259688 | solution.py:417
  9251.9 684.9 %while.69 = (s32[]{:T(128)}, f32[2,256,256]{2,1,0:T(8,128)S(1)}, f32[2,256,256]{1,2,0:T(8,128)S(1)}, f32[2,256,256]{2,1,0:T(8,128)S(1)}, s32[]{:T(128)}, /*index...) while((s32[]{:T(128)}, f32[2,256,256]{2,1,0:T(8,128)S(1)}, ...), condition=%wide.region_9.9_spmd, body=%wide.region_1.8_spmd.sunk | while | flops 1210352128 | bytes 15405615 | solution.py:426
  9252.9 341.4 %while.70 = (s32[]{:T(128)}, f32[2,256,256]{1,2,0:T(8,128)S(1)}, s32[]{:T(128)}, s32[]{:T(128)}, f32[]{:T(128)}, /*index=5*/f32[]{:T(128)}, f32[]{:T(128)}, s32[]{:T(128)}) while((s32[]{:T(128)}, f32[2,256,256]{1,2,0:T(8,128)S(1)}, s32[]{:T(128)}, s32[]{:T(128)}, f32[]{:T(128)}, /*index=5*/f32[]{:T(128)}, f32[]{:T(128)}, s32[]{:T(128)}) %tuple.132), condition=%wide.region_8.7_spmd, body=%wide.region_2.6_spmd.sunk | while | flops 807567872 | bytes 12259688 | solution.py:417
  9957.6 684.9 %while.69 = (s32[]{:T(128)}, f32[2,256,256]{2,1,0:T(8,128)S(1)}, f32[2,256,256]{1,2,0:T(8,128)S(1)}, f32[2,256,256]{2,1,0:T(8,128)S(1)}, s32[]{:T(128)}, /*index...) while((s32[]{:T(128)}, f32[2,256,256]{2,1,0:T(8,128)S(1)}, ...), condition=%wide.region_9.9_spmd, body=%wide.region_1.8_spmd.sunk | while | flops 1210352128 | bytes 15405615 | solution.py:426
  9958.6 341.4 %while.70 = (s32[]{:T(128)}, f32[2,256,256]{1,2,0:T(8,128)S(1)}, s32[]{:T(128)}, s32[]{:T(128)}, f32[]{:T(128)}, /*index=5*/f32[]{:T(128)}, f32[]{:T(128)}, s32[]{:T(128)}) while((s32[]{:T(128)}, f32[2,256,256]{1,2,0:T(8,128)S(1)}, s32[]{:T(128)}, s32[]{:T(128)}, f32[]{:T(128)}, /*index=5*/f32[]{:T(128)}, f32[]{:T(128)}, s32[]{:T(128)}) %tuple.132), condition=%wide.region_8.7_spmd, body=%wide.region_2.6_spmd.sunk | while | flops 807567872 | bytes 12259688 | solution.py:417
  10663.4 684.9 %while.69 = (s32[]{:T(128)}, f32[2,256,256]{2,1,0:T(8,128)S(1)}, f32[2,256,256]{1,2,0:T(8,128)S(1)}, f32[2,256,256]{2,1,0:T(8,128)S(1)}, s32[]{:T(128)}, /*index...) while((s32[]{:T(128)}, f32[2,256,256]{2,1,0:T(8,128)S(1)}, ...), condition=%wide.region_9.9_spmd, body=%wide.region_1.8_spmd.sunk | while | flops 1210352128 | bytes 15405615 | solution.py:426
  11006.9 341.4 %while.70 = (s32[]{:T(128)}, f32[2,256,256]{1,2,0:T(8,128)S(1)}, s32[]{:T(128)}, s32[]{:T(128)}, f32[]{:T(128)}, /*index=5*/f32[]{:T(128)}, f32[]{:T(128)}, s32[]{:T(128)}) while((s32[]{:T(128)}, f32[2,256,256]{1,2,0:T(8,128)S(1)}, s32[]{:T(128)}, s32[]{:T(128)}, f32[]{:T(128)}, /*index=5*/f32[]{:T(128)}, f32[]{:T(128)}, s32[]{:T(128)}) %tuple.132), condition=%wide.region_8.7_spmd, body=%wide.region_2.6_spmd.sunk | while | flops 807567872 | bytes 12259688 | solution.py:417
  (4012 shorter events, 17741.9 us)
Async XLA Ops:
  0.6 11.7 copy-start
  1.8 8.1 collective-permute-start.1
  3.3 9.0 collective-permute-start.2
  13.6 8.2 collective-permute-start.3
  15.8 6.6 collective-permute-start.4
  23.9 21.8 collective-permute-start.10
  24.6 21.1 collective-permute-start.8
  28.4 17.3 collective-permute-start.9
  37.1 4.9 collective-permute-start.5
  37.2 5.5 collective-permute-start.6
  42.0 3.6 collective-permute-start.7
  46.3 9.1 collective-permute-start.11
  46.4 7.6 collective-permute-start.12
  47.4 6.6 collective-permute-start.13
  51.8 3.6 collective-permute-start.14
  51.8 3.6 copy-start.1
  766.2 13.4 collective-permute-start
  1472.0 13.4 collective-permute-start
  2177.7 13.4 collective-permute-start
  2883.5 13.4 collective-permute-start
  3589.3 13.4 collective-permute-start
  4295.1 13.4 collective-permute-start
  5000.9 13.4 collective-permute-start
  5706.7 13.4 collective-permute-start
  6412.5 13.4 collective-permute-start
  7118.3 13.4 collective-permute-start
  7824.1 13.4 collective-permute-start
  8529.8 13.4 collective-permute-start
  9235.6 13.4 collective-permute-start
  9941.4 13.4 collective-permute-start
  10647.2 13.4 collective-permute-start
  11353.0 13.4 collective-permute-start
  (64 other events, 78.6 us)

commit v6 on v5

--- a/solution.py
+++ b/solution.py
@@ -326,13 +326,13 @@
         b_ref[m] = mm(g_ref[m], g_ref[m], passes=3)
     for _ in range(3):
         for m in range(2):
-            b_ref[m] = mm(b_ref[m], b_ref[m], passes=3)
+            b_ref[m] = mm(b_ref[m], b_ref[m], passes=1)
     for m in range(2):
         top = jnp.exp(0.0625 * 0.5 * jnp.log(total_of(b_ref[m] * b_ref[m]))) * 1.02
         b_ref[m] = eye - g_ref[m] / top
     for t in range(10):
         for m in range(2):
-            b_ref[m] = mm(b_ref[m], b_ref[m], passes=3 if t < 5 else 1)
+            b_ref[m] = mm(b_ref[m], b_ref[m], passes=3 if t < 3 else 1)
     out = jnp.zeros((8, HALF), F32)
     for m in range(2):
         norm = jnp.maximum(total_of(b_ref[m] * b_ref[m]), 1.0e-30)

time: 11400 us -> 11400 us (level)
  no operation moved by 1% of the time
where the time goes in v6:
time: 11400 us
  other arithmetic  10300 us (90%)
  local copies, waits for them, and re-layouts  450 us (4%)
  matrix products  331 us (3%)
  waiting for transfers between devices  200 us (2%)
    another operation x960, other arithmetic, turn(): lower = jnp.linalg.cholesky(gram)  6420 us
    another operation x384, other arithmetic, turn(): lax.linalg.triangular_solve(lower, flip(y), left_side=True, lower=True)  3790 us
    another operation x576, local copies, waits for them, and re-layouts  377 us

profile of v6, /device:TPU:48, one launch (start us, length us, event | category | flops | bytes accessed | tf_op | source)
XLA Modules:
  0.0 11367.4 jit_solution(4993864309173642118)
XLA Ops:
  74.9 11292.2 %while.68 = (s32[]{:T(128)}, f32[2,256,256]{2,1,0:T(8,128)}, f32[2,256,256]{2,1,0:T(8,128)}, f32[2,256,256]{2,1,0:T(8,128)}, s32[]{:T(128)}, /*index=5*/pred[]{:...) while((s32[]{:T(128)}, f32[2,256,256]{2,1,0:T(8,128)}, ...), condition=%wide.region_12.13_spmd, body=%wide.region_0.12_spmd.sunk | while | flops 2419032832 | bytes 36510736 | solution.py:496
  75.9 684.9 %while.69 = (s32[]{:T(128)}, f32[2,256,256]{2,1,0:T(8,128)S(1)}, f32[2,256,256]{1,2,0:T(8,128)S(1)}, f32[2,256,256]{2,1,0:T(8,128)S(1)}, s32[]{:T(128)}, /*index...) while((s32[]{:T(128)}, f32[2,256,256]{2,1,0:T(8,128)S(1)}, ...), condition=%wide.region_9.9_spmd, body=%wide.region_1.8_spmd.sunk | while | flops 1210352128 | bytes 15405615 | solution.py:426
  419.4 341.4 %while.70 = (s32[]{:T(128)}, f32[2,256,256]{1,2,0:T(8,128)S(1)}, s32[]{:T(128)}, s32[]{:T(128)}, f32[]{:T(128)}, /*index=5*/f32[]{:T(128)}, f32[]{:T(128)}, s32[]{:T(128)}) while((s32[]{:T(128)}, f32[2,256,256]{1,2,0:T(8,128)S(1)}, s32[]{:T(128)}, s32[]{:T(128)}, f32[]{:T(128)}, /*index=5*/f32[]{:T(128)}, f32[]{:T(128)}, s32[]{:T(128)}) %tuple.132), condition=%wide.region_8.7_spmd, body=%wide.region_2.6_spmd.sunk | while | flops 807567872 | bytes 12259688 | solution.py:417
  781.7 684.9 %while.69 = (s32[]{:T(128)}, f32[2,256,256]{2,1,0:T(8,128)S(1)}, f32[2,256,256]{1,2,0:T(8,128)S(1)}, f32[2,256,256]{2,1,0:T(8,128)S(1)}, s32[]{:T(128)}, /*index...) while((s32[]{:T(128)}, f32[2,256,256]{2,1,0:T(8,128)S(1)}, ...), condition=%wide.region_9.9_spmd, body=%wide.region_1.8_spmd.sunk | while | flops 1210352128 | bytes 15405615 | solution.py:426
  1487.5 684.9 %while.69 = (s32[]{:T(128)}, f32[2,256,256]{2,1,0:T(8,128)S(1)}, f32[2,256,256]{1,2,0:T(8,128)S(1)}, f32[2,256,256]{2,1,0:T(8,128)S(1)}, s32[]{:T(128)}, /*index...) while((s32[]{:T(128)}, f32[2,256,256]{2,1,0:T(8,128)S(1)}, ...), condition=%wide.region_9.9_spmd, body=%wide.region_1.8_spmd.sunk | while | flops 1210352128 | bytes 15405615 | solution.py:426
  1831.0 341.4 %while.70 = (s32[]{:T(128)}, f32[2,256,256]{1,2,0:T(8,128)S(1)}, s32[]{:T(128)}, s32[]{:T(128)}, f32[]{:T(128)}, /*index=5*/f32[]{:T(128)}, f32[]{:T(128)}, s32[]{:T(128)}) while((s32[]{:T(128)}, f32[2,256,256]{1,2,0:T(8,128)S(1)}, s32[]{:T(128)}, s32[]{:T(128)}, f32[]{:T(128)}, /*index=5*/f32[]{:T(128)}, f32[]{:T(128)}, s32[]{:T(128)}) %tuple.132), condition=%wide.region_8.7_spmd, body=%wide.region_2.6_spmd.sunk | while | flops 807567872 | bytes 12259688 | solution.py:417
  2193.3 684.9 %while.69 = (s32[]{:T(128)}, f32[2,256,256]{2,1,0:T(8,128)S(1)}, f32[2,256,256]{1,2,0:T(8,128)S(1)}, f32[2,256,256]{2,1,0:T(8,128)S(1)}, s32[]{:T(128)}, /*index...) while((s32[]{:T(128)}, f32[2,256,256]{2,1,0:T(8,128)S(1)}, ...), condition=%wide.region_9.9_spmd, body=%wide.region_1.8_spmd.sunk | while | flops 1210352128 | bytes 15405615 | solution.py:426
  2536.8 341.4 %while.70 = (s32[]{:T(128)}, f32[2,256,256]{1,2,0:T(8,128)S(1)}, s32[]{:T(128)}, s32[]{:T(128)}, f32[]{:T(128)}, /*index=5*/f32[]{:T(128)}, f32[]{:T(128)}, s32[]{:T(128)}) while((s32[]{:T(128)}, f32[2,256,256]{1,2,0:T(8,128)S(1)}, s32[]{:T(128)}, s32[]{:T(128)}, f32[]{:T(128)}, /*index=5*/f32[]{:T(128)}, f32[]{:T(128)}, s32[]{:T(128)}) %tuple.132), condition=%wide.region_8.7_spmd, body=%wide.region_2.6_spmd.sunk | while | flops 807567872 | bytes 12259688 | solution.py:417
  2899.1 684.9 %while.69 = (s32[]{:T(128)}, f32[2,256,256]{2,1,0:T(8,128)S(1)}, f32[2,256,256]{1,2,0:T(8,128)S(1)}, f32[2,256,256]{2,1,0:T(8,128)S(1)}, s32[]{:T(128)}, /*index...) while((s32[]{:T(128)}, f32[2,256,256]{2,1,0:T(8,128)S(1)}, ...), condition=%wide.region_9.9_spmd, body=%wide.region_1.8_spmd.sunk | while | flops 1210352128 | bytes 15405615 | solution.py:426
  2900.1 341.4 %while.70 = (s32[]{:T(128)}, f32[2,256,256]{1,2,0:T(8,128)S(1)}, s32[]{:T(128)}, s32[]{:T(128)}, f32[]{:T(128)}, /*index=5*/f32[]{:T(128)}, f32[]{:T(128)}, s32[]{:T(128)}) while((s32[]{:T(128)}, f32[2,256,256]{1,2,0:T(8,128)S(1)}, s32[]{:T(128)}, s32[]{:T(128)}, f32[]{:T(128)}, /*index=5*/f32[]{:T(128)}, f32[]{:T(128)}, s32[]{:T(128)}) %tuple.132), condition=%wide.region_8.7_spmd, body=%wide.region_2.6_spmd.sunk | while | flops 807567872 | bytes 12259688 | solution.py:417
  3604.9 684.9 %while.69 = (s32[]{:T(128)}, f32[2,256,256]{2,1,0:T(8,128)S(1)}, f32[2,256,256]{1,2,0:T(8,128)S(1)}, f32[2,256,256]{2,1,0:T(8,128)S(1)}, s32[]{:T(128)}, /*index...) while((s32[]{:T(128)}, f32[2,256,256]{2,1,0:T(8,128)S(1)}, ...), condition=%wide.region_9.9_spmd, body=%wide.region_1.8_spmd.sunk | while | flops 1210352128 | bytes 15405615 | solution.py:426
  3605.9 341.4 %while.70 = (s32[]{:T(128)}, f32[2,256,256]{1,2,0:T(8,128)S(1)}, s32[]{:T(128)}, s32[]{:T(128)}, f32[]{:T(128)}, /*index=5*/f32[]{:T(128)}, f32[]{:T(128)}, s32[]{:T(128)}) while((s32[]{:T(128)}, f32[2,256,256]{1,2,0:T(8,128)S(1)}, s32[]{:T(128)}, s32[]{:T(128)}, f32[]{:T(128)}, /*index=5*/f32[]{:T(128)}, f32[]{:T(128)}, s32[]{:T(128)}) %tuple.132), condition=%wide.region_8.7_spmd, body=%wide.region_2.6_spmd.sunk | while | flops 807567872 | bytes 12259688 | solution.py:417
  4310.7 684.9 %while.69 = (s32[]{:T(128)}, f32[2,256,256]{2,1,0:T(8,128)S(1)}, f32[2,256,256]{1,2,0:T(8,128)S(1)}, f32[2,256,256]{2,1,0:T(8,128)S(1)}, s32[]{:T(128)}, /*index...) while((s32[]{:T(128)}, f32[2,256,256]{2,1,0:T(8,128)S(1)}, ...), condition=%wide.region_9.9_spmd, body=%wide.region_1.8_spmd.sunk | while | flops 1210352128 | bytes 15405615 | solution.py:426
  4654.1 341.4 %while.70 = (s32[]{:T(128)}, f32[2,256,256]{1,2,0:T(8,128)S(1)}, s32[]{:T(128)}, s32[]{:T(128)}, f32[]{:T(128)}, /*index=5*/f32[]{:T(128)}, f32[]{:T(128)}, s32[]{:T(128)}) while((s32[]{:T(128)}, f32[2,256,256]{1,2,0:T(8,128)S(1)}, s32[]{:T(128)}, s32[]{:T(128)}, f32[]{:T(128)}, /*index=5*/f32[]{:T(128)}, f32[]{:T(128)}, s32[]{:T(128)}) %tuple.132), condition=%wide.region_8.7_spmd, body=%wide.region_2.6_spmd.sunk | while | flops 807567872 | bytes 12259688 | solution.py:417
  5016.5 684.9 %while.69 = (s32[]{:T(128)}, f32[2,256,256]{2,1,0:T(8,128)S(1)}, f32[2,256,256]{1,2,0:T(8,128)S(1)}, f32[2,256,256]{2,1,0:T(8,128)S(1)}, s32[]{:T(128)}, /*index...) while((s32[]{:T(128)}, f32[2,256,256]{2,1,0:T(8,128)S(1)}, ...), condition=%wide.region_9.9_spmd, body=%wide.region_1.8_spmd.sunk | while | flops 1210352128 | bytes 15405615 | solution.py:426
  5722.2 684.9 %while.69 = (s32[]{:T(128)}, f32[2,256,256]{2,1,0:T(8,128)S(1)}, f32[2,256,256]{1,2,0:T(8,128)S(1)}, f32[2,256,256]{2,1,0:T(8,128)S(1)}, s32[]{:T(128)}, /*index...) while((s32[]{:T(128)}, f32[2,256,256]{2,1,0:T(8,128)S(1)}, ...), condition=%wide.region_9.9_spmd, body=%wide.region_1.8_spmd.sunk | while | flops 1210352128 | bytes 15405615 | solution.py:426
  5723.3 341.4 %while.70 = (s32[]{:T(128)}, f32[2,256,256]{1,2,0:T(8,128)S(1)}, s32[]{:T(128)}, s32[]{:T(128)}, f32[]{:T(128)}, /*index=5*/f32[]{:T(128)}, f32[]{:T(128)}, s32[]{:T(128)}) while((s32[]{:T(128)}, f32[2,256,256]{1,2,0:T(8,128)S(1)}, s32[]{:T(128)}, s32[]{:T(128)}, f32[]{:T(128)}, /*index=5*/f32[]{:T(128)}, f32[]{:T(128)}, s32[]{:T(128)}) %tuple.132), condition=%wide.region_8.7_spmd, body=%wide.region_2.6_spmd.sunk | while | flops 807567872 | bytes 12259688 | solution.py:417
  6065.7 341.4 %while.70 = (s32[]{:T(128)}, f32[2,256,256]{1,2,0:T(8,128)S(1)}, s32[]{:T(128)}, s32[]{:T(128)}, f32[]{:T(128)}, /*index=5*/f32[]{:T(128)}, f32[]{:T(128)}, s32[]{:T(128)}) while((s32[]{:T(128)}, f32[2,256,256]{1,2,0:T(8,128)S(1)}, s32[]{:T(128)}, s32[]{:T(128)}, f32[]{:T(128)}, /*index=5*/f32[]{:T(128)}, f32[]{:T(128)}, s32[]{:T(128)}) %tuple.132), condition=%wide.region_8.7_spmd, body=%wide.region_2.6_spmd.sunk | while | flops 807567872 | bytes 12259688 | solution.py:417
  6428.0 684.9 %while.69 = (s32[]{:T(128)}, f32[2,256,256]{2,1,0:T(8,128)S(1)}, f32[2,256,256]{1,2,0:T(8,128)S(1)}, f32[2,256,256]{2,1,0:T(8,128)S(1)}, s32[]{:T(128)}, /*index...) while((s32[]{:T(128)}, f32[2,256,256]{2,1,0:T(8,128)S(1)}, ...), condition=%wide.region_9.9_spmd, body=%wide.region_1.8_spmd.sunk | while | flops 1210352128 | bytes 15405615 | solution.py:426
  6771.5 341.4 %while.70 = (s32[]{:T(128)}, f32[2,256,256]{1,2,0:T(8,128)S(1)}, s32[]{:T(128)}, s32[]{:T(128)}, f32[]{:T(128)}, /*index=5*/f32[]{:T(128)}, f32[]{:T(128)}, s32[]{:T(128)}) while((s32[]{:T(128)}, f32[2,256,256]{1,2,0:T(8,128)S(1)}, s32[]{:T(128)}, s32[]{:T(128)}, f32[]{:T(128)}, /*index=5*/f32[]{:T(128)}, f32[]{:T(128)}, s32[]{:T(128)}) %tuple.132), condition=%wide.region_8.7_spmd, body=%wide.region_2.6_spmd.sunk | while | flops 807567872 | bytes 12259688 | solution.py:417
  7133.8 684.9 %while.69 = (s32[]{:T(128)}, f32[2,256,256]{2,1,0:T(8,128)S(1)}, f32[2,256,256]{1,2,0:T(8,128)S(1)}, f32[2,256,256]{2,1,0:T(8,128)S(1)}, s32[]{:T(128)}, /*index...) while((s32[]{:T(128)}, f32[2,256,256]{2,1,0:T(8,128)S(1)}, ...), condition=%wide.region_9.9_spmd, body=%wide.region_1.8_spmd.sunk | while | flops 1210352128 | bytes 15405615 | solution.py:426
  7134.8 341.4 %while.70 = (s32[]{:T(128)}, f32[2,256,256]{1,2,0:T(8,128)S(1)}, s32[]{:T(128)}, s32[]{:T(128)}, f32[]{:T(128)}, /*index=5*/f32[]{:T(128)}, f32[]{:T(128)}, s32[]{:T(128)}) while((s32[]{:T(128)}, f32[2,256,256]{1,2,0:T(8,128)S(1)}, s32[]{:T(128)}, s32[]{:T(128)}, f32[]{:T(128)}, /*index=5*/f32[]{:T(128)}, f32[]{:T(128)}, s32[]{:T(128)}) %tuple.132), condition=%wide.region_8.7_spmd, body=%wide.region_2.6_spmd.sunk | while | flops 807567872 | bytes 12259688 | solution.py:417
  7839.6 684.9 %while.69 = (s32[]{:T(128)}, f32[2,256,256]{2,1,0:T(8,128)S(1)}, f32[2,256,256]{1,2,0:T(8,128)S(1)}, f32[2,256,256]{2,1,0:T(8,128)S(1)}, s32[]{:T(128)}, /*index...) while((s32[]{:T(128)}, f32[2,256,256]{2,1,0:T(8,128)S(1)}, ...), condition=%wide.region_9.9_spmd, body=%wide.region_1.8_spmd.sunk | while | flops 1210352128 | bytes 15405615 | solution.py:426
  8545.4 684.9 %while.69 = (s32[]{:T(128)}, f32[2,256,256]{2,1,0:T(8,128)S(1)}, f32[2,256,256]{1,2,0:T(8,128)S(1)}, f32[2,256,256]{2,1,0:T(8,128)S(1)}, s32[]{:T(128)}, /*index...) while((s32[]{:T(128)}, f32[2,256,256]{2,1,0:T(8,128)S(1)}, ...), condition=%wide.region_9.9_spmd, body=%wide.region_1.8_spmd.sunk | while | flops 1210352128 | bytes 15405615 | solution.py:426
  8888.8 341.4 %while.70 = (s32[]{:T(128)}, f32[2,256,256]{1,2,0:T(8,128)S(1)}, s32[]{:T(128)}, s32[]{:T(128)}, f32[]{:T(128)}, /*index=5*/f32[]{:T(128)}, f32[]{:T(128)}, s32[]{:T(128)}) while((s32[]{:T(128)}, f32[2,256,256]{1,2,0:T(8,128)S(1)}, s32[]{:T(128)}, s32[]{:T(128)}, f32[]{:T(128)}, /*index=5*/f32[]{:T(128)}, f32[]{:T(128)}, s32[]{:T(128)}) %tuple.132), condition=%wide.region_8.7_spmd, body=%wide.region_2.6_spmd.sunk | while | flops 807567872 | bytes 12259688 | solution.py:417
  9251.2 684.9 %while.69 = (s32[]{:T(128)}, f32[2,256,256]{2,1,0:T(8,128)S(1)}, f32[2,256,256]{1,2,0:T(8,128)S(1)}, f32[2,256,256]{2,1,0:T(8,128)S(1)}, s32[]{:T(128)}, /*index...) while((s32[]{:T(128)}, f32[2,256,256]{2,1,0:T(8,128)S(1)}, ...), condition=%wide.region_9.9_spmd, body=%wide.region_1.8_spmd.sunk | while | flops 1210352128 | bytes 15405615 | solution.py:426
  9252.2 341.4 %while.70 = (s32[]{:T(128)}, f32[2,256,256]{1,2,0:T(8,128)S(1)}, s32[]{:T(128)}, s32[]{:T(128)}, f32[]{:T(128)}, /*index=5*/f32[]{:T(128)}, f32[]{:T(128)}, s32[]{:T(128)}) while((s32[]{:T(128)}, f32[2,256,256]{1,2,0:T(8,128)S(1)}, s32[]{:T(128)}, s32[]{:T(128)}, f32[]{:T(128)}, /*index=5*/f32[]{:T(128)}, f32[]{:T(128)}, s32[]{:T(128)}) %tuple.132), condition=%wide.region_8.7_spmd, body=%wide.region_2.6_spmd.sunk | while | flops 807567872 | bytes 12259688 | solution.py:417
  9957.0 684.9 %while.69 = (s32[]{:T(128)}, f32[2,256,256]{2,1,0:T(8,128)S(1)}, f32[2,256,256]{1,2,0:T(8,128)S(1)}, f32[2,256,256]{2,1,0:T(8,128)S(1)}, s32[]{:T(128)}, /*index...) while((s32[]{:T(128)}, f32[2,256,256]{2,1,0:T(8,128)S(1)}, ...), condition=%wide.region_9.9_spmd, body=%wide.region_1.8_spmd.sunk | while | flops 1210352128 | bytes 15405615 | solution.py:426
  9958.0 341.4 %while.70 = (s32[]{:T(128)}, f32[2,256,256]{1,2,0:T(8,128)S(1)}, s32[]{:T(128)}, s32[]{:T(128)}, f32[]{:T(128)}, /*index=5*/f32[]{:T(128)}, f32[]{:T(128)}, s32[]{:T(128)}) while((s32[]{:T(128)}, f32[2,256,256]{1,2,0:T(8,128)S(1)}, s32[]{:T(128)}, s32[]{:T(128)}, f32[]{:T(128)}, /*index=5*/f32[]{:T(128)}, f32[]{:T(128)}, s32[]{:T(128)}) %tuple.132), condition=%wide.region_8.7_spmd, body=%wide.region_2.6_spmd.sunk | while | flops 807567872 | bytes 12259688 | solution.py:417
  10300.4 341.4 %while.70 = (s32[]{:T(128)}, f32[2,256,256]{1,2,0:T(8,128)S(1)}, s32[]{:T(128)}, s32[]{:T(128)}, f32[]{:T(128)}, /*index=5*/f32[]{:T(128)}, f32[]{:T(128)}, s32[]{:T(128)}) while((s32[]{:T(128)}, f32[2,256,256]{1,2,0:T(8,128)S(1)}, s32[]{:T(128)}, s32[]{:T(128)}, f32[]{:T(128)}, /*index=5*/f32[]{:T(128)}, f32[]{:T(128)}, s32[]{:T(128)}) %tuple.132), condition=%wide.region_8.7_spmd, body=%wide.region_2.6_spmd.sunk | while | flops 807567872 | bytes 12259688 | solution.py:417
  10662.8 684.9 %while.69 = (s32[]{:T(128)}, f32[2,256,256]{2,1,0:T(8,128)S(1)}, f32[2,256,256]{1,2,0:T(8,128)S(1)}, f32[2,256,256]{2,1,0:T(8,128)S(1)}, s32[]{:T(128)}, /*index...) while((s32[]{:T(128)}, f32[2,256,256]{2,1,0:T(8,128)S(1)}, ...), condition=%wide.region_9.9_spmd, body=%wide.region_1.8_spmd.sunk | while | flops 1210352128 | bytes 15405615 | solution.py:426
  11006.2 341.4 %while.70 = (s32[]{:T(128)}, f32[2,256,256]{1,2,0:T(8,128)S(1)}, s32[]{:T(128)}, s32[]{:T(128)}, f32[]{:T(128)}, /*index=5*/f32[]{:T(128)}, f32[]{:T(128)}, s32[]{:T(128)}) while((s32[]{:T(128)}, f32[2,256,256]{1,2,0:T(8,128)S(1)}, s32[]{:T(128)}, s32[]{:T(128)}, f32[]{:T(128)}, /*index=5*/f32[]{:T(128)}, f32[]{:T(128)}, s32[]{:T(128)}) %tuple.132), condition=%wide.region_8.7_spmd, body=%wide.region_2.6_spmd.sunk | while | flops 807567872 | bytes 12259688 | solution.py:417
  (4012 shorter events, 17741.2 us)
Async XLA Ops:
  0.6 11.7 copy-start
  1.8 8.1 collective-permute-start.1
  3.3 9.0 collective-permute-start.2
  13.6 8.2 collective-permute-start.3
  15.8 6.6 collective-permute-start.4
  23.9 21.1 collective-permute-start.10
  24.6 20.4 collective-permute-start.8
  28.4 16.6 collective-permute-start.9
  36.5 4.9 collective-permute-start.5
  36.6 5.5 collective-permute-start.6
  41.4 3.7 collective-permute-start.7
  45.7 9.1 collective-permute-start.11
  45.8 7.6 collective-permute-start.12
  46.8 6.6 collective-permute-start.13
  51.2 3.6 collective-permute-start.14
  51.2 3.6 copy-start.1
  765.5 13.4 collective-permute-start
  1471.3 13.4 collective-permute-start
  2177.1 13.4 collective-permute-start
  2882.9 13.4 collective-permute-start
  3588.7 13.4 collective-permute-start
  4294.4 13.4 collective-permute-start
  5000.2 13.4 collective-permute-start
  5706.0 13.4 collective-permute-start
  6411.8 13.4 collective-permute-start
  7117.6 13.4 collective-permute-start
  7823.4 13.4 collective-permute-start
  8529.2 13.4 collective-permute-start
  9235.0 13.4 collective-permute-start
  9940.8 13.4 collective-permute-start
  10646.5 13.4 collective-permute-start
  11352.3 13.4 collective-permute-start
  (64 other events, 78.6 us)
